TPU v7x, 512 devices: a whole 4x8x8 slice. The times are simulated.
512 devices in a mesh: dist: 4 (over y_lo, core), pix: 128 (over z, x, y_hi).
Axes of the slice: x: 4, y: 8 (y_hi: 4, y_lo: 2; y = y_hi * 2 + y_lo), z: 8, core: 2. Of those that a mesh axis runs over, the one named last changes fastest.
Arguments:
- contrast: float32 [4, 2, 2048, 2048], P('dist', None, 'pix'), may hold values from -6 to 6
- defocus: float32 [4], P('dist'), may hold values from 40 to 400
- blurring: float32 [4], P('dist'), may hold values from 0.5 to 4
Outputs:
- phase: float32 [2, 2048, 2048], P(None, 'pix')
All inputs are finite; a program needn't handle non-finite values.
Results may differ from a plain program's by a relative error of at most 0.0003.
Values sent between devices are 32-bit elements; how exact they have to be, the bound alone decides.
No kernel may reach another device: no remote copies, remote signals or barrier semaphores. Data moves between devices by JAX's collectives and lax.ppermute only.
A program may use at most 64 MiB of HBM per device.

v0:
```python
import math

import jax
import jax.numpy as jnp
from jax import lax
from jax.sharding import PartitionSpec as P

ABSORB_RATIO = 0.1
REGULARIZER = 0.05


def split_up(x, dim, length):
    before, after = (x.shape[:dim], x.shape[dim + 1 :])
    return jnp.moveaxis(x.reshape(*before, length, -1, *after), dim, 0)


def sum_at_owner(x, axis, dim):
    length = lax.axis_size(axis)
    parts = lax.all_to_all(split_up(x, dim, length), axis, 0, 0, tiled=True)
    return jnp.sum(parts, axis=0)


def sent_together(arrays, axis, dim, along):
    both = jnp.concatenate(arrays, axis=along)
    filled, at, done = (sum_at_owner(both, axis, dim), 0, [])
    for a in arrays:
        done.append(lax.slice_in_dim(filled, at, at + a.shape[along], axis=along))
        at += a.shape[along]
    return tuple(done)


def in_one_piece(arrays, axis, dim, along):
    both = jnp.concatenate(arrays, axis=along)
    filled, at, done = (lax.all_gather(both, axis, axis=dim, tiled=True), 0, [])
    for a in arrays:
        done.append(lax.slice_in_dim(filled, at, at + a.shape[along], axis=along))
        at += a.shape[along]
    return tuple(done)


def unit_phase(first_len, second_len, period):
    left_index = jnp.arange(first_len, dtype=jnp.int32)[:, None]
    right_index = jnp.arange(second_len, dtype=jnp.int32)[None, :]
    turn_count = left_index * right_index % period
    angles = 2.0 * math.pi / period * turn_count.astype(jnp.float32)
    return (jnp.cos(angles), -jnp.sin(angles))


def conjugate_flip(tables):
    return (tables[0], -tables[1])


def complex_product(pattern, real_part, imag_part, tables):
    cosine, sine_part = tables
    out_real = jnp.einsum(pattern, real_part, cosine, precision=lax.Precision.HIGHEST) - jnp.einsum(
        pattern, imag_part, sine_part, precision=lax.Precision.HIGHEST
    )
    out_imag = jnp.einsum(
        pattern, real_part, sine_part, precision=lax.Precision.HIGHEST
    ) + jnp.einsum(pattern, imag_part, cosine, precision=lax.Precision.HIGHEST)
    return (out_real, out_imag)


def apply_twist(real_part, imag_part, cosine, sine_part):
    return (real_part * cosine - imag_part * sine_part, real_part * sine_part + imag_part * cosine)


def signed_square(freq_index, period):
    shifted = freq_index - period * (2 * freq_index >= period).astype(jnp.int32)
    fraction = shifted.astype(jnp.float32) / period
    return fraction * fraction


def transfer(defocus_value, blur_rate, squared):
    return jnp.exp(-blur_rate * squared) * (
        jnp.sin(defocus_value * squared) + ABSORB_RATIO * jnp.cos(defocus_value * squared)
    )


def body(contrast, defocus, blurring):
    images = contrast[0]
    projections, rows_local, columns = images.shape
    pix_count = lax.axis_size("pix")
    col_block = columns // pix_count
    rows_total = rows_local * pix_count
    outer_table = unit_phase(col_block, col_block, col_block)
    pixel_lookup_table = unit_phase(pix_count, pix_count, pix_count)
    row_table = unit_phase(rows_local, rows_local, rows_local)
    col_twist = unit_phase(col_block, pix_count, columns)
    row_twist = unit_phase(rows_local, pix_count, rows_total)
    even_images = images[0::2]
    odd_images = images[1::2]
    shaped_real = even_images.reshape(projections // 2, rows_local, col_block, pix_count)
    shaped_imag = odd_images.reshape(projections // 2, rows_local, col_block, pix_count)
    section_real, section_imag = complex_product(
        "prbn,bc->pcrn", shaped_real, shaped_imag, outer_table
    )
    section_real, section_imag = apply_twist(
        section_real, section_imag, col_twist[0][:, None, :], col_twist[1][:, None, :]
    )
    spec_real, spec_imag = complex_product(
        "pcrn,nq->pcrq", section_real, section_imag, pixel_lookup_table
    )
    col_freq = col_block * lax.axis_index("pix") + jnp.arange(col_block, dtype=jnp.int32)
    row_freq = (
        pix_count * jnp.arange(rows_local, dtype=jnp.int32)[:, None]
        + jnp.arange(pix_count, dtype=jnp.int32)[None, :]
    )
    squared = (
        signed_square(row_freq, rows_total)[None, :, :]
        + signed_square(col_freq, columns)[:, None, None]
    )
    own_gain = transfer(defocus[0], blurring[0], squared)
    received_real = lax.all_to_all(spec_real, "pix", split_axis=3, concat_axis=3, tiled=True)
    received_imaginary = lax.all_to_all(spec_imag, "pix", split_axis=3, concat_axis=3, tiled=True)
    middle_real, middle_imaginary = complex_product(
        "uhqb,bn->uhqn", received_real, received_imaginary, pixel_lookup_table
    )
    middle_real, middle_imaginary = apply_twist(
        middle_real, middle_imaginary, row_twist[0], row_twist[1]
    )
    out_real, out_imag = complex_product("pcrk,rj->pcjk", middle_real, middle_imaginary, row_table)
    summands = (own_gain * out_real, own_gain * out_imag, (own_gain * own_gain)[None])
    band_width = col_block // lax.axis_size("dist")
    band_start = lax.axis_index("dist") * band_width
    totals = sent_together((summands[0], summands[1], summands[2]), "dist", 1, 0)
    den_sum = totals[2][0]
    bottom = 2.0 * (den_sum + REGULARIZER)
    quot_real = totals[0] / bottom
    quot_imag = totals[1] / bottom
    backward_real, backward_imaginary = complex_product(
        "pcjk,rj->pcrk", quot_real, quot_imag, conjugate_flip(row_table)
    )
    backward_real, backward_imaginary = apply_twist(
        backward_real, backward_imaginary, row_twist[0], -row_twist[1]
    )
    backward_real, backward_imaginary = complex_product(
        "uotv,zv->uotz", backward_real, backward_imaginary, conjugate_flip(pixel_lookup_table)
    )
    backward_real = backward_real / rows_total
    backward_imaginary = backward_imaginary / rows_total
    twist_cos = lax.dynamic_slice_in_dim(col_twist[0], band_start, band_width, 0)
    twist_sin = lax.dynamic_slice_in_dim(col_twist[1], band_start, band_width, 0)
    received_real = lax.all_to_all(backward_real, "pix", split_axis=3, concat_axis=3, tiled=True)
    received_imaginary = lax.all_to_all(
        backward_imaginary, "pix", split_axis=3, concat_axis=3, tiled=True
    )
    middle_real, middle_imaginary = complex_product(
        "pcrq,nq->pcrn", received_real, received_imaginary, conjugate_flip(pixel_lookup_table)
    )
    cols_real, cols_imag = apply_twist(
        middle_real, middle_imaginary, twist_cos[:, None, :], -twist_sin[:, None, :]
    )
    cols_real, cols_imag = in_one_piece((cols_real, cols_imag), "dist", 1, 0)
    phase_blocks = jnp.einsum(
        "pcrn,cb->prbn", cols_real, outer_table[0], precision=lax.Precision.HIGHEST
    ) + jnp.einsum("pcrn,cb->prbn", cols_imag, outer_table[1], precision=lax.Precision.HIGHEST)
    odd_blocks = jnp.einsum(
        "pcrn,cb->prbn", cols_imag, outer_table[0], precision=lax.Precision.HIGHEST
    ) - jnp.einsum("pcrn,cb->prbn", cols_real, outer_table[1], precision=lax.Precision.HIGHEST)
    paired_blocks = jnp.stack([phase_blocks, odd_blocks], axis=1)
    return (paired_blocks / columns).reshape(projections, rows_local, columns)


def solution(mesh):
    return jax.shard_map(
        body,
        mesh=mesh,
        in_specs=(P("dist", None, "pix", None), P("dist"), P("dist")),
        out_specs=P(None, "pix", None),
        check_vma=False,
    )
```

profile of v0, /device:TPU:1, one launch (start us, length us, event | category | flops | bytes accessed | tf_op | source)
XLA Modules:
  0.0 136.4 jit_solution(8077266745936653268)
XLA Ops:
  0.1 1.0 slice_bitcast_fusion.2
  2.1 0.3 multiply_add_fusion.1
  2.4 0.5 fusion.43
  2.9 0.5 fusion.5
  3.5 0.5 copy.18
  3.9 1.0 reshape.391
  5.0 20.8 %all-to-all-start = ((f32[128,1,256]{2,1,0:T(1,128)}), f32[128,1,256]{2,1,0:T(1,128)S(1)}, u32[]{:S(2)}, u32[]{:S(2)}) async-start(f32[128,1,256]{2,1,0:T(1,128)} %reshape.391), calls=%async_computation | async-start | bytes 262144 | tf_op jit(solution)/shard_map/all_to_all | solution.py:114
  25.8 0.5 fusion.41
  26.4 0.5 fusion.4
  27.0 0.5 copy.22
  27.5 1.0 reshape.393
  29.8 0.6 fusion.20
  30.4 9.1 %all-to-all-done = f32[128,1,256]{2,1,0:T(1,128)S(1)} async-done(((f32[128,1,256]{2,1,0:T(1,128)}), f32[128,1,256]{2,1,0:T(1,128)S(1)}, u32[]{:S(2)}, u32[]{:S(2)}) %all-to-all-start) | async-done | bytes 131104 | tf_op jit(solution)/shard_map/all_to_all | solution.py:114
  39.5 6.7 %all-to-all-start.1 = ((f32[128,1,256]{2,1,0:T(1,128)}), f32[128,1,256]{2,1,0:T(1,128)S(1)}, u32[]{:S(2)}, u32[]{:S(2)}) async-start(f32[128,1,256]{2,1,0:T(1,128)} %reshape.393), calls=%async_computation.1 | async-start | bytes 262144 | tf_op jit(solution)/shard_map/all_to_all | solution.py:115
  46.2 0.5 broadcast.577
  46.7 1.0 reduce
  47.7 0.3 reshape.392
  48.0 0.4 copy.19
  48.4 0.5 fusion.31
  48.9 0.5 fusion.29
  49.4 9.9 %all-to-all-done.1 = f32[128,1,256]{2,1,0:T(1,128)S(1)} async-done(((f32[128,1,256]{2,1,0:T(1,128)}), f32[128,1,256]{2,1,0:T(1,128)S(1)}, u32[]{:S(2)}, u32[]{:S(2)}) %all-to-all-start.1) | async-done | bytes 131104 | tf_op jit(solution)/shard_map/all_to_all | solution.py:115
  59.4 1.0 reduce.1
  60.3 0.3 reshape.394
  60.7 0.4 copy.23
  61.1 0.5 convolution_subtract_fusion.2
  61.6 0.5 convolution_add_fusion.2
  62.1 0.3 fusion.76
  62.8 0.7 fusion.6
  63.4 0.7 fusion.7
  64.1 0.8 maximum_bitcast_fusion
  64.9 6.1 %all-to-all-start.2 = ((f32[4,3,4,16,128]{4,3,2,1,0:T(8,128)}), f32[4,3,4,16,128]{4,3,2,1,0:T(8,128)S(1)}, u32[]{:S(2)}, u32[]{:S(2)}) async-start(f32[4,3,4,16,128]{4,3,2,1,0:T(8,128)} %maximum_bitcast_fusion), calls=%async_computation.2 | async-start | bytes 786432 | tf_op jit(solution)/shard_map/all_to_all | solution.py:19
  71.1 6.4 %all-to-all-done.2 = f32[4,3,4,16,128]{4,3,2,1,0:T(8,128)S(1)} async-done(((f32[4,3,4,16,128]{4,3,2,1,0:T(8,128)}), f32[4,3,4,16,128]{4,3,2,1,0:T(8,128)S(1)}, u32[]{:S(2)}, u32[]{:S(2)}) %all-to-all-start.2) | async-done | bytes 393248 | tf_op jit(solution)/shard_map/all_to_all | solution.py:19
  78.7 0.5 fusion.51
  79.2 0.5 fusion.62
  79.7 0.5 fusion.11
  80.1 0.8 copy.30
  81.0 6.2 %all-to-all-start.3 = ((f32[1,4,16,128]{2,1,0,3:T(4,128)}), f32[1,4,16,128]{2,1,0,3:T(4,128)S(1)}, u32[]{:S(2)}, u32[]{:S(2)}) async-start(f32[1,4,16,128]{2,1,0,3:T(4,128)} %copy.30), calls=%async_computation.3 | async-start | bytes 524288 | tf_op jit(solution)/shard_map/all_to_all | solution.py:144
  87.2 0.5 fusion.9
  87.6 0.8 copy.32
  88.5 13.6 %all-to-all-done.3 = f32[1,4,16,128]{2,1,0,3:T(4,128)S(1)} async-done(((f32[1,4,16,128]{2,1,0,3:T(4,128)}), f32[1,4,16,128]{2,1,0,3:T(4,128)S(1)}, u32[]{:S(2)}, u32[]{:S(2)}) %all-to-all-start.3) | async-done | bytes 32800 | tf_op jit(solution)/shard_map/all_to_all | solution.py:144
  102.1 7.6 %all-to-all-start.4 = ((f32[1,4,16,128]{2,1,0,3:T(4,128)}), f32[1,4,16,128]{2,1,0,3:T(4,128)S(1)}, u32[]{:S(2)}, u32[]{:S(2)}) async-start(f32[1,4,16,128]{2,1,0,3:T(4,128)} %copy.32), calls=%async_computation.4 | async-start | bytes 524288 | tf_op jit(solution)/shard_map/all_to_all | solution.py:145
  109.8 0.5 fusion.48
  110.3 0.5 fusion.60
  110.8 14.3 %all-to-all-done.4 = f32[1,4,16,128]{2,1,0,3:T(4,128)S(1)} async-done(((f32[1,4,16,128]{2,1,0,3:T(4,128)}), f32[1,4,16,128]{2,1,0,3:T(4,128)S(1)}, u32[]{:S(2)}, u32[]{:S(2)}) %all-to-all-start.4) | async-done | bytes 32800 | tf_op jit(solution)/shard_map/all_to_all | solution.py:145
  125.2 0.5 convolution_add_fusion.5
  125.7 0.5 subtract_bitcast_fusion
  126.2 8.1 %all_gather.3 = f32[2,16,16,128]{3,2,1,0:T(8,128)S(1)} all-gather(f32[2,4,16,128]{3,2,1,0:T(8,128)S(1)} %pad_maximum_fusion), channel_id=1, replica_groups=mesh['dist'=4,'pix'=128] {'dist'}, dimensions={1}, use_global_device_ids=true | all-gather | bytes 327680 | tf_op jit(solution)/shard_map/all_gather | solution.py:34
  135.7 0.7 maximum_multiply_fusion
  (29 shorter events, 4.2 us)
Async XLA Ops:
  5.0 34.5 %all-to-all-start = ((f32[128,1,256]{2,1,0:T(1,128)}), f32[128,1,256]{2,1,0:T(1,128)S(1)}, u32[]{:S(2)}, u32[]{:S(2)}) async-start(f32[128,1,256]{2,1,0:T(1,128)} %reshape.391), calls=%async_computation | async-start | bytes 262144 | tf_op jit(solution)/shard_map/all_to_all | solution.py:114
  39.5 19.9 %all-to-all-start.1 = ((f32[128,1,256]{2,1,0:T(1,128)}), f32[128,1,256]{2,1,0:T(1,128)S(1)}, u32[]{:S(2)}, u32[]{:S(2)}) async-start(f32[128,1,256]{2,1,0:T(1,128)} %reshape.393), calls=%async_computation.1 | async-start | bytes 262144 | tf_op jit(solution)/shard_map/all_to_all | solution.py:115
  64.9 12.6 %all-to-all-start.2 = ((f32[4,3,4,16,128]{4,3,2,1,0:T(8,128)}), f32[4,3,4,16,128]{4,3,2,1,0:T(8,128)S(1)}, u32[]{:S(2)}, u32[]{:S(2)}) async-start(f32[4,3,4,16,128]{4,3,2,1,0:T(8,128)} %maximum_bitcast_fusion), calls=%async_computation.2 | async-start | bytes 786432 | tf_op jit(solution)/shard_map/all_to_all | solution.py:19
  81.0 21.1 %all-to-all-start.3 = ((f32[1,4,16,128]{2,1,0,3:T(4,128)}), f32[1,4,16,128]{2,1,0,3:T(4,128)S(1)}, u32[]{:S(2)}, u32[]{:S(2)}) async-start(f32[1,4,16,128]{2,1,0,3:T(4,128)} %copy.30), calls=%async_computation.3 | async-start | bytes 524288 | tf_op jit(solution)/shard_map/all_to_all | solution.py:144
  102.1 23.0 %all-to-all-start.4 = ((f32[1,4,16,128]{2,1,0,3:T(4,128)}), f32[1,4,16,128]{2,1,0,3:T(4,128)S(1)}, u32[]{:S(2)}, u32[]{:S(2)}) async-start(f32[1,4,16,128]{2,1,0,3:T(4,128)} %copy.32), calls=%async_computation.4 | async-start | bytes 524288 | tf_op jit(solution)/shard_map/all_to_all | solution.py:145
where the time goes:
time: 137 us; the launch traced here: 136 us
  waiting for transfers between devices  53.2 us (39%)
  starting transfers between devices  47.5 us (35%)
  matrix products  13.6 us (10%)
  blocking collectives  8.11 us (6%)
  local copies, waits for them, and re-layouts  8 us (6%)
  other arithmetic  4.25 us (3%)
  between operations  1.7 us (1%)
    all_to_all x1, starting transfers between devices, body(): lax.all_to_all(spec_real, 'pix', split_axis=3, concat_axis=3, tiled=True)  20.8 us
    all_to_all x1, waiting for transfers between devices, body(): lax.all_to_all(backward_imaginary, 'pix', split_axis=3, concat_axis=3, ti...  14.3 us
    all_to_all x1, waiting for transfers between devices, body(): lax.all_to_all(backward_real, 'pix', split_axis=3, concat_axis=3, tiled=T...  13.6 us
    all_to_all x1, waiting for transfers between devices, body(): lax.all_to_all(spec_imag, 'pix', split_axis=3, concat_axis=3, tiled=True)  9.94 us
    all_to_all x1, waiting for transfers between devices, body(): lax.all_to_all(spec_real, 'pix', split_axis=3, concat_axis=3, tiled=True)  9.06 us
    all_gather x1, blocking collectives, in_one_piece(): filled, at, done = (lax.all_gather(both, axis, axis=dim, tiled=True), 0, [])  8.11 us
    all_to_all x1, starting transfers between devices, body(): lax.all_to_all(backward_imaginary, 'pix', split_axis=3, concat_axis=3, ti...  7.64 us
    all_to_all x1, starting transfers between devices, body(): lax.all_to_all(spec_imag, 'pix', split_axis=3, concat_axis=3, tiled=True)  6.72 us
  transfers between devices with their start and end apart: 5, of which 5 were waited for; matrix products, arithmetic and copies ran while one was open for 7% of the time, Pallas kernels for 0%

commit v1 on v0

v1 whole, which is shorter than its diff:
```python
import math

import jax
import jax.numpy as jnp
import numpy as np
from jax import lax
from jax.experimental import pallas as pl
from jax.experimental.pallas import tpu as pltpu
from jax.sharding import PartitionSpec as P

ABSORB_RATIO = 0.1
REGULARIZER = 0.05
SIZE = 2048
LONG = 128
SHORT = 16
NDIST = 4
WIDE = 4


def angle_tables(left, right, period):
    turns = np.outer(np.arange(left), np.arange(right)) % period
    angles = 2.0 * np.pi * turns / period
    return np.cos(angles), np.sin(angles)


def right_table():
    cosine, sine = angle_tables(SHORT, SHORT, SHORT)
    same = np.eye(WIDE)
    c, s = np.kron(same, cosine), np.kron(same, sine)
    return np.block([[c, -s], [s, c]])


def turn_lanes(table):
    half = table.shape[0] // 2
    return np.concatenate([-table[half:], table[:half]], axis=0)


def turn_after(table):
    half = table.shape[1] // 2
    return np.concatenate([table[:, half:], -table[:, :half]], axis=1)


COS, SIN = angle_tables(LONG, LONG, LONG)
RIGHT = right_table()
BACK = np.array(RIGHT.T)
ROW_TWIST = angle_tables(SHORT, LONG, SIZE)
COL_TWIST = tuple(np.tile(t, (1, 2 * WIDE)) for t in angle_tables(LONG, SHORT, SIZE))


def f32(x):
    return np.asarray(x, np.float32)


ROW_FORWARD = f32(np.concatenate([COS, SIN], axis=1))
COL_FORWARD = f32(np.concatenate([COS, SIN], axis=0))
COL_RIGHT = f32(np.concatenate([RIGHT, turn_lanes(RIGHT)], axis=0))
COL_LEFT = f32(np.concatenate([BACK, turn_after(BACK)], axis=1))
COL_BACK = f32(np.concatenate([COS, -SIN], axis=1))
ROW_BACK = f32(np.concatenate([COS, -SIN], axis=0))
ROW_TW = f32(np.stack(ROW_TWIST))
COL_TW = f32(np.stack(COL_TWIST))


def product(a, b, a_dim=1, b_dim=0):
    return lax.dot_general(
        a,
        b,
        (((a_dim,), (b_dim,)), ((), ())),
        precision=lax.Precision.HIGHEST,
        preferred_element_type=jnp.float32,
    )


def four_point(z, sign):
    (r0, i0), (r1, i1), (r2, i2), (r3, i3) = z
    ar, ai, br, bi = r0 + r2, i0 + i2, r0 - r2, i0 - i2
    cr, ci, dr, di = r1 + r3, i1 + i3, r1 - r3, i1 - i3
    if sign > 0:
        plus, minus = (br + di, bi - dr), (br - di, bi + dr)
    else:
        plus, minus = (br - di, bi + dr), (br + di, bi - dr)
    return [(ar + cr, ai + ci), plus, (ar - cr, ai - ci), minus]


def times(z, turns, sign):
    r, i = z
    if turns == 0:
        return z
    c = float(np.float32(math.cos(2 * math.pi * turns / 16)))
    s = float(np.float32(sign * math.sin(2 * math.pi * turns / 16)))
    return r * c + i * s, i * c - r * s


def sixteen_point(z, sign):
    inner = [four_point([z[4 * a + b] for a in range(4)], sign) for b in range(4)]
    out = [None] * 16
    for c in range(4):
        mixed = four_point([times(inner[b][c], b * c, sign) for b in range(4)], sign)
        for e in range(4):
            out[c + 4 * e] = mixed[e]
    return out


def row_forward(images, table, twist):
    z = [(images[0][:, LONG * j : LONG * (j + 1)], images[1][:, LONG * j : LONG * (j + 1)]) for j in range(SHORT)]
    spread = sixteen_point(z, 1)
    turned = []
    for j, (r, i) in enumerate(spread):
        c, s = twist[0][j : j + 1, :], twist[1][j : j + 1, :]
        turned.append((r * c + i * s, i * c - r * s))
    out = []
    for d in range(NDIST):
        part = turned[WIDE * d : WIDE * (d + 1)]
        re, im = [r for r, _ in part], [i for _, i in part]
        left = jnp.concatenate(re + im, axis=0)
        right = jnp.concatenate(im + [-r for r in re], axis=0)
        both = jnp.concatenate([left, right], axis=1)
        out.append(product(table, both, 1, 1))
    return jnp.concatenate(out, axis=0)


def wave(turns):
    r = turns - jnp.floor(turns + 0.5)
    r = jnp.where(r > 0.25, 0.5 - r, jnp.where(r < -0.25, -0.5 - r, r))
    x = r * (2.0 * math.pi)
    y = x * x
    p = -1.0 / 39916800.0
    for term in (1.0 / 362880.0, -1.0 / 5040.0, 1.0 / 120.0, -1.0 / 6.0, 1.0):
        p = p * y + term
    return x * p


def signed_square(index):
    shifted = jnp.where(2 * index >= SIZE, index - SIZE, index)
    fraction = shifted.astype(jnp.float32) * (1.0 / SIZE)
    return fraction * fraction


def gains(defocus, blurring, first_col):
    shape = (LONG, LONG)
    lane = lax.broadcasted_iota(jnp.int32, shape, 1)
    row = lax.broadcasted_iota(jnp.int32, shape, 0)
    squared = signed_square(row + LONG * (lane & 15)) + signed_square(first_col + ((lane >> 4) & 3))
    low = lane < LONG // 2
    amplitude = math.sqrt(1.0 + ABSORB_RATIO * ABSORB_RATIO)
    shift = math.atan(ABSORB_RATIO) / (2.0 * math.pi)
    out = []
    for d in range(0, NDIST, 2):
        focus = jnp.where(low, defocus[d], defocus[d + 1]) * (1.0 / (2.0 * math.pi))
        blur = jnp.where(low, blurring[d], blurring[d + 1])
        g = (amplitude * jnp.exp(-blur * squared)) * wave(focus * squared + shift)
        other = jnp.concatenate([g[:, LONG // 2 :], g[:, : LONG // 2]], axis=1)
        out += [jnp.where(low, g, other), jnp.where(low, other, g)]
    return out


def column_middle(x, gain, forward, right, left, back, twist):
    c, s = twist[0], twist[1]
    parts = []
    for d in range(NDIST):
        both = product(forward, x[LONG * d : LONG * (d + 1)])
        u, v = both[:LONG], both[LONG:]
        parts.append(jnp.concatenate([u * c - v * s, v * c + u * s], axis=1))
    spectra = product(jnp.concatenate(parts, axis=0), right)
    numerator = gain[0] * spectra[:LONG]
    weight = gain[0] * gain[0]
    for d in range(1, NDIST):
        numerator = numerator + gain[d] * spectra[LONG * d : LONG * (d + 1)]
        weight = weight + gain[d] * gain[d]
    quotient = numerator / (2.0 * (weight + REGULARIZER))
    both = product(quotient, left)
    a, b = both[:, :LONG], both[:, LONG:]
    upright = jnp.concatenate([a * c - b * s, b * c + a * s], axis=0)
    return product(back, upright)


def row_back(x, table, twist):
    z = []
    scale = 1.0 / (SIZE * SIZE)
    for d in range(NDIST):
        t = x[LONG * d : LONG * (d + 1)].T
        half = LONG // 2
        turned = jnp.concatenate([t[half:], -t[:half]], axis=0)
        o = product(jnp.concatenate([t, turned], axis=1), table)
        for j in range(WIDE):
            r = o[SHORT * j : SHORT * (j + 1)]
            i = o[half + SHORT * j : half + SHORT * (j + 1)]
            v = WIDE * d + j
            c, s = twist[0][v : v + 1, :] * scale, twist[1][v : v + 1, :] * scale
            z.append((r * c - i * s, i * c + r * s))
    return sixteen_point(z, -1)


def first_kernel(images, table, twist, out):
    out[...] = row_forward(images[...], table[...], twist[...])


def middle_kernel(par, x, forward, right, left, back, twist, out):
    first_col = SHORT * lax.axis_index("pix") + WIDE * lax.axis_index("dist")
    table = gains([par[d, 0] for d in range(NDIST)], [par[d, 1] for d in range(NDIST)], first_col)
    out[...] = column_middle(x[...], table, forward[...], right[...], left[...], back[...], twist[...])


def last_kernel(x, table, twist, out):
    for j, (r, i) in enumerate(row_back(x[...], table[...], twist[...])):
        out[0, :, LONG * j : LONG * (j + 1)] = r
        out[1, :, LONG * j : LONG * (j + 1)] = i


def call(kernel, shape, name, smem_first=False):
    def run(*args):
        specs = [pl.BlockSpec(memory_space=pltpu.VMEM) for _ in args]
        if smem_first:
            specs[0] = pl.BlockSpec(memory_space=pltpu.SMEM)
        return pl.pallas_call(
            kernel,
            out_shape=jax.ShapeDtypeStruct(shape, jnp.float32),
            in_specs=specs,
            out_specs=pl.BlockSpec(memory_space=pltpu.VMEM),
            name=name,
        )(*args)

    return run


def body(contrast, defocus, blurring):
    par = lax.all_gather(jnp.stack([defocus, blurring], axis=1), "dist", axis=0, tiled=True)
    sent = call(first_kernel, (NDIST * LONG, LONG), "rows_forward")(contrast[0], ROW_FORWARD, ROW_TW)
    got = lax.all_to_all(sent.reshape(NDIST * LONG, 1, LONG), ("dist", "pix"), 0, 0, tiled=True)
    middle = call(middle_kernel, (LONG, LONG), "columns", True)(
        par, got.reshape(NDIST * LONG, LONG), COL_FORWARD, COL_RIGHT, COL_LEFT, COL_BACK, COL_TW
    )
    mine = lax.all_to_all(middle.reshape(LONG, 1, LONG), "pix", 0, 0, tiled=True).reshape(LONG, LONG)
    whole = lax.all_gather(mine, "dist", axis=0, tiled=True)
    return call(last_kernel, (2, SHORT, SIZE), "rows_back")(whole, ROW_BACK, ROW_TW)


def solution(mesh):
    return jax.shard_map(
        body,
        mesh=mesh,
        in_specs=(P("dist", None, "pix", None), P("dist"), P("dist")),
        out_specs=P(None, "pix", None),
        check_vma=False,
    )
```

time: 137 us -> 77.7 us (0.57)
  waiting for transfers between devices: 53.2 us -> 5.56 us
  blocking collectives: 8.11 us -> 39.2 us
  starting transfers between devices: 47.5 us -> 22.2 us
  matrix products: 13.6 us -> 0 us
  Pallas kernels: 0 us -> 8.38 us
  local copies, waits for them, and re-layouts: 8 us -> 0.7 us
  other arithmetic: 4.25 us -> 0.07 us
    all_to_all x5 -> x1, waiting for transfers between devices: 53.2 us -> 5.56 us  [body(): lax.all_to_all(sent.reshape(NDIST * LONG, 1, LONG), ('dist', 'pix'), 0, 0...]
    all_to_all x5 -> x1, starting transfers between devices: 47.5 us -> 22.2 us  [body(): lax.all_to_all(sent.reshape(NDIST * LONG, 1, LONG), ('dist', 'pix'), 0, 0...]
    all_to_all x0 -> x1, blocking collectives: none -> 22 us  [body(): lax.all_to_all(middle.reshape(LONG, 1, LONG), 'pix', 0, 0, tiled=True)]
    dot_general x32 -> x0, matrix products: 13.6 us -> none  [the longest x7 3.3 us: complex_product(): jnp.einsum(pattern, imag_part, cosine, precision=lax.Precision.HIGHEST)]
    all_gather x1 -> x2, blocking collectives: 8.11 us -> 17.2 us  [the longest x1 9.63 us: body(): lax.all_gather(jnp.stack([defocus, blurring], axis=1), 'dist', axis=0, ti...]
    pallas_call x0 -> x3, Pallas kernels: none -> 8.38 us  [run(): pl.pallas_call(kernel, out_shape=jax.ShapeDtypeStruct(shape, jnp.float32)...]
    unnamed x7 -> x2, local copies, waits for them, and re-layouts: 3.78 us -> 0.7 us
    all_to_all x2 -> x0, other arithmetic: 1.9 us -> none  [the longest x1 0.95 us: body(): lax.all_to_all(spec_imag, 'pix', split_axis=3, concat_axis=3, tiled=True)]
  transfers between devices with their start and end apart: 5 -> 1, of which waited for: 5 -> 1; matrix products, arithmetic and copies ran while one was open for 7% -> 0% of each run, Pallas kernels for 0% -> 0%
where the time goes in v1:
time: 77.7 us; the launch traced here: 77.4 us
  blocking collectives  39.2 us (50%)
  starting transfers between devices  22.2 us (29%)
  Pallas kernels  8.38 us (11%)
  waiting for transfers between devices  5.56 us (7%)
  between operations  1.31 us (2%)
    all_to_all x1, starting transfers between devices, body(): lax.all_to_all(sent.reshape(NDIST * LONG, 1, LONG), ('dist', 'pix'), 0, 0...  22.2 us
    all_to_all x1, blocking collectives, body(): lax.all_to_all(middle.reshape(LONG, 1, LONG), 'pix', 0, 0, tiled=True)  22 us
    all_gather x1, blocking collectives, body(): lax.all_gather(jnp.stack([defocus, blurring], axis=1), 'dist', axis=0, ti...  9.63 us
    pallas_call x3, Pallas kernels, run(): pl.pallas_call(kernel, out_shape=jax.ShapeDtypeStruct(shape, jnp.float32)...  8.38 us
    all_gather x1, blocking collectives, body(): whole = lax.all_gather(mine, 'dist', axis=0, tiled=True)  7.62 us
    all_to_all x1, waiting for transfers between devices, body(): lax.all_to_all(sent.reshape(NDIST * LONG, 1, LONG), ('dist', 'pix'), 0, 0...  5.56 us
  transfers between devices with their start and end apart: 1, of which 1 were waited for; matrix products, arithmetic and copies ran while one was open for 0% of the time, Pallas kernels for 0%

profile of v1, /device:TPU:1, one launch (start us, length us, event | category | flops | bytes accessed | tf_op | source)
XLA Modules:
  0.0 77.4 jit_solution(10088581533185664986)
XLA Ops:
  0.0 2.4 %rows_forward.1 = f32[512,128]{1,0:T(8,128)} custom-call(f32[2,16,2048]{2,1,0:T(8,128)} %bitcast.21, f32[128,256]{1,0:T(8,128)} %constant.16.clone.table, f32[2,16,128]{2,1,0:T(8,128)} %constant.17.clone.twist), custom_call_target="tpu_custom_call" | custom-call | tf_op jit(solution)/shard_map/rows_forward/pallas_call | solution.py:215
  2.4 22.2 %all-to-all-start = ((f32[512,1,128]{2,1,0:T(1,128)}), f32[512,1,128]{2,1,0:T(1,128)S(1)}, u32[]{:S(2)}, u32[]{:S(2)}) async-start(f32[512,1,128]{2,1,0:T(1,128)} %bitcast.19), calls=%async_computation | async-start | bytes 524288 | tf_op jit(solution)/shard_map/all_to_all | solution.py:229
  25.8 0.1 maximum_bitcast_fusion
  25.9 9.6 %all-gather.1 = f32[4,1,2]{2,1,0:T(1,128)} all-gather(f32[1,1,2]{2,1,0:T(1,128)S(1)} %maximum_bitcast_fusion), channel_id=1, replica_groups=mesh['dist'=4,'pix'=128] {'dist'}, dimensions={0}, use_global_device_ids=true | all-gather | bytes 40 | tf_op jit(solution)/shard_map/all_gather | solution.py:227
  35.5 5.6 %all-to-all-done = f32[512,1,128]{2,1,0:T(1,128)S(1)} async-done(((f32[512,1,128]{2,1,0:T(1,128)}), f32[512,1,128]{2,1,0:T(1,128)S(1)}, u32[]{:S(2)}, u32[]{:S(2)}) %all-to-all-start) | async-done | bytes 262176 | tf_op jit(solution)/shard_map/all_to_all | solution.py:229
  41.1 0.0 copy-start
  41.1 0.7 copy-done
  41.8 3.6 %columns.1 = f32[128,128]{1,0:T(8,128)} custom-call(f32[4,2]{1,0:T(4,128)} %bitcast.23, f32[512,128]{1,0:T(8,128)} %bitcast.18, f32[256,128]{1,0:T(8,128)} %constant.18.clone.forward, f32[256,128]{1,0:T(8,128)} %constant.19.clone.right, f32[128,256]{1,0:T(8,128)} %constant.20.clone.left, f32[128,256]{1,0:T(8,128)} %constant.21.clone.back, ...), custom_call_target="tpu_custom_call" | custom-call | tf_op jit(solution)/shard_map/columns/pallas_call | solution.py:215
  45.4 22.0 %all_to_all.10 = f32[128,1,128]{2,1,0:T(1,128)S(1)} all-to-all(f32[128,1,128]{2,1,0:T(1,128)} %bitcast.22), channel_id=1, replica_groups=mesh['dist'=4,'pix'=128] {'pix'}, dimensions={0} | all-to-all | bytes 131072 | tf_op jit(solution)/shard_map/all_to_all | solution.py:233
  67.4 7.6 %all-gather = f32[512,1,128]{2,0,1:T(8,128)} all-gather(f32[128,1,128]{2,0,1:T(8,128)S(1)} %bitcast.20), channel_id=2, replica_groups=mesh['dist'=4,'pix'=128] {'dist'}, dimensions={0}, use_global_device_ids=true | all-gather | bytes 327680 | tf_op jit(solution)/shard_map/all_gather | solution.py:234
  75.0 2.4 %rows_back.1 = f32[2,16,2048]{2,1,0:T(8,128)} custom-call(f32[512,128]{1,0:T(8,128)} %bitcast.17, f32[256,128]{1,0:T(8,128)} %constant.23.clone.table, f32[2,16,128]{2,1,0:T(8,128)} %constant.17.clone.twist), custom_call_target="tpu_custom_call" | custom-call | tf_op jit(solution)/shard_map/rows_back/pallas_call | solution.py:215
Async XLA Ops:
  2.4 38.7 %all-to-all-start = ((f32[512,1,128]{2,1,0:T(1,128)}), f32[512,1,128]{2,1,0:T(1,128)S(1)}, u32[]{:S(2)}, u32[]{:S(2)}) async-start(f32[512,1,128]{2,1,0:T(1,128)} %bitcast.19), calls=%async_computation | async-start | bytes 524288 | tf_op jit(solution)/shard_map/all_to_all | solution.py:229
  41.1 0.7 copy-start

commit v2 on v1

--- a/solution.py
+++ b/solution.py
@@ -15,6 +15,7 @@
 SHORT = 16
 NDIST = 4
 WIDE = 4
+VMEM_LIMIT = 8 << 20
 
 
 def angle_tables(left, right, period):
@@ -154,11 +155,11 @@
     return out
 
 
-def column_middle(x, gain, forward, right, left, back, twist):
+def column_middle(blocks, gain, forward, right, left, back, twist):
     c, s = twist[0], twist[1]
     parts = []
-    for d in range(NDIST):
-        both = product(forward, x[LONG * d : LONG * (d + 1)])
+    for x in blocks:
+        both = product(forward, x)
         u, v = both[:LONG], both[LONG:]
         parts.append(jnp.concatenate([u * c - v * s, v * c + u * s], axis=1))
     spectra = product(jnp.concatenate(parts, axis=0), right)
@@ -191,14 +192,25 @@
     return sixteen_point(z, -1)
 
 
-def first_kernel(images, table, twist, out):
+def first_kernel(images, defocus, blurring, table, twist, out, own):
     out[...] = row_forward(images[...], table[...], twist[...])
-
-
-def middle_kernel(par, x, forward, right, left, back, twist, out):
-    first_col = SHORT * lax.axis_index("pix") + WIDE * lax.axis_index("dist")
-    table = gains([par[d, 0] for d in range(NDIST)], [par[d, 1] for d in range(NDIST)], first_col)
-    out[...] = column_middle(x[...], table, forward[...], right[...], left[...], back[...], twist[...])
+    lane = lax.broadcasted_iota(jnp.int32, own.shape, 1)
+    own[...] = jnp.where(lane < LONG // 2, defocus[0], blurring[0])
+
+
+def middle_kernel(par0, par1, par2, par3, x, forward, right, left, back, twist, out):
+    distance = lax.axis_index("dist")
+    first_col = SHORT * lax.axis_index("pix") + WIDE * distance
+    half = LONG // 2
+    pars = [p[...] for p in (par0, par1, par2, par3)]
+    table = gains([p[:1, :1] for p in pars], [p[:1, half : half + 1] for p in pars], first_col)
+    blocks = []
+    for j in range(NDIST):
+        start = pl.multiple_of(LONG * (distance ^ j), LONG)
+        blocks.append(x[pl.ds(start, LONG), :])
+    y = column_middle(blocks, table, forward[...], right[...], left[...], back[...], twist[...])
+    for j in range(NDIST):
+        out[LONG * j : LONG * (j + 1), :] = y
 
 
 def last_kernel(x, table, twist, out):
@@ -207,32 +219,39 @@
         out[1, :, LONG * j : LONG * (j + 1)] = i
 
 
-def call(kernel, shape, name, smem_first=False):
+def call(kernel, shapes, name, smem=()):
     def run(*args):
-        specs = [pl.BlockSpec(memory_space=pltpu.VMEM) for _ in args]
-        if smem_first:
-            specs[0] = pl.BlockSpec(memory_space=pltpu.SMEM)
+        specs = [pl.BlockSpec(memory_space=pltpu.SMEM if i in smem else pltpu.VMEM) for i in range(len(args))]
         return pl.pallas_call(
             kernel,
-            out_shape=jax.ShapeDtypeStruct(shape, jnp.float32),
+            out_shape=[jax.ShapeDtypeStruct(shape, jnp.float32) for shape in shapes],
             in_specs=specs,
-            out_specs=pl.BlockSpec(memory_space=pltpu.VMEM),
+            out_specs=[pl.BlockSpec(memory_space=pltpu.VMEM) for _ in shapes],
+            compiler_params=pltpu.CompilerParams(vmem_limit_bytes=VMEM_LIMIT),
             name=name,
         )(*args)
 
     return run
 
 
+def exchange(x):
+    return lax.all_to_all(x.reshape(x.shape[0], 1, LONG), ("dist", "pix"), 0, 0, tiled=True).reshape(x.shape)
+
+
 def body(contrast, defocus, blurring):
-    par = lax.all_gather(jnp.stack([defocus, blurring], axis=1), "dist", axis=0, tiled=True)
-    sent = call(first_kernel, (NDIST * LONG, LONG), "rows_forward")(contrast[0], ROW_FORWARD, ROW_TW)
-    got = lax.all_to_all(sent.reshape(NDIST * LONG, 1, LONG), ("dist", "pix"), 0, 0, tiled=True)
-    middle = call(middle_kernel, (LONG, LONG), "columns", True)(
-        par, got.reshape(NDIST * LONG, LONG), COL_FORWARD, COL_RIGHT, COL_LEFT, COL_BACK, COL_TW
-    )
-    mine = lax.all_to_all(middle.reshape(LONG, 1, LONG), "pix", 0, 0, tiled=True).reshape(LONG, LONG)
-    whole = lax.all_gather(mine, "dist", axis=0, tiled=True)
-    return call(last_kernel, (2, SHORT, SIZE), "rows_back")(whole, ROW_BACK, ROW_TW)
+    rows = NDIST * LONG
+    sent, own = call(first_kernel, ((rows, LONG), (8, LONG)), "rows_forward", (1, 2))(
+        contrast[0], defocus, blurring, ROW_FORWARD, ROW_TW
+    )
+    pars = [own]
+    for j in range(1, NDIST):
+        pars.append(lax.ppermute(own, "dist", [(i, i ^ j) for i in range(NDIST)]))
+    got = exchange(sent)
+    (middle,) = call(middle_kernel, ((rows, LONG),), "columns")(
+        *pars, got, COL_FORWARD, COL_RIGHT, COL_LEFT, COL_BACK, COL_TW
+    )
+    whole = exchange(middle)
+    return call(last_kernel, ((2, SHORT, SIZE),), "rows_back")(whole, ROW_BACK, ROW_TW)[0]
 
 
 def solution(mesh):

time: 77.7 us -> 74.8 us (0.963)
  blocking collectives: 39.2 us -> 27.9 us
  starting transfers between devices: 22.2 us -> 33.5 us
  Pallas kernels: 8.38 us -> 4.55 us
  local copies, waits for them, and re-layouts: 0.7 us -> 1.88 us
    all_gather x2 -> x0, blocking collectives: 17.2 us -> none  [the longest x1 9.63 us: body(): lax.all_gather(jnp.stack([defocus, blurring], axis=1), 'dist', axis=0, ti...]
    ppermute x0 -> x3, starting transfers between devices: none -> 11.4 us  [body(): pars.append(lax.ppermute(own, 'dist', [(i, i ^ j) for i in range(NDIST)]))]
    all_to_all x1, blocking collectives: 22 us -> 27.9 us  [exchange(): lax.all_to_all(x.reshape(x.shape[0], 1, LONG), ('dist', 'pix'), 0, 0, til...]
    pallas_call x3, Pallas kernels: 8.38 us -> 4.55 us  [run(): pl.pallas_call(kernel, out_shape=[jax.ShapeDtypeStruct(shape, jnp.float32...]
    all_to_all x1, waiting for transfers between devices: 5.56 us -> 4.01 us  [exchange(): lax.all_to_all(x.reshape(x.shape[0], 1, LONG), ('dist', 'pix'), 0, 0, til...]
    unnamed x2 -> x18, local copies, waits for them, and re-layouts: 0.7 us -> 1.88 us
    ppermute x0 -> x3, waiting for transfers between devices: none -> 1.12 us  [body(): pars.append(lax.ppermute(own, 'dist', [(i, i ^ j) for i in range(NDIST)]))]
  transfers between devices with their start and end apart: 1 -> 4, of which waited for: 1 -> 2; matrix products, arithmetic and copies ran while one was open for 0% -> 0% of each run, Pallas kernels for 0% -> 0%
where the time goes in v2:
time: 74.8 us; the launch traced here: 74.4 us
  starting transfers between devices  33.5 us (45%)
  blocking collectives  27.9 us (37%)
  waiting for transfers between devices  5.13 us (7%)
  Pallas kernels  4.55 us (6%)
  local copies, waits for them, and re-layouts  1.88 us (3%)
  between operations  1.41 us (2%)
    all_to_all x1, blocking collectives, exchange(): lax.all_to_all(x.reshape(x.shape[0], 1, LONG), ('dist', 'pix'), 0, 0, til...  27.9 us
    all_to_all x1, starting transfers between devices, exchange(): lax.all_to_all(x.reshape(x.shape[0], 1, LONG), ('dist', 'pix'), 0, 0, til...  22.2 us
    ppermute x3, starting transfers between devices, body(): pars.append(lax.ppermute(own, 'dist', [(i, i ^ j) for i in range(NDIST)]))  11.4 us
    pallas_call x3, Pallas kernels, run(): pl.pallas_call(kernel, out_shape=[jax.ShapeDtypeStruct(shape, jnp.float32...  4.55 us
    all_to_all x1, waiting for transfers between devices, exchange(): lax.all_to_all(x.reshape(x.shape[0], 1, LONG), ('dist', 'pix'), 0, 0, til...  4.01 us
    unnamed x18, local copies, waits for them, and re-layouts  1.88 us
  transfers between devices with their start and end apart: 4, of which 2 were waited for; matrix products, arithmetic and copies ran while one was open for 0% of the time, Pallas kernels for 0%

profile of v2, /device:TPU:1, one launch (start us, length us, event | category | flops | bytes accessed | tf_op | source)
XLA Modules:
  0.0 74.4 jit_solution(5436238785486764803)
XLA Ops:
  0.0 0.0 copy-start.8
  1.3 0.0 copy-done.8
  1.3 0.0 copy-start
  1.3 0.9 %copy-done = f32[1,2,16,2048]{3,2,1,0:T(8,128)S(1)} copy-done((f32[1,2,16,2048]{3,2,1,0:T(8,128)S(1)}, f32[1,2,16,2048]{3,2,1,0:T(8,128)}, u32[]{:S(2)}) %copy-start) | copy-done | bytes 262168
  2.3 0.0 copy-start.6
  2.3 0.9 %copy-done.6 = f32[128,256]{1,0:T(8,128)S(1)} copy-done((f32[128,256]{1,0:T(8,128)S(1)}, f32[128,256]{1,0:T(8,128)}, u32[]{:S(2)}) %copy-start.6) | copy-done | bytes 131096
  3.2 0.0 copy-start.5
  3.2 1.3 %rows_forward.1 = (f32[512,128]{1,0:T(8,128)}, f32[8,128]{1,0:T(8,128)S(1)}) custom-call(f32[2,16,2048]{2,1,0:T(8,128)S(1)} %bitcast.12, f32[1]{0:T(128)S(6)} %copy.14.defocus, f32[1]{0:T(128)S(6)} %copy.15.blurring, f32[128,256]{1,0:T(8,128)S(1)} %copy-done.6, f32[2,16,128]{2,1,0:T(8,128)S(1)} %copy-done.8), custom_call_target="tpu_custom_call" | custom-call | tf_op jit(solution)/shard_map/rows_forward/pallas_call | solution.py:225
  4.5 0.0 copy-start.1
  4.5 0.0 copy-start.2
  4.5 0.0 copy-start.3
  4.5 0.0 copy-start.4
  4.5 22.2 %all-to-all-start = ((f32[512,1,128]{2,1,0:T(1,128)}), f32[512,1,128]{2,1,0:T(1,128)S(1)}, u32[]{:S(2)}, u32[]{:S(2)}) async-start(f32[512,1,128]{2,1,0:T(1,128)} %bitcast.2), calls=%async_computation | async-start | bytes 524288 | tf_op jit(solution)/shard_map/all_to_all | solution.py:238
  26.7 3.5 %collective-permute-start.2 = (f32[8,128]{1,0:T(8,128)S(1)}, f32[8,128]{1,0:T(8,128)S(1)}, u32[]{:S(2)}, u32[]{:S(2)}) collective-permute-start(f32[8,128]{1,0:T(8,128)S(1)} %get-tuple-element.7.par0), channel_id=1, source_target_pairs={{0,384},{128,256},{256,128},{384,0},{1,385},{129,257},{257,129},{3... | collective-permute-start | bytes 12296 | tf_op jit(solution)/shard_map/ppermute | solution.py:248
  30.2 5.9 %collective-permute-start.1 = (f32[8,128]{1,0:T(8,128)S(1)}, f32[8,128]{1,0:T(8,128)S(1)}, u32[]{:S(2)}, u32[]{:S(2)}) collective-permute-start(f32[8,128]{1,0:T(8,128)S(1)} %get-tuple-element.7.par0), channel_id=1, source_target_pairs={{0,256},{128,384},{256,0},{384,128},{1,257},{129,385},{257,1},{385... | collective-permute-start | bytes 12296 | tf_op jit(solution)/shard_map/ppermute | solution.py:248
  36.2 1.9 %collective-permute-start = (f32[8,128]{1,0:T(8,128)S(1)}, f32[8,128]{1,0:T(8,128)S(1)}, u32[]{:S(2)}, u32[]{:S(2)}) collective-permute-start(f32[8,128]{1,0:T(8,128)S(1)} %get-tuple-element.7.par0), channel_id=1, source_target_pairs={{0,128},{128,0},{256,384},{384,256},{1,129},{129,1},{257,385},{385... | collective-permute-start | bytes 12296 | tf_op jit(solution)/shard_map/ppermute | solution.py:248
  38.1 0.0 collective-permute-done.2.par3
  38.1 0.0 collective-permute-done.1.par2
  38.1 1.1 %collective-permute-done.par1 = f32[8,128]{1,0:T(8,128)S(1)} collective-permute-done((f32[8,128]{1,0:T(8,128)S(1)}, f32[8,128]{1,0:T(8,128)S(1)}, u32[]{:S(2)}, u32[]{:S(2)}) %collective-permute-start) | collective-permute-done | bytes 4128 | tf_op jit(solution)/shard_map/ppermute | solution.py:248
  39.2 4.0 %all-to-all-done = f32[512,1,128]{2,1,0:T(1,128)S(1)} async-done(((f32[512,1,128]{2,1,0:T(1,128)}), f32[512,1,128]{2,1,0:T(1,128)S(1)}, u32[]{:S(2)}, u32[]{:S(2)}) %all-to-all-start) | async-done | bytes 262176 | tf_op jit(solution)/shard_map/all_to_all | solution.py:238
  43.3 0.0 copy-done.5
  43.3 0.0 copy-done.1
  43.3 0.0 copy-done.2
  43.3 0.0 copy-done.3
  43.3 0.0 copy-done.4
  43.3 1.8 %columns.1 = f32[512,128]{1,0:T(8,128)S(1)} custom-call(f32[8,128]{1,0:T(8,128)S(1)} %get-tuple-element.7.par0, f32[8,128]{1,0:T(8,128)S(1)} %collective-permute-done.par1, f32[8,128]{1,0:T(8,128)S(1)} %collective-permute-done.1.par2, f32[8,128]{1,0:T(8,128)S(1)} %collective-permute-done.2.par3, f32[512,128]{1,0:T(8,128)S(1)} %bitcast.9, ...), custom_call_target="tpu_custom_call" | custom-call | tf_op jit(solution)/shard_map/columns/pallas_call | solution.py:225
  45.1 0.0 copy-start.7
  45.1 27.9 %all_to_all.10 = f32[512,1,128]{2,1,0:T(1,128)S(1)} all-to-all(f32[512,1,128]{2,1,0:T(1,128)S(1)} %bitcast.10), channel_id=1, replica_groups=mesh['dist'=4,'pix'=128] {'dist','pix'}, dimensions={0} | all-to-all | bytes 524288 | tf_op jit(solution)/shard_map/all_to_all | solution.py:238
  73.0 0.0 copy-done.7
  73.0 1.4 %rows_back.1 = f32[2,16,2048]{2,1,0:T(8,128)} custom-call(f32[512,128]{1,0:T(8,128)S(1)} %bitcast.11, f32[256,128]{1,0:T(8,128)S(1)} %copy-done.7, f32[2,16,128]{2,1,0:T(8,128)S(1)} %copy-done.8), custom_call_target="tpu_custom_call" | custom-call | tf_op jit(solution)/shard_map/rows_back/pallas_call | solution.py:225
Async XLA Ops:
  0.0 1.3 %copy-start.8 = (f32[2,16,128]{2,1,0:T(8,128)S(1)}, f32[2,16,128]{2,1,0:T(8,128)}, u32[]{:S(2)}) copy-start(f32[2,16,128]{2,1,0:T(8,128)} %constant.17.clone.twist) | copy-start | bytes 49156
  1.3 1.0 %copy-start = (f32[1,2,16,2048]{3,2,1,0:T(8,128)S(1)}, f32[1,2,16,2048]{3,2,1,0:T(8,128)}, u32[]{:S(2)}) copy-start(f32[1,2,16,2048]{3,2,1,0:T(8,128)} %param.11) | copy-start | bytes 786436
  2.3 0.9 %copy-start.6 = (f32[128,256]{1,0:T(8,128)S(1)}, f32[128,256]{1,0:T(8,128)}, u32[]{:S(2)}) copy-start(f32[128,256]{1,0:T(8,128)} %constant.16.clone.table) | copy-start | bytes 393220
  3.2 40.1 %copy-start.5 = (f32[256,128]{1,0:T(8,128)S(1)}, f32[256,128]{1,0:T(8,128)}, u32[]{:S(2)}) copy-start(f32[256,128]{1,0:T(8,128)} %constant.18.clone.forward) | copy-start | bytes 393220
  4.5 38.7 %copy-start.1 = (f32[2,128,128]{2,1,0:T(8,128)S(1)}, f32[2,128,128]{2,1,0:T(8,128)}, u32[]{:S(2)}) copy-start(f32[2,128,128]{2,1,0:T(8,128)} %constant.22.clone.twist) | copy-start | bytes 393220
  4.5 38.7 %copy-start.2 = (f32[128,256]{1,0:T(8,128)S(1)}, f32[128,256]{1,0:T(8,128)}, u32[]{:S(2)}) copy-start(f32[128,256]{1,0:T(8,128)} %constant.21.clone.back) | copy-start | bytes 393220
  4.5 38.7 %copy-start.3 = (f32[128,256]{1,0:T(8,128)S(1)}, f32[128,256]{1,0:T(8,128)}, u32[]{:S(2)}) copy-start(f32[128,256]{1,0:T(8,128)} %constant.20.clone.left) | copy-start | bytes 393220
  4.5 38.7 %copy-start.4 = (f32[256,128]{1,0:T(8,128)S(1)}, f32[256,128]{1,0:T(8,128)}, u32[]{:S(2)}) copy-start(f32[256,128]{1,0:T(8,128)} %constant.19.clone.right) | copy-start | bytes 393220
  4.5 38.7 %all-to-all-start = ((f32[512,1,128]{2,1,0:T(1,128)}), f32[512,1,128]{2,1,0:T(1,128)S(1)}, u32[]{:S(2)}, u32[]{:S(2)}) async-start(f32[512,1,128]{2,1,0:T(1,128)} %bitcast.2), calls=%async_computation | async-start | bytes 524288 | tf_op jit(solution)/shard_map/all_to_all | solution.py:238
  26.7 11.4 %collective-permute-start.2 = (f32[8,128]{1,0:T(8,128)S(1)}, f32[8,128]{1,0:T(8,128)S(1)}, u32[]{:S(2)}, u32[]{:S(2)}) collective-permute-start(f32[8,128]{1,0:T(8,128)S(1)} %get-tuple-element.7.par0), channel_id=1, source_target_pairs={{0,384},{128,256},{256,128},{384,0},{1,385},{129,257},{257,129},{3... | collective-permute-start | bytes 12296 | tf_op jit(solution)/shard_map/ppermute | solution.py:248
  30.2 7.9 %collective-permute-start.1 = (f32[8,128]{1,0:T(8,128)S(1)}, f32[8,128]{1,0:T(8,128)S(1)}, u32[]{:S(2)}, u32[]{:S(2)}) collective-permute-start(f32[8,128]{1,0:T(8,128)S(1)} %get-tuple-element.7.par0), channel_id=1, source_target_pairs={{0,256},{128,384},{256,0},{384,128},{1,257},{129,385},{257,1},{385... | collective-permute-start | bytes 12296 | tf_op jit(solution)/shard_map/ppermute | solution.py:248
  36.2 3.1 %collective-permute-start = (f32[8,128]{1,0:T(8,128)S(1)}, f32[8,128]{1,0:T(8,128)S(1)}, u32[]{:S(2)}, u32[]{:S(2)}) collective-permute-start(f32[8,128]{1,0:T(8,128)S(1)} %get-tuple-element.7.par0), channel_id=1, source_target_pairs={{0,128},{128,0},{256,384},{384,256},{1,129},{129,1},{257,385},{385... | collective-permute-start | bytes 12296 | tf_op jit(solution)/shard_map/ppermute | solution.py:248
  45.1 27.9 %copy-start.7 = (f32[256,128]{1,0:T(8,128)S(1)}, f32[256,128]{1,0:T(8,128)}, u32[]{:S(2)}) copy-start(f32[256,128]{1,0:T(8,128)} %constant.23.clone.table) | copy-start | bytes 393220

commit v3 on v1

--- a/solution.py
+++ b/solution.py
@@ -6,6 +6,7 @@
 from jax import lax
 from jax.experimental import pallas as pl
 from jax.experimental.pallas import tpu as pltpu
+from jax.sharding import Mesh
 from jax.sharding import PartitionSpec as P
 
 ABSORB_RATIO = 0.1
@@ -15,6 +16,11 @@
 SHORT = 16
 NDIST = 4
 WIDE = 4
+VMEM_LIMIT = 8 << 20
+DIST = ("l", "c")
+PIX = ("z", "x", "h")
+PIX_SIZES = (8, 4, 4)
+BACK_ORDER = np.arange(LONG).reshape(PIX_SIZES).transpose(2, 1, 0).reshape(-1)
 
 
 def angle_tables(left, right, period):
@@ -55,8 +61,8 @@
 COL_FORWARD = f32(np.concatenate([COS, SIN], axis=0))
 COL_RIGHT = f32(np.concatenate([RIGHT, turn_lanes(RIGHT)], axis=0))
 COL_LEFT = f32(np.concatenate([BACK, turn_after(BACK)], axis=1))
-COL_BACK = f32(np.concatenate([COS, -SIN], axis=1))
-ROW_BACK = f32(np.concatenate([COS, -SIN], axis=0))
+COL_BACK = f32(np.concatenate([COS, -SIN], axis=1)[BACK_ORDER])
+ROW_BACK = f32(np.concatenate([COS[BACK_ORDER], -SIN[BACK_ORDER]], axis=0))
 ROW_TW = f32(np.stack(ROW_TWIST))
 COL_TW = f32(np.stack(COL_TWIST))
 
@@ -154,11 +160,11 @@
     return out
 
 
-def column_middle(x, gain, forward, right, left, back, twist):
+def column_middle(blocks, gain, forward, right, left, back, twist):
     c, s = twist[0], twist[1]
     parts = []
-    for d in range(NDIST):
-        both = product(forward, x[LONG * d : LONG * (d + 1)])
+    for x in blocks:
+        both = product(forward, x)
         u, v = both[:LONG], both[LONG:]
         parts.append(jnp.concatenate([u * c - v * s, v * c + u * s], axis=1))
     spectra = product(jnp.concatenate(parts, axis=0), right)
@@ -178,7 +184,8 @@
     z = []
     scale = 1.0 / (SIZE * SIZE)
     for d in range(NDIST):
-        t = x[LONG * d : LONG * (d + 1)].T
+        start = LONG * (2 * (d % 2) + d // 2)
+        t = x[start : start + LONG].T
         half = LONG // 2
         turned = jnp.concatenate([t[half:], -t[:half]], axis=0)
         o = product(jnp.concatenate([t, turned], axis=1), table)
@@ -191,14 +198,26 @@
     return sixteen_point(z, -1)
 
 
-def first_kernel(images, table, twist, out):
+def pair_kernel(defocus, blurring, out):
+    lane = lax.broadcasted_iota(jnp.int32, out.shape, 1)
+    out[...] = jnp.where(lane < LONG // 2, defocus[...], blurring[...])
+
+
+def first_kernel(images, par, table, twist, out, par_out):
     out[...] = row_forward(images[...], table[...], twist[...])
+    par_out[...] = par[...]
 
 
 def middle_kernel(par, x, forward, right, left, back, twist, out):
-    first_col = SHORT * lax.axis_index("pix") + WIDE * lax.axis_index("dist")
-    table = gains([par[d, 0] for d in range(NDIST)], [par[d, 1] for d in range(NDIST)], first_col)
-    out[...] = column_middle(x[...], table, forward[...], right[...], left[...], back[...], twist[...])
+    first_col = SHORT * lax.axis_index(PIX) + WIDE * lax.axis_index(DIST)
+    half = LONG // 2
+    defocus = [par[8 * d : 8 * d + 1, :1] for d in range(NDIST)]
+    blurring = [par[8 * d : 8 * d + 1, half : half + 1] for d in range(NDIST)]
+    table = gains(defocus, blurring, first_col)
+    blocks = [x[LONG * d : LONG * (d + 1), :] for d in range(NDIST)]
+    y = column_middle(blocks, table, forward[...], right[...], left[...], back[...], twist[...])
+    out[:LONG, :] = y
+    out[LONG:, :] = y
 
 
 def last_kernel(x, table, twist, out):
@@ -207,39 +226,44 @@
         out[1, :, LONG * j : LONG * (j + 1)] = i
 
 
-def call(kernel, shape, name, smem_first=False):
+def call(kernel, shapes, name, limit=VMEM_LIMIT):
     def run(*args):
-        specs = [pl.BlockSpec(memory_space=pltpu.VMEM) for _ in args]
-        if smem_first:
-            specs[0] = pl.BlockSpec(memory_space=pltpu.SMEM)
         return pl.pallas_call(
             kernel,
-            out_shape=jax.ShapeDtypeStruct(shape, jnp.float32),
-            in_specs=specs,
-            out_specs=pl.BlockSpec(memory_space=pltpu.VMEM),
+            out_shape=[jax.ShapeDtypeStruct(shape, jnp.float32) for shape in shapes],
+            in_specs=[pl.BlockSpec(memory_space=pltpu.VMEM) for _ in args],
+            out_specs=[pl.BlockSpec(memory_space=pltpu.VMEM) for _ in shapes],
+            compiler_params=pltpu.CompilerParams(vmem_limit_bytes=limit),
             name=name,
         )(*args)
 
     return run
 
 
+def exchange(x, axes):
+    return lax.all_to_all(x.reshape(x.shape[0], 1, LONG), axes, 0, 0, tiled=True).reshape(x.shape)
+
+
 def body(contrast, defocus, blurring):
-    par = lax.all_gather(jnp.stack([defocus, blurring], axis=1), "dist", axis=0, tiled=True)
-    sent = call(first_kernel, (NDIST * LONG, LONG), "rows_forward")(contrast[0], ROW_FORWARD, ROW_TW)
-    got = lax.all_to_all(sent.reshape(NDIST * LONG, 1, LONG), ("dist", "pix"), 0, 0, tiled=True)
-    middle = call(middle_kernel, (LONG, LONG), "columns", True)(
-        par, got.reshape(NDIST * LONG, LONG), COL_FORWARD, COL_RIGHT, COL_LEFT, COL_BACK, COL_TW
+    rows = NDIST * LONG
+    (pair,) = call(pair_kernel, ((8, LONG),), "pair")(defocus.reshape(1, 1), blurring.reshape(1, 1))
+    par = lax.all_gather(pair, DIST, axis=0, tiled=True)
+    sent, par = call(first_kernel, ((rows, LONG), par.shape), "rows_forward")(contrast[0], par, ROW_FORWARD, ROW_TW)
+    got = exchange(sent, DIST + PIX)
+    (middle,) = call(middle_kernel, ((2 * LONG, LONG),), "columns")(
+        par, got, COL_FORWARD, COL_RIGHT, COL_LEFT, COL_BACK, COL_TW
     )
-    mine = lax.all_to_all(middle.reshape(LONG, 1, LONG), "pix", 0, 0, tiled=True).reshape(LONG, LONG)
-    whole = lax.all_gather(mine, "dist", axis=0, tiled=True)
-    return call(last_kernel, (2, SHORT, SIZE), "rows_back")(whole, ROW_BACK, ROW_TW)
+    bands = exchange(middle, ("l", "h", "x", "z"))
+    whole = lax.all_gather(bands, "c", axis=0, tiled=True)
+    return call(last_kernel, ((2, SHORT, SIZE),), "rows_back")(whole, ROW_BACK, ROW_TW)[0]
 
 
 def solution(mesh):
+    parts = Mesh(mesh.devices.reshape((2, 2) + PIX_SIZES), DIST + PIX)
     return jax.shard_map(
         body,
-        mesh=mesh,
-        in_specs=(P("dist", None, "pix", None), P("dist"), P("dist")),
-        out_specs=P(None, "pix", None),
+        mesh=parts,
+        in_specs=(P(DIST, None, PIX, None), P(DIST), P(DIST)),
+        out_specs=P(None, PIX, None),
         check_vma=False,
     )

time: 77.7 us -> 76.4 us (0.983)
  blocking collectives: 39.2 us -> 68.9 us
  starting transfers between devices: 22.2 us -> 0 us
  waiting for transfers between devices: 5.56 us -> 0 us
  Pallas kernels: 8.38 us -> 3.91 us
  local copies, waits for them, and re-layouts: 0.7 us -> 1.9 us
    all_to_all x1 -> x2, blocking collectives: 22 us -> 53.6 us  [exchange(): lax.all_to_all(x.reshape(x.shape[0], 1, LONG), axes, 0, 0, tiled=True)]
    all_to_all x1 -> x0, starting transfers between devices: 22.2 us -> none  [body(): lax.all_to_all(sent.reshape(NDIST * LONG, 1, LONG), ('dist', 'pix'), 0, 0...]
    all_to_all x1 -> x0, waiting for transfers between devices: 5.56 us -> none  [body(): lax.all_to_all(sent.reshape(NDIST * LONG, 1, LONG), ('dist', 'pix'), 0, 0...]
    pallas_call x3 -> x4, Pallas kernels: 8.38 us -> 3.91 us  [run(): pl.pallas_call(kernel, out_shape=[jax.ShapeDtypeStruct(shape, jnp.float32...]
    all_gather x2, blocking collectives: 17.2 us -> 15.3 us  [the longest x1 11.9 us: body(): par = lax.all_gather(pair, DIST, axis=0, tiled=True)]
    unnamed x2 -> x18, local copies, waits for them, and re-layouts: 0.7 us -> 1.9 us
  transfers between devices with their start and end apart: 1 -> 0, of which waited for: 1 -> 0; matrix products, arithmetic and copies ran while one was open for 0% -> 0% of each run, Pallas kernels for 0% -> 0%
where the time goes in v3:
time: 76.4 us; the launch traced here: 76.1 us
  blocking collectives  68.9 us (90%)
  Pallas kernels  3.91 us (5%)
  local copies, waits for them, and re-layouts  1.9 us (2%)
  between operations  1.39 us (2%)
    all_to_all x2, blocking collectives, exchange(): lax.all_to_all(x.reshape(x.shape[0], 1, LONG), axes, 0, 0, tiled=True)  53.6 us
    all_gather x1, blocking collectives, body(): par = lax.all_gather(pair, DIST, axis=0, tiled=True)  11.9 us
    pallas_call x4, Pallas kernels, run(): pl.pallas_call(kernel, out_shape=[jax.ShapeDtypeStruct(shape, jnp.float32...  3.91 us
    all_gather x1, blocking collectives, body(): whole = lax.all_gather(bands, 'c', axis=0, tiled=True)  3.45 us
    unnamed x18, local copies, waits for them, and re-layouts  1.9 us

profile of v3, /device:TPU:1, one launch (start us, length us, event | category | flops | bytes accessed | tf_op | source)
XLA Modules:
  0.0 76.1 jit_solution(16602536618702961674)
XLA Ops:
  0.7 0.0 copy-start.8
  1.3 0.1 pair.1
  1.4 11.9 %all_gather.6.par = f32[32,128]{1,0:T(8,128)S(1)} all-gather(f32[8,128]{1,0:T(8,128)S(1)} %pair.1), channel_id=1, replica_groups=mesh['l'=2,'c'=2,'z'=8,'x'=4,'h'=4] {'l','c'}, dimensions={0}, use_global_device_ids=true | all-gather | bytes 20480 | tf_op jit(solution)/shard_map/all_gather | solution.py:250
  13.3 0.0 copy-done.8
  13.3 0.0 copy-start
  13.3 0.9 %copy-done = f32[1,2,16,2048]{3,2,1,0:T(8,128)S(1)} copy-done((f32[1,2,16,2048]{3,2,1,0:T(8,128)S(1)}, f32[1,2,16,2048]{3,2,1,0:T(8,128)}, u32[]{:S(2)}) %copy-start) | copy-done | bytes 262168
  14.2 0.0 copy-start.1
  14.2 0.9 %copy-done.1 = f32[128,256]{1,0:T(8,128)S(1)} copy-done((f32[128,256]{1,0:T(8,128)S(1)}, f32[128,256]{1,0:T(8,128)}, u32[]{:S(2)}) %copy-start.1) | copy-done | bytes 131096
  15.1 0.0 copy-start.7
  15.1 0.6 rows_forward.1
  15.8 0.0 copy-start.3
  15.8 0.0 copy-start.4
  15.8 0.0 copy-start.5
  15.8 0.0 copy-start.6
  15.8 31.9 %all_to_all.10 = f32[512,1,128]{2,1,0:T(1,128)S(1)} all-to-all(f32[512,1,128]{2,1,0:T(1,128)S(1)} %bitcast.17), channel_id=1, replica_groups=mesh['l'=2,'c'=2,'z'=8,'x'=4,'h'=4] {'l','c','z','x','h'}, dimensions={0} | all-to-all | bytes 524288 | tf_op jit(solution)/shard_map/all_to_all | solution.py:244
  47.7 0.0 copy-done.7
  47.7 0.0 copy-done.3
  47.7 0.0 copy-done.4
  47.7 0.0 copy-done.5
  47.8 0.0 copy-done.6
  47.8 1.8 %columns.1 = f32[256,128]{1,0:T(8,128)S(1)} custom-call(f32[32,128]{1,0:T(8,128)S(1)} %get-tuple-element.7.par, f32[512,128]{1,0:T(8,128)S(1)} %bitcast.14, f32[256,128]{1,0:T(8,128)S(1)} %copy-done.7, f32[256,128]{1,0:T(8,128)S(1)} %copy-done.6, f32[128,256]{1,0:T(8,128)S(1)} %copy-done.5, f32[128,256]{1,0:T(8,128)S(1)} %copy-done.4, ...), custom_call_target="tpu_custom_call" | custom-call | tf_op jit(solution)/shard_map/columns/pallas_call | solution.py:231
  49.6 21.7 %all_to_all.11 = f32[256,1,128]{2,1,0:T(1,128)S(1)} all-to-all(f32[256,1,128]{2,1,0:T(1,128)S(1)} %bitcast.16), channel_id=1, replica_groups=mesh['l'=2,'c'=2,'z'=8,'x'=4,'h'=4] {'l','h','x','z'}, dimensions={0} | all-to-all | bytes 262144 | tf_op jit(solution)/shard_map/all_to_all | solution.py:244
  71.3 0.0 copy-start.2
  71.3 3.4 %all-gather = f32[512,1,128]{2,0,1:T(8,128)S(1)} all-gather(f32[256,1,128]{2,0,1:T(8,128)S(1)} %bitcast.19), channel_id=2, replica_groups=mesh['l'=2,'c'=2,'z'=8,'x'=4,'h'=4] {'c'}, dimensions={0}, use_global_device_ids=true | all-gather | bytes 393216 | tf_op jit(solution)/shard_map/all_gather | solution.py:257
  74.7 0.0 copy-done.2
  74.7 1.4 %rows_back.1 = f32[2,16,2048]{2,1,0:T(8,128)} custom-call(f32[512,128]{1,0:T(8,128)S(1)} %bitcast.15, f32[256,128]{1,0:T(8,128)S(1)} %copy-done.2, f32[2,16,128]{2,1,0:T(8,128)S(1)} %copy-done.8), custom_call_target="tpu_custom_call" | custom-call | tf_op jit(solution)/shard_map/rows_back/pallas_call | solution.py:231
Async XLA Ops:
  0.7 12.6 %copy-start.8 = (f32[2,16,128]{2,1,0:T(8,128)S(1)}, f32[2,16,128]{2,1,0:T(8,128)}, u32[]{:S(2)}) copy-start(f32[2,16,128]{2,1,0:T(8,128)} %constant.17.clone.twist) | copy-start | bytes 49156
  13.3 1.0 %copy-start = (f32[1,2,16,2048]{3,2,1,0:T(8,128)S(1)}, f32[1,2,16,2048]{3,2,1,0:T(8,128)}, u32[]{:S(2)}) copy-start(f32[1,2,16,2048]{3,2,1,0:T(8,128)} %param.11) | copy-start | bytes 786436
  14.2 0.9 %copy-start.1 = (f32[128,256]{1,0:T(8,128)S(1)}, f32[128,256]{1,0:T(8,128)}, u32[]{:S(2)}) copy-start(f32[128,256]{1,0:T(8,128)} %constant.16.clone.table) | copy-start | bytes 393220
  15.1 32.6 %copy-start.7 = (f32[256,128]{1,0:T(8,128)S(1)}, f32[256,128]{1,0:T(8,128)}, u32[]{:S(2)}) copy-start(f32[256,128]{1,0:T(8,128)} %constant.18.clone.forward) | copy-start | bytes 393220
  15.8 32.0 %copy-start.3 = (f32[2,128,128]{2,1,0:T(8,128)S(1)}, f32[2,128,128]{2,1,0:T(8,128)}, u32[]{:S(2)}) copy-start(f32[2,128,128]{2,1,0:T(8,128)} %constant.22.clone.twist) | copy-start | bytes 393220
  15.8 32.0 %copy-start.4 = (f32[128,256]{1,0:T(8,128)S(1)}, f32[128,256]{1,0:T(8,128)}, u32[]{:S(2)}) copy-start(f32[128,256]{1,0:T(8,128)} %constant.21.clone.back) | copy-start | bytes 393220
  15.8 32.0 %copy-start.5 = (f32[128,256]{1,0:T(8,128)S(1)}, f32[128,256]{1,0:T(8,128)}, u32[]{:S(2)}) copy-start(f32[128,256]{1,0:T(8,128)} %constant.20.clone.left) | copy-start | bytes 393220
  15.8 32.0 %copy-start.6 = (f32[256,128]{1,0:T(8,128)S(1)}, f32[256,128]{1,0:T(8,128)}, u32[]{:S(2)}) copy-start(f32[256,128]{1,0:T(8,128)} %constant.19.clone.right) | copy-start | bytes 393220
  71.3 3.5 %copy-start.2 = (f32[256,128]{1,0:T(8,128)S(1)}, f32[256,128]{1,0:T(8,128)}, u32[]{:S(2)}) copy-start(f32[256,128]{1,0:T(8,128)} %constant.23.clone.table) | copy-start | bytes 393220

commit v4 on v3

--- a/solution.py
+++ b/solution.py
@@ -198,21 +198,14 @@
     return sixteen_point(z, -1)
 
 
-def pair_kernel(defocus, blurring, out):
-    lane = lax.broadcasted_iota(jnp.int32, out.shape, 1)
-    out[...] = jnp.where(lane < LONG // 2, defocus[...], blurring[...])
-
-
-def first_kernel(images, par, table, twist, out, par_out):
+def first_kernel(images, table, twist, out):
     out[...] = row_forward(images[...], table[...], twist[...])
-    par_out[...] = par[...]
 
 
 def middle_kernel(par, x, forward, right, left, back, twist, out):
     first_col = SHORT * lax.axis_index(PIX) + WIDE * lax.axis_index(DIST)
-    half = LONG // 2
-    defocus = [par[8 * d : 8 * d + 1, :1] for d in range(NDIST)]
-    blurring = [par[8 * d : 8 * d + 1, half : half + 1] for d in range(NDIST)]
+    defocus = [par[d : d + 1, :1] for d in range(NDIST)]
+    blurring = [par[d : d + 1, 1:] for d in range(NDIST)]
     table = gains(defocus, blurring, first_col)
     blocks = [x[LONG * d : LONG * (d + 1), :] for d in range(NDIST)]
     y = column_middle(blocks, table, forward[...], right[...], left[...], back[...], twist[...])
@@ -246,9 +239,8 @@
 
 def body(contrast, defocus, blurring):
     rows = NDIST * LONG
-    (pair,) = call(pair_kernel, ((8, LONG),), "pair")(defocus.reshape(1, 1), blurring.reshape(1, 1))
-    par = lax.all_gather(pair, DIST, axis=0, tiled=True)
-    sent, par = call(first_kernel, ((rows, LONG), par.shape), "rows_forward")(contrast[0], par, ROW_FORWARD, ROW_TW)
+    (sent,) = call(first_kernel, ((rows, LONG),), "rows_forward", None)(contrast[0], ROW_FORWARD, ROW_TW)
+    par = lax.all_gather(jnp.stack([defocus, blurring], axis=1), DIST, axis=0, tiled=True)
     got = exchange(sent, DIST + PIX)
     (middle,) = call(middle_kernel, ((2 * LONG, LONG),), "columns")(
         par, got, COL_FORWARD, COL_RIGHT, COL_LEFT, COL_BACK, COL_TW

time: 76.4 us -> 70.8 us (0.927)
  blocking collectives: 68.9 us -> 35.4 us
  starting transfers between devices: 0 us -> 22.2 us
  waiting for transfers between devices: 0 us -> 6 us
  local copies, waits for them, and re-layouts: 1.9 us -> 0.03 us
  Pallas kernels: 3.91 us -> 5.59 us
    all_to_all x2 -> x1, blocking collectives: 53.6 us -> 22.9 us  [exchange(): lax.all_to_all(x.reshape(x.shape[0], 1, LONG), axes, 0, 0, tiled=True)]
    all_to_all x0 -> x1, starting transfers between devices: none -> 22.2 us  [exchange(): lax.all_to_all(x.reshape(x.shape[0], 1, LONG), axes, 0, 0, tiled=True)]
    all_to_all x0 -> x1, waiting for transfers between devices: none -> 6 us  [exchange(): lax.all_to_all(x.reshape(x.shape[0], 1, LONG), axes, 0, 0, tiled=True)]
    all_gather x1, blocking collectives: 11.9 us -> 9.18 us  [body(): lax.all_gather(jnp.stack([defocus, blurring], axis=1), DIST, axis=0, tile...]
    unnamed x18 -> x14, local copies, waits for them, and re-layouts: 1.9 us -> 0.03 us
    pallas_call x4 -> x3, Pallas kernels: 3.91 us -> 5.59 us  [run(): pl.pallas_call(kernel, out_shape=[jax.ShapeDtypeStruct(shape, jnp.float32...]
  transfers between devices with their start and end apart: 0 -> 1, of which waited for: 0 -> 1; matrix products, arithmetic and copies ran while one was open for 0% -> 0% of each run, Pallas kernels for 0% -> 0%
where the time goes in v4:
time: 70.8 us; the launch traced here: 70.5 us
  blocking collectives  35.4 us (50%)
  starting transfers between devices  22.2 us (31%)
  waiting for transfers between devices  6 us (8%)
  Pallas kernels  5.59 us (8%)
  between operations  1.34 us (2%)
    all_to_all x1, blocking collectives, exchange(): lax.all_to_all(x.reshape(x.shape[0], 1, LONG), axes, 0, 0, tiled=True)  22.9 us
    all_to_all x1, starting transfers between devices, exchange(): lax.all_to_all(x.reshape(x.shape[0], 1, LONG), axes, 0, 0, tiled=True)  22.2 us
    all_gather x1, blocking collectives, body(): lax.all_gather(jnp.stack([defocus, blurring], axis=1), DIST, axis=0, tile...  9.18 us
    all_to_all x1, waiting for transfers between devices, exchange(): lax.all_to_all(x.reshape(x.shape[0], 1, LONG), axes, 0, 0, tiled=True)  6 us
    pallas_call x3, Pallas kernels, run(): pl.pallas_call(kernel, out_shape=[jax.ShapeDtypeStruct(shape, jnp.float32...  5.59 us
    all_gather x1, blocking collectives, body(): whole = lax.all_gather(bands, 'c', axis=0, tiled=True)  3.29 us
  transfers between devices with their start and end apart: 1, of which 1 were waited for; matrix products, arithmetic and copies ran while one was open for 0% of the time, Pallas kernels for 0%

profile of v4, /device:TPU:1, one launch (start us, length us, event | category | flops | bytes accessed | tf_op | source)
XLA Modules:
  0.0 70.5 jit_solution(7860075749738804984)
XLA Ops:
  0.0 0.0 copy-start.5
  0.0 2.4 %rows_forward.1 = f32[512,128]{1,0:T(8,128)} custom-call(f32[2,16,2048]{2,1,0:T(8,128)} %bitcast.23, f32[128,256]{1,0:T(8,128)} %constant.16.clone.table, f32[2,16,128]{2,1,0:T(8,128)} %constant.17.clone.twist), custom_call_target="tpu_custom_call" | custom-call | tf_op jit(solution)/shard_map/rows_forward/pallas_call | solution.py:224
  2.4 0.0 copy-start.1
  2.4 0.0 copy-start.2
  2.4 0.0 copy-start.3
  2.4 0.0 copy-start.4
  2.4 22.2 %all-to-all-start = ((f32[512,1,128]{2,1,0:T(1,128)}), f32[512,1,128]{2,1,0:T(1,128)S(1)}, u32[]{:S(2)}, u32[]{:S(2)}) async-start(f32[512,1,128]{2,1,0:T(1,128)} %bitcast.21), calls=%async_computation | async-start | bytes 524288 | tf_op jit(solution)/shard_map/all_to_all | solution.py:237
  25.9 0.1 maximum_bitcast_fusion
  25.9 9.2 %all-gather.1 = f32[4,1,2]{2,1,0:T(1,128)S(1)} all-gather(f32[1,1,2]{2,1,0:T(1,128)S(1)} %maximum_bitcast_fusion), channel_id=1, replica_groups=mesh['l'=2,'c'=2,'z'=8,'x'=4,'h'=4] {'l','c'}, dimensions={0}, use_global_device_ids=true | all-gather | bytes 40 | tf_op jit(solution)/shard_map/all_gather | solution.py:243
  35.1 6.0 %all-to-all-done = f32[512,1,128]{2,1,0:T(1,128)S(1)} async-done(((f32[512,1,128]{2,1,0:T(1,128)}), f32[512,1,128]{2,1,0:T(1,128)S(1)}, u32[]{:S(2)}, u32[]{:S(2)}) %all-to-all-start) | async-done | bytes 262176 | tf_op jit(solution)/shard_map/all_to_all | solution.py:237
  41.1 0.0 copy-done.5
  41.1 0.0 copy-done.1
  41.1 0.0 copy-done.2
  41.1 0.0 copy-done.3
  41.1 0.0 copy-done.4
  41.2 1.8 %columns.1 = f32[256,128]{1,0:T(8,128)S(1)} custom-call(f32[4,2]{1,0:T(4,128)S(1)} %bitcast.20, f32[512,128]{1,0:T(8,128)S(1)} %bitcast.17, f32[256,128]{1,0:T(8,128)S(1)} %copy-done.1, f32[256,128]{1,0:T(8,128)S(1)} %copy-done.2, f32[128,256]{1,0:T(8,128)S(1)} %copy-done.3, f32[128,256]{1,0:T(8,128)S(1)} %copy-done.4, f32[2,128,128]{2,1,0:T(8,128)S(1)} %copy-done.5), custom_call_target="tpu_custom_call" | custom-call | tf_op jit(solution)/shard_map/columns/pallas_call | solution.py:224
  43.0 22.9 %all_to_all.10 = f32[256,1,128]{2,1,0:T(1,128)S(1)} all-to-all(f32[256,1,128]{2,1,0:T(1,128)S(1)} %bitcast.19), channel_id=1, replica_groups=mesh['l'=2,'c'=2,'z'=8,'x'=4,'h'=4] {'l','h','x','z'}, dimensions={0} | all-to-all | bytes 262144 | tf_op jit(solution)/shard_map/all_to_all | solution.py:237
  65.9 0.0 copy-start
  65.9 0.0 copy-start.6
  65.9 3.3 %all-gather = f32[512,1,128]{2,0,1:T(8,128)S(1)} all-gather(f32[256,1,128]{2,0,1:T(8,128)S(1)} %bitcast.22), channel_id=2, replica_groups=mesh['l'=2,'c'=2,'z'=8,'x'=4,'h'=4] {'c'}, dimensions={0}, use_global_device_ids=true | all-gather | bytes 393216 | tf_op jit(solution)/shard_map/all_gather | solution.py:249
  69.2 0.0 copy-done
  69.2 0.0 copy-done.6
  69.2 1.4 %rows_back.1 = f32[2,16,2048]{2,1,0:T(8,128)} custom-call(f32[512,128]{1,0:T(8,128)S(1)} %bitcast.18, f32[256,128]{1,0:T(8,128)S(1)} %copy-done, f32[2,16,128]{2,1,0:T(8,128)S(1)} %copy-done.6), custom_call_target="tpu_custom_call" | custom-call | tf_op jit(solution)/shard_map/rows_back/pallas_call | solution.py:224
Async XLA Ops:
  0.0 41.1 %copy-start.5 = (f32[2,128,128]{2,1,0:T(8,128)S(1)}, f32[2,128,128]{2,1,0:T(8,128)}, u32[]{:S(2)}) copy-start(f32[2,128,128]{2,1,0:T(8,128)} %constant.22.clone.twist) | copy-start | bytes 393220
  2.4 38.7 %copy-start.1 = (f32[256,128]{1,0:T(8,128)S(1)}, f32[256,128]{1,0:T(8,128)}, u32[]{:S(2)}) copy-start(f32[256,128]{1,0:T(8,128)} %constant.18.clone.forward) | copy-start | bytes 393220
  2.4 38.7 %copy-start.2 = (f32[256,128]{1,0:T(8,128)S(1)}, f32[256,128]{1,0:T(8,128)}, u32[]{:S(2)}) copy-start(f32[256,128]{1,0:T(8,128)} %constant.19.clone.right) | copy-start | bytes 393220
  2.4 38.7 %copy-start.3 = (f32[128,256]{1,0:T(8,128)S(1)}, f32[128,256]{1,0:T(8,128)}, u32[]{:S(2)}) copy-start(f32[128,256]{1,0:T(8,128)} %constant.20.clone.left) | copy-start | bytes 393220
  2.4 38.7 %copy-start.4 = (f32[128,256]{1,0:T(8,128)S(1)}, f32[128,256]{1,0:T(8,128)}, u32[]{:S(2)}) copy-start(f32[128,256]{1,0:T(8,128)} %constant.21.clone.back) | copy-start | bytes 393220
  2.4 38.7 %all-to-all-start = ((f32[512,1,128]{2,1,0:T(1,128)}), f32[512,1,128]{2,1,0:T(1,128)S(1)}, u32[]{:S(2)}, u32[]{:S(2)}) async-start(f32[512,1,128]{2,1,0:T(1,128)} %bitcast.21), calls=%async_computation | async-start | bytes 524288 | tf_op jit(solution)/shard_map/all_to_all | solution.py:237
  65.9 3.3 %copy-start = (f32[256,128]{1,0:T(8,128)S(1)}, f32[256,128]{1,0:T(8,128)}, u32[]{:S(2)}) copy-start(f32[256,128]{1,0:T(8,128)} %constant.23.clone.table) | copy-start | bytes 393220
  65.9 3.3 %copy-start.6 = (f32[2,16,128]{2,1,0:T(8,128)S(1)}, f32[2,16,128]{2,1,0:T(8,128)}, u32[]{:S(2)}) copy-start(f32[2,16,128]{2,1,0:T(8,128)} %constant.17.clone.twist) | copy-start | bytes 49156

commit v5 on v4

--- a/solution.py
+++ b/solution.py
@@ -57,24 +57,37 @@
     return np.asarray(x, np.float32)
 
 
-ROW_FORWARD = f32(np.concatenate([COS, SIN], axis=1))
-COL_FORWARD = f32(np.concatenate([COS, SIN], axis=0))
-COL_RIGHT = f32(np.concatenate([RIGHT, turn_lanes(RIGHT)], axis=0))
-COL_LEFT = f32(np.concatenate([BACK, turn_after(BACK)], axis=1))
-COL_BACK = f32(np.concatenate([COS, -SIN], axis=1)[BACK_ORDER])
-ROW_BACK = f32(np.concatenate([COS[BACK_ORDER], -SIN[BACK_ORDER]], axis=0))
+def split_table(x):
+    high = np.asarray(x, jnp.bfloat16)
+    return np.stack([high, np.asarray(x - high.astype(np.float64), jnp.bfloat16)])
+
+
+ROW_FORWARD = split_table(np.concatenate([COS, SIN], axis=1))
+COL_FORWARD = split_table(np.concatenate([COS, SIN], axis=0))
+COL_RIGHT = split_table(np.concatenate([RIGHT, turn_lanes(RIGHT)], axis=0))
+COL_LEFT = split_table(np.concatenate([BACK, turn_after(BACK)], axis=1))
+COL_BACK = split_table(np.concatenate([COS, -SIN], axis=1)[BACK_ORDER])
+ROW_BACK = split_table(np.concatenate([COS[BACK_ORDER], -SIN[BACK_ORDER]], axis=0))
 ROW_TW = f32(np.stack(ROW_TWIST))
 COL_TW = f32(np.stack(COL_TWIST))
 
 
+def halves(x):
+    high = x.astype(jnp.bfloat16)
+    return high, (x - high.astype(jnp.float32)).astype(jnp.bfloat16)
+
+
+def joined(parts, axis):
+    return tuple(jnp.concatenate([p[i] for p in parts], axis=axis) for i in range(2))
+
+
 def product(a, b, a_dim=1, b_dim=0):
-    return lax.dot_general(
-        a,
-        b,
-        (((a_dim,), (b_dim,)), ((), ())),
-        precision=lax.Precision.HIGHEST,
-        preferred_element_type=jnp.float32,
-    )
+    def one(x, y):
+        return lax.dot_general(
+            x, y, (((a_dim,), (b_dim,)), ((), ())), preferred_element_type=jnp.float32
+        )
+
+    return one(a[0], b[0]) + (one(a[0], b[1]) + one(a[1], b[0]))
 
 
 def four_point(z, sign):
@@ -118,9 +131,9 @@
     for d in range(NDIST):
         part = turned[WIDE * d : WIDE * (d + 1)]
         re, im = [r for r, _ in part], [i for _, i in part]
-        left = jnp.concatenate(re + im, axis=0)
-        right = jnp.concatenate(im + [-r for r in re], axis=0)
-        both = jnp.concatenate([left, right], axis=1)
+        re, im = halves(jnp.concatenate(re, axis=0)), halves(jnp.concatenate(im, axis=0))
+        minus = tuple(-r for r in re)
+        both = joined([joined([re, im], 0), joined([im, minus], 0)], 1)
         out.append(product(table, both, 1, 1))
     return jnp.concatenate(out, axis=0)
 
@@ -164,19 +177,19 @@
     c, s = twist[0], twist[1]
     parts = []
     for x in blocks:
-        both = product(forward, x)
+        both = product(forward, halves(x))
         u, v = both[:LONG], both[LONG:]
-        parts.append(jnp.concatenate([u * c - v * s, v * c + u * s], axis=1))
-    spectra = product(jnp.concatenate(parts, axis=0), right)
+        parts.append(joined([halves(u * c - v * s), halves(v * c + u * s)], 1))
+    spectra = product(joined(parts, 0), right)
     numerator = gain[0] * spectra[:LONG]
     weight = gain[0] * gain[0]
     for d in range(1, NDIST):
         numerator = numerator + gain[d] * spectra[LONG * d : LONG * (d + 1)]
         weight = weight + gain[d] * gain[d]
     quotient = numerator / (2.0 * (weight + REGULARIZER))
-    both = product(quotient, left)
+    both = product(halves(quotient), left)
     a, b = both[:, :LONG], both[:, LONG:]
-    upright = jnp.concatenate([a * c - b * s, b * c + a * s], axis=0)
+    upright = joined([halves(a * c - b * s), halves(b * c + a * s)], 0)
     return product(back, upright)
 
 
@@ -185,10 +198,10 @@
     scale = 1.0 / (SIZE * SIZE)
     for d in range(NDIST):
         start = LONG * (2 * (d % 2) + d // 2)
-        t = x[start : start + LONG].T
         half = LONG // 2
-        turned = jnp.concatenate([t[half:], -t[:half]], axis=0)
-        o = product(jnp.concatenate([t, turned], axis=1), table)
+        t = halves(x[start : start + LONG].T)
+        turned = joined([tuple(p[half:] for p in t), tuple(-p[:half] for p in t)], 0)
+        o = product(joined([t, turned], 1), table)
         for j in range(WIDE):
             r = o[SHORT * j : SHORT * (j + 1)]
             i = o[half + SHORT * j : half + SHORT * (j + 1)]

time: 70.8 us -> 69.7 us (0.984)
  Pallas kernels: 5.59 us -> 4.49 us
    pallas_call x3, Pallas kernels: 5.59 us -> 4.49 us  [run(): pl.pallas_call(kernel, out_shape=[jax.ShapeDtypeStruct(shape, jnp.float32...]
where the time goes in v5:
time: 69.7 us; the launch traced here: 69.4 us
  blocking collectives  35.4 us (51%)
  starting transfers between devices  22.1 us (32%)
  waiting for transfers between devices  6 us (9%)
  Pallas kernels  4.49 us (6%)
  between operations  1.34 us (2%)
    all_to_all x1, blocking collectives, exchange(): lax.all_to_all(x.reshape(x.shape[0], 1, LONG), axes, 0, 0, tiled=True)  22.9 us
    all_to_all x1, starting transfers between devices, exchange(): lax.all_to_all(x.reshape(x.shape[0], 1, LONG), axes, 0, 0, tiled=True)  22.1 us
    all_gather x1, blocking collectives, body(): lax.all_gather(jnp.stack([defocus, blurring], axis=1), DIST, axis=0, tile...  9.18 us
    all_to_all x1, waiting for transfers between devices, exchange(): lax.all_to_all(x.reshape(x.shape[0], 1, LONG), axes, 0, 0, tiled=True)  6 us
    pallas_call x3, Pallas kernels, run(): pl.pallas_call(kernel, out_shape=[jax.ShapeDtypeStruct(shape, jnp.float32...  4.49 us
    all_gather x1, blocking collectives, body(): whole = lax.all_gather(bands, 'c', axis=0, tiled=True)  3.28 us
  transfers between devices with their start and end apart: 1, of which 1 were waited for; matrix products, arithmetic and copies ran while one was open for 0% of the time, Pallas kernels for 0%

profile of v5, /device:TPU:1, one launch (start us, length us, event | category | flops | bytes accessed | tf_op | source)
XLA Modules:
  0.0 69.4 jit_solution(6244876534487710042)
XLA Ops:
  0.0 0.0 copy-start.5
  0.0 2.2 %rows_forward.1 = f32[512,128]{1,0:T(8,128)} custom-call(f32[2,16,2048]{2,1,0:T(8,128)} %bitcast.23, bf16[2,128,256]{2,1,0:T(8,128)(2,1)} %constant.16.clone.table, f32[2,16,128]{2,1,0:T(8,128)} %constant.17.clone.twist), custom_call_target="tpu_custom_call" | custom-call | tf_op jit(solution)/shard_map/rows_forward/pallas_call | solution.py:237
  2.2 0.0 copy-start.1
  2.2 0.0 copy-start.2
  2.2 0.0 copy-start.3
  2.2 0.0 copy-start.4
  2.2 22.1 %all-to-all-start = ((f32[512,1,128]{2,1,0:T(1,128)}), f32[512,1,128]{2,1,0:T(1,128)S(1)}, u32[]{:S(2)}, u32[]{:S(2)}) async-start(f32[512,1,128]{2,1,0:T(1,128)} %bitcast.21), calls=%async_computation | async-start | bytes 524288 | tf_op jit(solution)/shard_map/all_to_all | solution.py:250
  25.6 0.1 maximum_bitcast_fusion
  25.7 9.2 %all-gather.1 = f32[4,1,2]{2,1,0:T(1,128)S(1)} all-gather(f32[1,1,2]{2,1,0:T(1,128)S(1)} %maximum_bitcast_fusion), channel_id=1, replica_groups=mesh['l'=2,'c'=2,'z'=8,'x'=4,'h'=4] {'l','c'}, dimensions={0}, use_global_device_ids=true | all-gather | bytes 40 | tf_op jit(solution)/shard_map/all_gather | solution.py:256
  34.9 6.0 %all-to-all-done = f32[512,1,128]{2,1,0:T(1,128)S(1)} async-done(((f32[512,1,128]{2,1,0:T(1,128)}), f32[512,1,128]{2,1,0:T(1,128)S(1)}, u32[]{:S(2)}, u32[]{:S(2)}) %all-to-all-start) | async-done | bytes 262176 | tf_op jit(solution)/shard_map/all_to_all | solution.py:250
  40.9 0.0 copy-done.5
  40.9 0.0 copy-done.1
  40.9 0.0 copy-done.2
  40.9 0.0 copy-done.3
  40.9 0.0 copy-done.4
  40.9 1.1 %columns.1 = f32[256,128]{1,0:T(8,128)S(1)} custom-call(f32[4,2]{1,0:T(4,128)S(1)} %bitcast.20, f32[512,128]{1,0:T(8,128)S(1)} %bitcast.17, bf16[2,256,128]{2,1,0:T(8,128)(2,1)S(1)} %copy-done.1, bf16[2,256,128]{2,1,0:T(8,128)(2,1)S(1)} %copy-done.2, bf16[2,128,256]{2,1,0:T(8,128)(2,1)S(1)} %copy-done.3, bf16[2,128,256]{2,1,0:T(8,128)(2,1)S(1)} %copy-done.4, ...), custom_call_target="tpu_custom_call" | custom-call | tf_op jit(solution)/shard_map/columns/pallas_call | solution.py:237
  42.1 22.9 %all_to_all.10 = f32[256,1,128]{2,1,0:T(1,128)S(1)} all-to-all(f32[256,1,128]{2,1,0:T(1,128)S(1)} %bitcast.19), channel_id=1, replica_groups=mesh['l'=2,'c'=2,'z'=8,'x'=4,'h'=4] {'l','h','x','z'}, dimensions={0} | all-to-all | bytes 262144 | tf_op jit(solution)/shard_map/all_to_all | solution.py:250
  65.0 0.0 copy-start
  65.0 0.0 copy-start.6
  65.0 3.3 %all-gather = f32[512,1,128]{2,0,1:T(8,128)S(1)} all-gather(f32[256,1,128]{2,0,1:T(8,128)S(1)} %bitcast.22), channel_id=2, replica_groups=mesh['l'=2,'c'=2,'z'=8,'x'=4,'h'=4] {'c'}, dimensions={0}, use_global_device_ids=true | all-gather | bytes 393216 | tf_op jit(solution)/shard_map/all_gather | solution.py:262
  68.3 0.0 copy-done
  68.3 0.0 copy-done.6
  68.3 1.2 %rows_back.1 = f32[2,16,2048]{2,1,0:T(8,128)} custom-call(f32[512,128]{1,0:T(8,128)S(1)} %bitcast.18, bf16[2,256,128]{2,1,0:T(8,128)(2,1)S(1)} %copy-done, f32[2,16,128]{2,1,0:T(8,128)S(1)} %copy-done.6), custom_call_target="tpu_custom_call" | custom-call | tf_op jit(solution)/shard_map/rows_back/pallas_call | solution.py:237
Async XLA Ops:
  0.0 40.9 %copy-start.5 = (f32[2,128,128]{2,1,0:T(8,128)S(1)}, f32[2,128,128]{2,1,0:T(8,128)}, u32[]{:S(2)}) copy-start(f32[2,128,128]{2,1,0:T(8,128)} %constant.22.clone.twist) | copy-start | bytes 393220
  2.2 38.7 %copy-start.1 = (bf16[2,256,128]{2,1,0:T(8,128)(2,1)S(1)}, bf16[2,256,128]{2,1,0:T(8,128)(2,1)}, u32[]{:S(2)}) copy-start(bf16[2,256,128]{2,1,0:T(8,128)(2,1)} %constant.18.clone.forward) | copy-start | bytes 393220
  2.2 38.7 %copy-start.2 = (bf16[2,256,128]{2,1,0:T(8,128)(2,1)S(1)}, bf16[2,256,128]{2,1,0:T(8,128)(2,1)}, u32[]{:S(2)}) copy-start(bf16[2,256,128]{2,1,0:T(8,128)(2,1)} %constant.19.clone.right) | copy-start | bytes 393220
  2.2 38.7 %copy-start.3 = (bf16[2,128,256]{2,1,0:T(8,128)(2,1)S(1)}, bf16[2,128,256]{2,1,0:T(8,128)(2,1)}, u32[]{:S(2)}) copy-start(bf16[2,128,256]{2,1,0:T(8,128)(2,1)} %constant.20.clone.left) | copy-start | bytes 393220
  2.2 38.7 %copy-start.4 = (bf16[2,128,256]{2,1,0:T(8,128)(2,1)S(1)}, bf16[2,128,256]{2,1,0:T(8,128)(2,1)}, u32[]{:S(2)}) copy-start(bf16[2,128,256]{2,1,0:T(8,128)(2,1)} %constant.21.clone.back) | copy-start | bytes 393220
  2.2 38.7 %all-to-all-start = ((f32[512,1,128]{2,1,0:T(1,128)}), f32[512,1,128]{2,1,0:T(1,128)S(1)}, u32[]{:S(2)}, u32[]{:S(2)}) async-start(f32[512,1,128]{2,1,0:T(1,128)} %bitcast.21), calls=%async_computation | async-start | bytes 524288 | tf_op jit(solution)/shard_map/all_to_all | solution.py:250
  65.0 3.3 %copy-start = (bf16[2,256,128]{2,1,0:T(8,128)(2,1)S(1)}, bf16[2,256,128]{2,1,0:T(8,128)(2,1)}, u32[]{:S(2)}) copy-start(bf16[2,256,128]{2,1,0:T(8,128)(2,1)} %constant.23.clone.table) | copy-start | bytes 393220
  65.0 3.3 %copy-start.6 = (f32[2,16,128]{2,1,0:T(8,128)S(1)}, f32[2,16,128]{2,1,0:T(8,128)}, u32[]{:S(2)}) copy-start(f32[2,16,128]{2,1,0:T(8,128)} %constant.17.clone.twist) | copy-start | bytes 49156

commit v6 on v5

--- a/solution.py
+++ b/solution.py
@@ -20,7 +20,6 @@
 DIST = ("l", "c")
 PIX = ("z", "x", "h")
 PIX_SIZES = (8, 4, 4)
-BACK_ORDER = np.arange(LONG).reshape(PIX_SIZES).transpose(2, 1, 0).reshape(-1)
 
 
 def angle_tables(left, right, period):
@@ -66,8 +65,8 @@
 COL_FORWARD = split_table(np.concatenate([COS, SIN], axis=0))
 COL_RIGHT = split_table(np.concatenate([RIGHT, turn_lanes(RIGHT)], axis=0))
 COL_LEFT = split_table(np.concatenate([BACK, turn_after(BACK)], axis=1))
-COL_BACK = split_table(np.concatenate([COS, -SIN], axis=1)[BACK_ORDER])
-ROW_BACK = split_table(np.concatenate([COS[BACK_ORDER], -SIN[BACK_ORDER]], axis=0))
+COL_BACK = split_table(np.concatenate([COS, -SIN], axis=1))
+ROW_BACK = split_table(np.concatenate([COS, -SIN], axis=0))
 ROW_TW = f32(np.stack(ROW_TWIST))
 COL_TW = f32(np.stack(COL_TWIST))
 
@@ -258,7 +257,7 @@
     (middle,) = call(middle_kernel, ((2 * LONG, LONG),), "columns")(
         par, got, COL_FORWARD, COL_RIGHT, COL_LEFT, COL_BACK, COL_TW
     )
-    bands = exchange(middle, ("l", "h", "x", "z"))
+    bands = exchange(middle, ("l",) + PIX)
     whole = lax.all_gather(bands, "c", axis=0, tiled=True)
     return call(last_kernel, ((2, SHORT, SIZE),), "rows_back")(whole, ROW_BACK, ROW_TW)[0]
 

time: 69.7 us -> 69.8 us (level)
  no operation moved by 1% of the time
where the time goes in v6:
time: 69.8 us; the launch traced here: 69.5 us
  blocking collectives  35.4 us (51%)
  starting transfers between devices  22.1 us (32%)
  waiting for transfers between devices  6 us (9%)
  Pallas kernels  4.48 us (6%)
  between operations  1.34 us (2%)
    all_to_all x1, blocking collectives, exchange(): lax.all_to_all(x.reshape(x.shape[0], 1, LONG), axes, 0, 0, tiled=True)  22.8 us
    all_to_all x1, starting transfers between devices, exchange(): lax.all_to_all(x.reshape(x.shape[0], 1, LONG), axes, 0, 0, tiled=True)  22.1 us
    all_gather x1, blocking collectives, body(): lax.all_gather(jnp.stack([defocus, blurring], axis=1), DIST, axis=0, tile...  9.18 us
    all_to_all x1, waiting for transfers between devices, exchange(): lax.all_to_all(x.reshape(x.shape[0], 1, LONG), axes, 0, 0, tiled=True)  6 us
    pallas_call x3, Pallas kernels, run(): pl.pallas_call(kernel, out_shape=[jax.ShapeDtypeStruct(shape, jnp.float32...  4.48 us
    all_gather x1, blocking collectives, body(): whole = lax.all_gather(bands, 'c', axis=0, tiled=True)  3.45 us
  transfers between devices with their start and end apart: 1, of which 1 were waited for; matrix products, arithmetic and copies ran while one was open for 0% of the time, Pallas kernels for 0%

profile of v6, /device:TPU:1, one launch (start us, length us, event | category | flops | bytes accessed | tf_op | source)
XLA Modules:
  0.0 69.5 jit_solution(7207058548337037768)
XLA Ops:
  0.0 0.0 copy-start.5
  0.0 2.2 %rows_forward.1 = f32[512,128]{1,0:T(8,128)} custom-call(f32[2,16,2048]{2,1,0:T(8,128)} %bitcast.23, bf16[2,128,256]{2,1,0:T(8,128)(2,1)} %constant.16.clone.table, f32[2,16,128]{2,1,0:T(8,128)} %constant.17.clone.twist), custom_call_target="tpu_custom_call" | custom-call | tf_op jit(solution)/shard_map/rows_forward/pallas_call | solution.py:236
  2.2 0.0 copy-start.1
  2.2 0.0 copy-start.2
  2.2 0.0 copy-start.3
  2.2 0.0 copy-start.4
  2.2 22.1 %all-to-all-start = ((f32[512,1,128]{2,1,0:T(1,128)}), f32[512,1,128]{2,1,0:T(1,128)S(1)}, u32[]{:S(2)}, u32[]{:S(2)}) async-start(f32[512,1,128]{2,1,0:T(1,128)} %bitcast.21), calls=%async_computation | async-start | bytes 524288 | tf_op jit(solution)/shard_map/all_to_all | solution.py:249
  25.6 0.1 maximum_bitcast_fusion
  25.7 9.2 %all-gather.1 = f32[4,1,2]{2,1,0:T(1,128)S(1)} all-gather(f32[1,1,2]{2,1,0:T(1,128)S(1)} %maximum_bitcast_fusion), channel_id=1, replica_groups=mesh['l'=2,'c'=2,'z'=8,'x'=4,'h'=4] {'l','c'}, dimensions={0}, use_global_device_ids=true | all-gather | bytes 40 | tf_op jit(solution)/shard_map/all_gather | solution.py:255
  34.9 6.0 %all-to-all-done = f32[512,1,128]{2,1,0:T(1,128)S(1)} async-done(((f32[512,1,128]{2,1,0:T(1,128)}), f32[512,1,128]{2,1,0:T(1,128)S(1)}, u32[]{:S(2)}, u32[]{:S(2)}) %all-to-all-start) | async-done | bytes 262176 | tf_op jit(solution)/shard_map/all_to_all | solution.py:249
  40.9 0.0 copy-done.5
  40.9 0.0 copy-done.1
  40.9 0.0 copy-done.2
  40.9 0.0 copy-done.3
  40.9 0.0 copy-done.4
  40.9 1.1 %columns.1 = f32[256,128]{1,0:T(8,128)S(1)} custom-call(f32[4,2]{1,0:T(4,128)S(1)} %bitcast.20, f32[512,128]{1,0:T(8,128)S(1)} %bitcast.17, bf16[2,256,128]{2,1,0:T(8,128)(2,1)S(1)} %copy-done.1, bf16[2,256,128]{2,1,0:T(8,128)(2,1)S(1)} %copy-done.2, bf16[2,128,256]{2,1,0:T(8,128)(2,1)S(1)} %copy-done.3, bf16[2,128,256]{2,1,0:T(8,128)(2,1)S(1)} %copy-done.4, ...), custom_call_target="tpu_custom_call" | custom-call | tf_op jit(solution)/shard_map/columns/pallas_call | solution.py:236
  42.1 22.8 %all_to_all.10 = f32[256,1,128]{2,1,0:T(1,128)S(1)} all-to-all(f32[256,1,128]{2,1,0:T(1,128)S(1)} %bitcast.19), channel_id=1, replica_groups=mesh['l'=2,'c'=2,'z'=8,'x'=4,'h'=4] {'l','z','x','h'}, dimensions={0} | all-to-all | bytes 262144 | tf_op jit(solution)/shard_map/all_to_all | solution.py:249
  64.9 0.0 copy-start
  64.9 0.0 copy-start.6
  64.9 3.4 %all-gather = f32[512,1,128]{2,0,1:T(8,128)S(1)} all-gather(f32[256,1,128]{2,0,1:T(8,128)S(1)} %bitcast.22), channel_id=2, replica_groups=mesh['l'=2,'c'=2,'z'=8,'x'=4,'h'=4] {'c'}, dimensions={0}, use_global_device_ids=true | all-gather | bytes 393216 | tf_op jit(solution)/shard_map/all_gather | solution.py:261
  68.3 0.0 copy-done
  68.3 0.0 copy-done.6
  68.3 1.2 %rows_back.1 = f32[2,16,2048]{2,1,0:T(8,128)} custom-call(f32[512,128]{1,0:T(8,128)S(1)} %bitcast.18, bf16[2,256,128]{2,1,0:T(8,128)(2,1)S(1)} %copy-done, f32[2,16,128]{2,1,0:T(8,128)S(1)} %copy-done.6), custom_call_target="tpu_custom_call" | custom-call | tf_op jit(solution)/shard_map/rows_back/pallas_call | solution.py:236
Async XLA Ops:
  0.0 40.9 %copy-start.5 = (f32[2,128,128]{2,1,0:T(8,128)S(1)}, f32[2,128,128]{2,1,0:T(8,128)}, u32[]{:S(2)}) copy-start(f32[2,128,128]{2,1,0:T(8,128)} %constant.22.clone.twist) | copy-start | bytes 393220
  2.2 38.7 %copy-start.1 = (bf16[2,256,128]{2,1,0:T(8,128)(2,1)S(1)}, bf16[2,256,128]{2,1,0:T(8,128)(2,1)}, u32[]{:S(2)}) copy-start(bf16[2,256,128]{2,1,0:T(8,128)(2,1)} %constant.18.clone.forward) | copy-start | bytes 393220
  2.2 38.7 %copy-start.2 = (bf16[2,256,128]{2,1,0:T(8,128)(2,1)S(1)}, bf16[2,256,128]{2,1,0:T(8,128)(2,1)}, u32[]{:S(2)}) copy-start(bf16[2,256,128]{2,1,0:T(8,128)(2,1)} %constant.19.clone.right) | copy-start | bytes 393220
  2.2 38.7 %copy-start.3 = (bf16[2,128,256]{2,1,0:T(8,128)(2,1)S(1)}, bf16[2,128,256]{2,1,0:T(8,128)(2,1)}, u32[]{:S(2)}) copy-start(bf16[2,128,256]{2,1,0:T(8,128)(2,1)} %constant.20.clone.left) | copy-start | bytes 393220
  2.2 38.7 %copy-start.4 = (bf16[2,128,256]{2,1,0:T(8,128)(2,1)S(1)}, bf16[2,128,256]{2,1,0:T(8,128)(2,1)}, u32[]{:S(2)}) copy-start(bf16[2,128,256]{2,1,0:T(8,128)(2,1)} %constant.21.clone.back) | copy-start | bytes 393220
  2.2 38.7 %all-to-all-start = ((f32[512,1,128]{2,1,0:T(1,128)}), f32[512,1,128]{2,1,0:T(1,128)S(1)}, u32[]{:S(2)}, u32[]{:S(2)}) async-start(f32[512,1,128]{2,1,0:T(1,128)} %bitcast.21), calls=%async_computation | async-start | bytes 524288 | tf_op jit(solution)/shard_map/all_to_all | solution.py:249
  64.9 3.5 %copy-start = (bf16[2,256,128]{2,1,0:T(8,128)(2,1)S(1)}, bf16[2,256,128]{2,1,0:T(8,128)(2,1)}, u32[]{:S(2)}) copy-start(bf16[2,256,128]{2,1,0:T(8,128)(2,1)} %constant.23.clone.table) | copy-start | bytes 393220
  64.9 3.5 %copy-start.6 = (f32[2,16,128]{2,1,0:T(8,128)S(1)}, f32[2,16,128]{2,1,0:T(8,128)}, u32[]{:S(2)}) copy-start(f32[2,16,128]{2,1,0:T(8,128)} %constant.17.clone.twist) | copy-start | bytes 49156

commit v7 on v5

--- a/solution.py
+++ b/solution.py
@@ -20,7 +20,21 @@
 DIST = ("l", "c")
 PIX = ("z", "x", "h")
 PIX_SIZES = (8, 4, 4)
-BACK_ORDER = np.arange(LONG).reshape(PIX_SIZES).transpose(2, 1, 0).reshape(-1)
+FLAT = DIST + PIX
+
+
+def far_first():
+    z, x, h = np.unravel_index(np.arange(LONG), PIX_SIZES)
+    hops = np.minimum(z, 8 - z) + np.minimum(x, 4 - x) + 2 * np.minimum(h, 4 - h)
+    hops[0] = 99
+    return np.argsort(-hops, kind="stable")
+
+
+BACK_ORDER = far_first()
+
+
+def back_groups():
+    return [[(2 * low + core) * LONG + int(k) for k in BACK_ORDER for low in range(2)] for core in range(2)]
 
 
 def angle_tables(left, right, period):
@@ -193,13 +207,12 @@
     return product(back, upright)
 
 
-def row_back(x, table, twist):
+def row_back(blocks, table, twist):
     z = []
     scale = 1.0 / (SIZE * SIZE)
     for d in range(NDIST):
-        start = LONG * (2 * (d % 2) + d // 2)
         half = LONG // 2
-        t = halves(x[start : start + LONG].T)
+        t = halves(blocks[d].T)
         turned = joined([tuple(p[half:] for p in t), tuple(-p[:half] for p in t)], 0)
         o = product(joined([t, turned], 1), table)
         for j in range(WIDE):
@@ -222,12 +235,13 @@
     table = gains(defocus, blurring, first_col)
     blocks = [x[LONG * d : LONG * (d + 1), :] for d in range(NDIST)]
     y = column_middle(blocks, table, forward[...], right[...], left[...], back[...], twist[...])
-    out[:LONG, :] = y
-    out[LONG:, :] = y
+    for low in range(2):
+        out[pl.ds(low, LONG, stride=2), :] = y
 
 
 def last_kernel(x, table, twist, out):
-    for j, (r, i) in enumerate(row_back(x[...], table[...], twist[...])):
+    blocks = [x[pl.ds(2 * LONG * (d % 2) + d // 2, LONG, stride=2), :] for d in range(NDIST)]
+    for j, (r, i) in enumerate(row_back(blocks, table[...], twist[...])):
         out[0, :, LONG * j : LONG * (j + 1)] = r
         out[1, :, LONG * j : LONG * (j + 1)] = i
 
@@ -246,25 +260,26 @@
     return run
 
 
-def exchange(x, axes):
-    return lax.all_to_all(x.reshape(x.shape[0], 1, LONG), axes, 0, 0, tiled=True).reshape(x.shape)
+def exchange(x, groups=None):
+    sent = x.reshape(x.shape[0], 1, LONG)
+    return lax.all_to_all(sent, FLAT, 0, 0, axis_index_groups=groups, tiled=True).reshape(x.shape)
 
 
 def body(contrast, defocus, blurring):
     rows = NDIST * LONG
     (sent,) = call(first_kernel, ((rows, LONG),), "rows_forward", None)(contrast[0], ROW_FORWARD, ROW_TW)
     par = lax.all_gather(jnp.stack([defocus, blurring], axis=1), DIST, axis=0, tiled=True)
-    got = exchange(sent, DIST + PIX)
+    got = exchange(sent)
     (middle,) = call(middle_kernel, ((2 * LONG, LONG),), "columns")(
         par, got, COL_FORWARD, COL_RIGHT, COL_LEFT, COL_BACK, COL_TW
     )
-    bands = exchange(middle, ("l", "h", "x", "z"))
+    bands = exchange(middle, back_groups())
     whole = lax.all_gather(bands, "c", axis=0, tiled=True)
     return call(last_kernel, ((2, SHORT, SIZE),), "rows_back")(whole, ROW_BACK, ROW_TW)[0]
 
 
 def solution(mesh):
-    parts = Mesh(mesh.devices.reshape((2, 2) + PIX_SIZES), DIST + PIX)
+    parts = Mesh(mesh.devices.reshape((2, 2) + PIX_SIZES), FLAT)
     return jax.shard_map(
         body,
         mesh=parts,

time: 69.7 us -> 69.3 us (level)
  no operation moved by 1% of the time
where the time goes in v7:
time: 69.3 us; the launch traced here: 69 us
  blocking collectives  35 us (51%)
  starting transfers between devices  22.1 us (32%)
  waiting for transfers between devices  6 us (9%)
  Pallas kernels  4.49 us (6%)
  between operations  1.34 us (2%)
    all_to_all x1, blocking collectives, exchange(): lax.all_to_all(sent, FLAT, 0, 0, axis_index_groups=groups, tiled=True)  22.5 us
    all_to_all x1, starting transfers between devices, exchange(): lax.all_to_all(sent, FLAT, 0, 0, axis_index_groups=groups, tiled=True)  22.1 us
    all_gather x1, blocking collectives, body(): lax.all_gather(jnp.stack([defocus, blurring], axis=1), DIST, axis=0, tile...  9.18 us
    all_to_all x1, waiting for transfers between devices, exchange(): lax.all_to_all(sent, FLAT, 0, 0, axis_index_groups=groups, tiled=True)  6 us
    pallas_call x3, Pallas kernels, run(): pl.pallas_call(kernel, out_shape=[jax.ShapeDtypeStruct(shape, jnp.float32...  4.49 us
    all_gather x1, blocking collectives, body(): whole = lax.all_gather(bands, 'c', axis=0, tiled=True)  3.27 us
  transfers between devices with their start and end apart: 1, of which 1 were waited for; matrix products, arithmetic and copies ran while one was open for 0% of the time, Pallas kernels for 0%

profile of v7, /device:TPU:1, one launch (start us, length us, event | category | flops | bytes accessed | tf_op | source)
XLA Modules:
  0.0 69.0 jit_solution(10583908481166762536)
XLA Ops:
  0.0 0.0 copy-start.5
  0.0 2.2 %rows_forward.1 = f32[512,128]{1,0:T(8,128)} custom-call(f32[2,16,2048]{2,1,0:T(8,128)} %bitcast.23, bf16[2,128,256]{2,1,0:T(8,128)(2,1)} %constant.16.clone.table, f32[2,16,128]{2,1,0:T(8,128)} %constant.17.clone.twist), custom_call_target="tpu_custom_call" | custom-call | tf_op jit(solution)/shard_map/rows_forward/pallas_call | solution.py:251
  2.2 0.0 copy-start.1
  2.2 0.0 copy-start.2
  2.2 0.0 copy-start.3
  2.2 0.0 copy-start.4
  2.2 22.1 %all-to-all-start = ((f32[512,1,128]{2,1,0:T(1,128)}), f32[512,1,128]{2,1,0:T(1,128)S(1)}, u32[]{:S(2)}, u32[]{:S(2)}) async-start(f32[512,1,128]{2,1,0:T(1,128)} %bitcast.21), calls=%async_computation | async-start | bytes 524288 | tf_op jit(solution)/shard_map/all_to_all | solution.py:265
  25.6 0.1 maximum_bitcast_fusion
  25.7 9.2 %all-gather.1 = f32[4,1,2]{2,1,0:T(1,128)S(1)} all-gather(f32[1,1,2]{2,1,0:T(1,128)S(1)} %maximum_bitcast_fusion), channel_id=1, replica_groups=mesh['l'=2,'c'=2,'z'=8,'x'=4,'h'=4] {'l','c'}, dimensions={0}, use_global_device_ids=true | all-gather | bytes 40 | tf_op jit(solution)/shard_map/all_gather | solution.py:271
  34.9 6.0 %all-to-all-done = f32[512,1,128]{2,1,0:T(1,128)S(1)} async-done(((f32[512,1,128]{2,1,0:T(1,128)}), f32[512,1,128]{2,1,0:T(1,128)S(1)}, u32[]{:S(2)}, u32[]{:S(2)}) %all-to-all-start) | async-done | bytes 262176 | tf_op jit(solution)/shard_map/all_to_all | solution.py:265
  40.9 0.0 copy-done.5
  40.9 0.0 copy-done.1
  40.9 0.0 copy-done.2
  40.9 0.0 copy-done.3
  40.9 0.0 copy-done.4
  40.9 1.1 %columns.1 = f32[256,128]{1,0:T(8,128)S(1)} custom-call(f32[4,2]{1,0:T(4,128)S(1)} %bitcast.20, f32[512,128]{1,0:T(8,128)S(1)} %bitcast.17, bf16[2,256,128]{2,1,0:T(8,128)(2,1)S(1)} %copy-done.1, bf16[2,256,128]{2,1,0:T(8,128)(2,1)S(1)} %copy-done.2, bf16[2,128,256]{2,1,0:T(8,128)(2,1)S(1)} %copy-done.3, bf16[2,128,256]{2,1,0:T(8,128)(2,1)S(1)} %copy-done.4, ...), custom_call_target="tpu_custom_call" | custom-call | tf_op jit(solution)/shard_map/columns/pallas_call | solution.py:251
  42.1 22.5 %all_to_all.10 = f32[256,1,128]{2,1,0:T(1,128)S(1)} all-to-all(f32[256,1,128]{2,1,0:T(1,128)S(1)} %bitcast.19), channel_id=1, replica_groups={{0,256,74,330,58,314,70,326,78,334,90,346,42,298,54,310,62,318,66,322,7..., dimensions={0} | all-to-all | bytes 262144 | tf_op jit(solution)/shard_map/all_to_all | solution.py:265
  64.6 0.0 copy-start
  64.6 0.0 copy-start.6
  64.6 3.3 %all-gather = f32[512,1,128]{2,0,1:T(8,128)S(1)} all-gather(f32[256,1,128]{2,0,1:T(8,128)S(1)} %bitcast.22), channel_id=2, replica_groups=mesh['l'=2,'c'=2,'z'=8,'x'=4,'h'=4] {'c'}, dimensions={0}, use_global_device_ids=true | all-gather | bytes 393216 | tf_op jit(solution)/shard_map/all_gather | solution.py:277
  67.9 0.0 copy-done
  67.9 0.0 copy-done.6
  67.9 1.2 %rows_back.1 = f32[2,16,2048]{2,1,0:T(8,128)} custom-call(f32[512,128]{1,0:T(8,128)S(1)} %bitcast.18, bf16[2,256,128]{2,1,0:T(8,128)(2,1)S(1)} %copy-done, f32[2,16,128]{2,1,0:T(8,128)S(1)} %copy-done.6), custom_call_target="tpu_custom_call" | custom-call | tf_op jit(solution)/shard_map/rows_back/pallas_call | solution.py:251
Async XLA Ops:
  0.0 40.9 %copy-start.5 = (f32[2,128,128]{2,1,0:T(8,128)S(1)}, f32[2,128,128]{2,1,0:T(8,128)}, u32[]{:S(2)}) copy-start(f32[2,128,128]{2,1,0:T(8,128)} %constant.22.clone.twist) | copy-start | bytes 393220
  2.2 38.7 %copy-start.1 = (bf16[2,256,128]{2,1,0:T(8,128)(2,1)S(1)}, bf16[2,256,128]{2,1,0:T(8,128)(2,1)}, u32[]{:S(2)}) copy-start(bf16[2,256,128]{2,1,0:T(8,128)(2,1)} %constant.18.clone.forward) | copy-start | bytes 393220
  2.2 38.7 %copy-start.2 = (bf16[2,256,128]{2,1,0:T(8,128)(2,1)S(1)}, bf16[2,256,128]{2,1,0:T(8,128)(2,1)}, u32[]{:S(2)}) copy-start(bf16[2,256,128]{2,1,0:T(8,128)(2,1)} %constant.19.clone.right) | copy-start | bytes 393220
  2.2 38.7 %copy-start.3 = (bf16[2,128,256]{2,1,0:T(8,128)(2,1)S(1)}, bf16[2,128,256]{2,1,0:T(8,128)(2,1)}, u32[]{:S(2)}) copy-start(bf16[2,128,256]{2,1,0:T(8,128)(2,1)} %constant.20.clone.left) | copy-start | bytes 393220
  2.2 38.7 %copy-start.4 = (bf16[2,128,256]{2,1,0:T(8,128)(2,1)S(1)}, bf16[2,128,256]{2,1,0:T(8,128)(2,1)}, u32[]{:S(2)}) copy-start(bf16[2,128,256]{2,1,0:T(8,128)(2,1)} %constant.21.clone.back) | copy-start | bytes 393220
  2.2 38.7 %all-to-all-start = ((f32[512,1,128]{2,1,0:T(1,128)}), f32[512,1,128]{2,1,0:T(1,128)S(1)}, u32[]{:S(2)}, u32[]{:S(2)}) async-start(f32[512,1,128]{2,1,0:T(1,128)} %bitcast.21), calls=%async_computation | async-start | bytes 524288 | tf_op jit(solution)/shard_map/all_to_all | solution.py:265
  64.6 3.3 %copy-start = (bf16[2,256,128]{2,1,0:T(8,128)(2,1)S(1)}, bf16[2,256,128]{2,1,0:T(8,128)(2,1)}, u32[]{:S(2)}) copy-start(bf16[2,256,128]{2,1,0:T(8,128)(2,1)} %constant.23.clone.table) | copy-start | bytes 393220
  64.6 3.3 %copy-start.6 = (f32[2,16,128]{2,1,0:T(8,128)S(1)}, f32[2,16,128]{2,1,0:T(8,128)}, u32[]{:S(2)}) copy-start(f32[2,16,128]{2,1,0:T(8,128)} %constant.17.clone.twist) | copy-start | bytes 49156

commit v8 on v7

--- a/solution.py
+++ b/solution.py
@@ -23,18 +23,26 @@
 FLAT = DIST + PIX
 
 
+FIRST = (7, 2, 2)
+
+
 def far_first():
-    z, x, h = np.unravel_index(np.arange(LONG), PIX_SIZES)
+    place = np.unravel_index(np.arange(LONG), PIX_SIZES)
+    z, x, h = [np.abs(p - f) for p, f in zip(place, FIRST)]
     hops = np.minimum(z, 8 - z) + np.minimum(x, 4 - x) + 2 * np.minimum(h, 4 - h)
-    hops[0] = 99
+    hops[np.ravel_multi_index(FIRST, PIX_SIZES)] = 99
     return np.argsort(-hops, kind="stable")
 
 
-BACK_ORDER = far_first()
+ORDER = far_first()
+
+
+def all_groups():
+    return [[LONG * d + int(k) for d in range(NDIST) for k in ORDER]]
 
 
 def back_groups():
-    return [[(2 * low + core) * LONG + int(k) for k in BACK_ORDER for low in range(2)] for core in range(2)]
+    return [[(2 * low + core) * LONG + int(k) for k in ORDER for low in range(2)] for core in range(2)]
 
 
 def angle_tables(left, right, period):
@@ -76,12 +84,12 @@
     return np.stack([high, np.asarray(x - high.astype(np.float64), jnp.bfloat16)])
 
 
-ROW_FORWARD = split_table(np.concatenate([COS, SIN], axis=1))
-COL_FORWARD = split_table(np.concatenate([COS, SIN], axis=0))
+ROW_FORWARD = split_table(np.concatenate([COS, SIN], axis=1)[ORDER])
+COL_FORWARD = split_table(np.concatenate([COS[:, ORDER], SIN[:, ORDER]], axis=0))
 COL_RIGHT = split_table(np.concatenate([RIGHT, turn_lanes(RIGHT)], axis=0))
 COL_LEFT = split_table(np.concatenate([BACK, turn_after(BACK)], axis=1))
-COL_BACK = split_table(np.concatenate([COS, -SIN], axis=1)[BACK_ORDER])
-ROW_BACK = split_table(np.concatenate([COS[BACK_ORDER], -SIN[BACK_ORDER]], axis=0))
+COL_BACK = split_table(np.concatenate([COS, -SIN], axis=1)[ORDER])
+ROW_BACK = split_table(np.concatenate([COS[ORDER], -SIN[ORDER]], axis=0))
 ROW_TW = f32(np.stack(ROW_TWIST))
 COL_TW = f32(np.stack(COL_TWIST))
 
@@ -260,7 +268,7 @@
     return run
 
 
-def exchange(x, groups=None):
+def exchange(x, groups):
     sent = x.reshape(x.shape[0], 1, LONG)
     return lax.all_to_all(sent, FLAT, 0, 0, axis_index_groups=groups, tiled=True).reshape(x.shape)
 
@@ -269,7 +277,7 @@
     rows = NDIST * LONG
     (sent,) = call(first_kernel, ((rows, LONG),), "rows_forward", None)(contrast[0], ROW_FORWARD, ROW_TW)
     par = lax.all_gather(jnp.stack([defocus, blurring], axis=1), DIST, axis=0, tiled=True)
-    got = exchange(sent)
+    got = exchange(sent, all_groups())
     (middle,) = call(middle_kernel, ((2 * LONG, LONG),), "columns")(
         par, got, COL_FORWARD, COL_RIGHT, COL_LEFT, COL_BACK, COL_TW
     )

time: 69.3 us -> 68.5 us (0.988)
    all_to_all x1, blocking collectives: 22.5 us -> 21.4 us  [exchange(): lax.all_to_all(sent, FLAT, 0, 0, axis_index_groups=groups, tiled=True)]
    all_gather x1, blocking collectives: 3.27 us -> 4.08 us  [body(): whole = lax.all_gather(bands, 'c', axis=0, tiled=True)]
where the time goes in v8:
time: 68.5 us; the launch traced here: 68.2 us
  blocking collectives  34.6 us (51%)
  starting transfers between devices  22.1 us (32%)
  waiting for transfers between devices  5.52 us (8%)
  Pallas kernels  4.49 us (7%)
  between operations  1.34 us (2%)
    all_to_all x1, starting transfers between devices, exchange(): lax.all_to_all(sent, FLAT, 0, 0, axis_index_groups=groups, tiled=True)  22.1 us
    all_to_all x1, blocking collectives, exchange(): lax.all_to_all(sent, FLAT, 0, 0, axis_index_groups=groups, tiled=True)  21.4 us
    all_gather x1, blocking collectives, body(): lax.all_gather(jnp.stack([defocus, blurring], axis=1), DIST, axis=0, tile...  9.18 us
    all_to_all x1, waiting for transfers between devices, exchange(): lax.all_to_all(sent, FLAT, 0, 0, axis_index_groups=groups, tiled=True)  5.52 us
    pallas_call x3, Pallas kernels, run(): pl.pallas_call(kernel, out_shape=[jax.ShapeDtypeStruct(shape, jnp.float32...  4.49 us
    all_gather x1, blocking collectives, body(): whole = lax.all_gather(bands, 'c', axis=0, tiled=True)  4.08 us
  transfers between devices with their start and end apart: 1, of which 1 were waited for; matrix products, arithmetic and copies ran while one was open for 0% of the time, Pallas kernels for 0%

profile of v8, /device:TPU:1, one launch (start us, length us, event | category | flops | bytes accessed | tf_op | source)
XLA Modules:
  0.0 68.2 jit_solution(15041285628968145095)
XLA Ops:
  0.0 0.0 copy-start.5
  0.0 2.2 %rows_forward.1 = f32[512,128]{1,0:T(8,128)} custom-call(f32[2,16,2048]{2,1,0:T(8,128)} %bitcast.23, bf16[2,128,256]{2,1,0:T(8,128)(2,1)} %constant.16.clone.table, f32[2,16,128]{2,1,0:T(8,128)} %constant.17.clone.twist), custom_call_target="tpu_custom_call" | custom-call | tf_op jit(solution)/shard_map/rows_forward/pallas_call | solution.py:259
  2.2 0.0 copy-start.1
  2.2 0.0 copy-start.2
  2.2 0.0 copy-start.3
  2.2 0.0 copy-start.4
  2.2 22.1 %all-to-all-start = ((f32[512,1,128]{2,1,0:T(1,128)}), f32[512,1,128]{2,1,0:T(1,128)S(1)}, u32[]{:S(2)}, u32[]{:S(2)}) async-start(f32[512,1,128]{2,1,0:T(1,128)} %bitcast.21), calls=%async_computation | async-start | bytes 524288 | tf_op jit(solution)/shard_map/all_to_all | solution.py:273
  25.6 0.1 maximum_bitcast_fusion
  25.7 9.2 %all-gather.1 = f32[4,1,2]{2,1,0:T(1,128)S(1)} all-gather(f32[1,1,2]{2,1,0:T(1,128)S(1)} %maximum_bitcast_fusion), channel_id=1, replica_groups=mesh['l'=2,'c'=2,'z'=8,'x'=4,'h'=4] {'l','c'}, dimensions={0}, use_global_device_ids=true | all-gather | bytes 40 | tf_op jit(solution)/shard_map/all_gather | solution.py:279
  34.9 5.5 %all-to-all-done = f32[512,1,128]{2,1,0:T(1,128)S(1)} async-done(((f32[512,1,128]{2,1,0:T(1,128)}), f32[512,1,128]{2,1,0:T(1,128)S(1)}, u32[]{:S(2)}, u32[]{:S(2)}) %all-to-all-start) | async-done | bytes 262176 | tf_op jit(solution)/shard_map/all_to_all | solution.py:273
  40.4 0.0 copy-done.5
  40.4 0.0 copy-done.1
  40.4 0.0 copy-done.2
  40.4 0.0 copy-done.3
  40.4 0.0 copy-done.4
  40.5 1.1 %columns.1 = f32[256,128]{1,0:T(8,128)S(1)} custom-call(f32[4,2]{1,0:T(4,128)S(1)} %bitcast.20, f32[512,128]{1,0:T(8,128)S(1)} %bitcast.17, bf16[2,256,128]{2,1,0:T(8,128)(2,1)S(1)} %copy-done.1, bf16[2,256,128]{2,1,0:T(8,128)(2,1)S(1)} %copy-done.2, bf16[2,128,256]{2,1,0:T(8,128)(2,1)S(1)} %copy-done.3, bf16[2,128,256]{2,1,0:T(8,128)(2,1)S(1)} %copy-done.4, ...), custom_call_target="tpu_custom_call" | custom-call | tf_op jit(solution)/shard_map/columns/pallas_call | solution.py:259
  41.6 21.4 %all_to_all.10 = f32[256,1,128]{2,1,0:T(1,128)S(1)} all-to-all(f32[256,1,128]{2,1,0:T(1,128)S(1)} %bitcast.19), channel_id=1, replica_groups={{122,378,48,304,32,288,52,308,60,316,64,320,16,272,36,292,44,300,49,305..., dimensions={0} | all-to-all | bytes 262144 | tf_op jit(solution)/shard_map/all_to_all | solution.py:273
  63.0 0.0 copy-start
  63.0 0.0 copy-start.6
  63.0 4.1 %all-gather = f32[512,1,128]{2,0,1:T(8,128)S(1)} all-gather(f32[256,1,128]{2,0,1:T(8,128)S(1)} %bitcast.22), channel_id=2, replica_groups=mesh['l'=2,'c'=2,'z'=8,'x'=4,'h'=4] {'c'}, dimensions={0}, use_global_device_ids=true | all-gather | bytes 393216 | tf_op jit(solution)/shard_map/all_gather | solution.py:285
  67.0 0.0 copy-done
  67.0 0.0 copy-done.6
  67.1 1.2 %rows_back.1 = f32[2,16,2048]{2,1,0:T(8,128)} custom-call(f32[512,128]{1,0:T(8,128)S(1)} %bitcast.18, bf16[2,256,128]{2,1,0:T(8,128)(2,1)S(1)} %copy-done, f32[2,16,128]{2,1,0:T(8,128)S(1)} %copy-done.6), custom_call_target="tpu_custom_call" | custom-call | tf_op jit(solution)/shard_map/rows_back/pallas_call | solution.py:259
Async XLA Ops:
  0.0 40.4 %copy-start.5 = (f32[2,128,128]{2,1,0:T(8,128)S(1)}, f32[2,128,128]{2,1,0:T(8,128)}, u32[]{:S(2)}) copy-start(f32[2,128,128]{2,1,0:T(8,128)} %constant.22.clone.twist) | copy-start | bytes 393220
  2.2 38.2 %copy-start.1 = (bf16[2,256,128]{2,1,0:T(8,128)(2,1)S(1)}, bf16[2,256,128]{2,1,0:T(8,128)(2,1)}, u32[]{:S(2)}) copy-start(bf16[2,256,128]{2,1,0:T(8,128)(2,1)} %constant.18.clone.forward) | copy-start | bytes 393220
  2.2 38.3 %copy-start.2 = (bf16[2,256,128]{2,1,0:T(8,128)(2,1)S(1)}, bf16[2,256,128]{2,1,0:T(8,128)(2,1)}, u32[]{:S(2)}) copy-start(bf16[2,256,128]{2,1,0:T(8,128)(2,1)} %constant.19.clone.right) | copy-start | bytes 393220
  2.2 38.3 %copy-start.3 = (bf16[2,128,256]{2,1,0:T(8,128)(2,1)S(1)}, bf16[2,128,256]{2,1,0:T(8,128)(2,1)}, u32[]{:S(2)}) copy-start(bf16[2,128,256]{2,1,0:T(8,128)(2,1)} %constant.20.clone.left) | copy-start | bytes 393220
  2.2 38.3 %copy-start.4 = (bf16[2,128,256]{2,1,0:T(8,128)(2,1)S(1)}, bf16[2,128,256]{2,1,0:T(8,128)(2,1)}, u32[]{:S(2)}) copy-start(bf16[2,128,256]{2,1,0:T(8,128)(2,1)} %constant.21.clone.back) | copy-start | bytes 393220
  2.2 38.2 %all-to-all-start = ((f32[512,1,128]{2,1,0:T(1,128)}), f32[512,1,128]{2,1,0:T(1,128)S(1)}, u32[]{:S(2)}, u32[]{:S(2)}) async-start(f32[512,1,128]{2,1,0:T(1,128)} %bitcast.21), calls=%async_computation | async-start | bytes 524288 | tf_op jit(solution)/shard_map/all_to_all | solution.py:273
  63.0 4.1 %copy-start = (bf16[2,256,128]{2,1,0:T(8,128)(2,1)S(1)}, bf16[2,256,128]{2,1,0:T(8,128)(2,1)}, u32[]{:S(2)}) copy-start(bf16[2,256,128]{2,1,0:T(8,128)(2,1)} %constant.23.clone.table) | copy-start | bytes 393220
  63.0 4.1 %copy-start.6 = (f32[2,16,128]{2,1,0:T(8,128)S(1)}, f32[2,16,128]{2,1,0:T(8,128)}, u32[]{:S(2)}) copy-start(f32[2,16,128]{2,1,0:T(8,128)} %constant.17.clone.twist) | copy-start | bytes 49156

commit v9 on v8

--- a/solution.py
+++ b/solution.py
@@ -37,11 +37,7 @@
 ORDER = far_first()
 
 
-def all_groups():
-    return [[LONG * d + int(k) for d in range(NDIST) for k in ORDER]]
-
-
-def back_groups():
+def chip_groups():
     return [[(2 * low + core) * LONG + int(k) for k in ORDER for low in range(2)] for core in range(2)]
 
 
@@ -157,7 +153,7 @@
         minus = tuple(-r for r in re)
         both = joined([joined([re, im], 0), joined([im, minus], 0)], 1)
         out.append(product(table, both, 1, 1))
-    return jnp.concatenate(out, axis=0)
+    return out
 
 
 def wave(turns):
@@ -233,7 +229,8 @@
 
 
 def first_kernel(images, table, twist, out):
-    out[...] = row_forward(images[...], table[...], twist[...])
+    for d, band in enumerate(row_forward(images[...], table[...], twist[...])):
+        out[pl.ds(d, LONG, stride=NDIST), :] = band
 
 
 def middle_kernel(par, x, forward, right, left, back, twist, out):
@@ -241,7 +238,11 @@
     defocus = [par[d : d + 1, :1] for d in range(NDIST)]
     blurring = [par[d : d + 1, 1:] for d in range(NDIST)]
     table = gains(defocus, blurring, first_col)
-    blocks = [x[LONG * d : LONG * (d + 1), :] for d in range(NDIST)]
+    core = lax.axis_index("c")
+    blocks = []
+    for d in range(NDIST):
+        start = NDIST * LONG * (d % 2) + 2 * (d // 2) + core
+        blocks.append(x[pl.ds(start, LONG, stride=NDIST), :])
     y = column_middle(blocks, table, forward[...], right[...], left[...], back[...], twist[...])
     for low in range(2):
         out[pl.ds(low, LONG, stride=2), :] = y
@@ -268,21 +269,21 @@
     return run
 
 
-def exchange(x, groups):
-    sent = x.reshape(x.shape[0], 1, LONG)
-    return lax.all_to_all(sent, FLAT, 0, 0, axis_index_groups=groups, tiled=True).reshape(x.shape)
+def exchange(x):
+    sent = x.reshape(2 * LONG, -1, LONG)
+    got = lax.all_to_all(sent, FLAT, 0, 0, axis_index_groups=chip_groups(), tiled=True)
+    return lax.all_gather(got.reshape(x.shape), "c", axis=0, tiled=True)
 
 
 def body(contrast, defocus, blurring):
     rows = NDIST * LONG
     (sent,) = call(first_kernel, ((rows, LONG),), "rows_forward", None)(contrast[0], ROW_FORWARD, ROW_TW)
     par = lax.all_gather(jnp.stack([defocus, blurring], axis=1), DIST, axis=0, tiled=True)
-    got = exchange(sent, all_groups())
+    got = exchange(sent)
     (middle,) = call(middle_kernel, ((2 * LONG, LONG),), "columns")(
         par, got, COL_FORWARD, COL_RIGHT, COL_LEFT, COL_BACK, COL_TW
     )
-    bands = exchange(middle, back_groups())
-    whole = lax.all_gather(bands, "c", axis=0, tiled=True)
+    whole = exchange(middle)
     return call(last_kernel, ((2, SHORT, SIZE),), "rows_back")(whole, ROW_BACK, ROW_TW)[0]
 
 

time: 68.5 us -> 64.9 us (0.947)
  waiting for transfers between devices: 5.52 us -> 0.05 us
  starting transfers between devices: 22.1 us -> 24.8 us
  blocking collectives: 34.6 us -> 33.9 us
    all_to_all x1, waiting for transfers between devices: 5.52 us -> 0.05 us  [exchange(): lax.all_to_all(sent, FLAT, 0, 0, axis_index_groups=chip_groups(), tiled=T...]
    all_gather x1, blocking collectives: 9.18 us -> 5.84 us  [body(): lax.all_gather(jnp.stack([defocus, blurring], axis=1), DIST, axis=0, tile...]
    all_gather x1 -> x2, blocking collectives: 4.08 us -> 7 us  [exchange(): return lax.all_gather(got.reshape(x.shape), 'c', axis=0, tiled=True)]
    all_to_all x1, starting transfers between devices: 22.1 us -> 24.8 us  [exchange(): lax.all_to_all(sent, FLAT, 0, 0, axis_index_groups=chip_groups(), tiled=T...]
where the time goes in v9:
time: 64.9 us; the launch traced here: 64.6 us
  blocking collectives  33.9 us (52%)
  starting transfers between devices  24.8 us (38%)
  Pallas kernels  4.47 us (7%)
  between operations  1.34 us (2%)
    all_to_all x1, starting transfers between devices, exchange(): lax.all_to_all(sent, FLAT, 0, 0, axis_index_groups=chip_groups(), tiled=T...  24.8 us
    all_to_all x1, blocking collectives, exchange(): lax.all_to_all(sent, FLAT, 0, 0, axis_index_groups=chip_groups(), tiled=T...  21.1 us
    all_gather x2, blocking collectives, exchange(): return lax.all_gather(got.reshape(x.shape), 'c', axis=0, tiled=True)  7 us
    all_gather x1, blocking collectives, body(): lax.all_gather(jnp.stack([defocus, blurring], axis=1), DIST, axis=0, tile...  5.84 us
    pallas_call x3, Pallas kernels, run(): pl.pallas_call(kernel, out_shape=[jax.ShapeDtypeStruct(shape, jnp.float32...  4.47 us
  transfers between devices with their start and end apart: 1, of which 1 were waited for; matrix products, arithmetic and copies ran while one was open for 0% of the time, Pallas kernels for 0%

profile of v9, /device:TPU:1, one launch (start us, length us, event | category | flops | bytes accessed | tf_op | source)
XLA Modules:
  0.0 64.6 jit_solution(15226887287552211214)
XLA Ops:
  0.0 2.1 %rows_forward.1 = f32[512,128]{1,0:T(8,128)} custom-call(f32[2,16,2048]{2,1,0:T(8,128)} %bitcast.21, bf16[2,128,256]{2,1,0:T(8,128)(2,1)} %constant.16.clone.table, f32[2,16,128]{2,1,0:T(8,128)} %constant.17.clone.twist), custom_call_target="tpu_custom_call" | custom-call | tf_op jit(solution)/shard_map/rows_forward/pallas_call | solution.py:260
  2.1 24.8 %all-to-all-start = ((f32[256,2,128]{2,1,0:T(2,128)}), f32[256,2,128]{2,1,0:T(2,128)S(1)}, u32[]{:S(2)}, u32[]{:S(2)}) async-start(f32[256,2,128]{2,1,0:T(2,128)} %bitcast.19), calls=%async_computation | async-start | bytes 524288 | tf_op jit(solution)/shard_map/all_to_all | solution.py:274
  28.2 0.1 maximum_bitcast_fusion
  28.3 5.8 %all-gather.1 = f32[4,1,2]{2,1,0:T(1,128)S(1)} all-gather(f32[1,1,2]{2,1,0:T(1,128)S(1)} %maximum_bitcast_fusion), channel_id=1, replica_groups=mesh['l'=2,'c'=2,'z'=8,'x'=4,'h'=4] {'l','c'}, dimensions={0}, use_global_device_ids=true | all-gather | bytes 40 | tf_op jit(solution)/shard_map/all_gather | solution.py:281
  34.2 0.1 all-to-all-done
  34.2 0.0 copy-start
  34.2 0.0 copy-start.1
  34.2 0.0 copy-start.2
  34.2 0.0 copy-start.3
  34.2 0.0 copy-start.4
  34.2 3.7 %all_gather.10.x = f32[1024,128]{1,0:T(8,128)S(1)} all-gather(f32[512,128]{1,0:T(8,128)S(1)} %bitcast.18), channel_id=1, replica_groups=mesh['l'=2,'c'=2,'z'=8,'x'=4,'h'=4] {'c'}, dimensions={0}, use_global_device_ids=true | all-gather | bytes 786432 | tf_op jit(solution)/shard_map/all_gather | solution.py:275
  37.9 0.0 copy-done
  37.9 0.0 copy-done.1
  37.9 0.0 copy-done.2
  37.9 0.0 copy-done.3
  37.9 0.0 copy-done.4
  38.0 1.1 %columns.1 = f32[256,128]{1,0:T(8,128)S(1)} custom-call(f32[4,2]{1,0:T(4,128)S(1)} %bitcast.17, f32[1024,128]{1,0:T(8,128)S(1)} %all_gather.10.x, bf16[2,256,128]{2,1,0:T(8,128)(2,1)S(1)} %copy-done, bf16[2,256,128]{2,1,0:T(8,128)(2,1)S(1)} %copy-done.1, bf16[2,128,256]{2,1,0:T(8,128)(2,1)S(1)} %copy-done.2, bf16[2,128,256]{2,1,0:T(8,128)(2,1)S(1)} %copy-done.3, ...), custom_call_target="tpu_custom_call" | custom-call | tf_op jit(solution)/shard_map/columns/pallas_call | solution.py:260
  39.1 21.1 %all_to_all.10 = f32[256,1,128]{2,1,0:T(1,128)S(1)} all-to-all(f32[256,1,128]{2,1,0:T(1,128)S(1)} %bitcast.16), channel_id=1, replica_groups={{122,378,48,304,32,288,52,308,60,316,64,320,16,272,36,292,44,300,49,305..., dimensions={0} | all-to-all | bytes 262144 | tf_op jit(solution)/shard_map/all_to_all | solution.py:274
  60.2 0.0 copy-start.5
  60.2 0.0 copy-start.6
  60.2 3.3 %all-gather = f32[512,1,128]{2,0,1:T(8,128)S(1)} all-gather(f32[256,1,128]{2,0,1:T(8,128)S(1)} %bitcast.20), channel_id=2, replica_groups=mesh['l'=2,'c'=2,'z'=8,'x'=4,'h'=4] {'c'}, dimensions={0}, use_global_device_ids=true | all-gather | bytes 393216 | tf_op jit(solution)/shard_map/all_gather | solution.py:275
  63.5 0.0 copy-done.5
  63.5 0.0 copy-done.6
  63.5 1.2 %rows_back.1 = f32[2,16,2048]{2,1,0:T(8,128)} custom-call(f32[512,128]{1,0:T(8,128)S(1)} %bitcast.15, bf16[2,256,128]{2,1,0:T(8,128)(2,1)S(1)} %copy-done.5, f32[2,16,128]{2,1,0:T(8,128)S(1)} %copy-done.6), custom_call_target="tpu_custom_call" | custom-call | tf_op jit(solution)/shard_map/rows_back/pallas_call | solution.py:260
Async XLA Ops:
  2.1 32.1 %all-to-all-start = ((f32[256,2,128]{2,1,0:T(2,128)}), f32[256,2,128]{2,1,0:T(2,128)S(1)}, u32[]{:S(2)}, u32[]{:S(2)}) async-start(f32[256,2,128]{2,1,0:T(2,128)} %bitcast.19), calls=%async_computation | async-start | bytes 524288 | tf_op jit(solution)/shard_map/all_to_all | solution.py:274
  34.2 3.7 %copy-start = (bf16[2,256,128]{2,1,0:T(8,128)(2,1)S(1)}, bf16[2,256,128]{2,1,0:T(8,128)(2,1)}, u32[]{:S(2)}) copy-start(bf16[2,256,128]{2,1,0:T(8,128)(2,1)} %constant.18.clone.forward) | copy-start | bytes 393220
  34.2 3.7 %copy-start.1 = (bf16[2,256,128]{2,1,0:T(8,128)(2,1)S(1)}, bf16[2,256,128]{2,1,0:T(8,128)(2,1)}, u32[]{:S(2)}) copy-start(bf16[2,256,128]{2,1,0:T(8,128)(2,1)} %constant.19.clone.right) | copy-start | bytes 393220
  34.2 3.7 %copy-start.2 = (bf16[2,128,256]{2,1,0:T(8,128)(2,1)S(1)}, bf16[2,128,256]{2,1,0:T(8,128)(2,1)}, u32[]{:S(2)}) copy-start(bf16[2,128,256]{2,1,0:T(8,128)(2,1)} %constant.20.clone.left) | copy-start | bytes 393220
  34.2 3.7 %copy-start.3 = (bf16[2,128,256]{2,1,0:T(8,128)(2,1)S(1)}, bf16[2,128,256]{2,1,0:T(8,128)(2,1)}, u32[]{:S(2)}) copy-start(bf16[2,128,256]{2,1,0:T(8,128)(2,1)} %constant.21.clone.back) | copy-start | bytes 393220
  34.2 3.7 %copy-start.4 = (f32[2,128,128]{2,1,0:T(8,128)S(1)}, f32[2,128,128]{2,1,0:T(8,128)}, u32[]{:S(2)}) copy-start(f32[2,128,128]{2,1,0:T(8,128)} %constant.22.clone.twist) | copy-start | bytes 393220
  60.2 3.3 %copy-start.5 = (bf16[2,256,128]{2,1,0:T(8,128)(2,1)S(1)}, bf16[2,256,128]{2,1,0:T(8,128)(2,1)}, u32[]{:S(2)}) copy-start(bf16[2,256,128]{2,1,0:T(8,128)(2,1)} %constant.23.clone.table) | copy-start | bytes 393220
  60.2 3.3 %copy-start.6 = (f32[2,16,128]{2,1,0:T(8,128)S(1)}, f32[2,16,128]{2,1,0:T(8,128)}, u32[]{:S(2)}) copy-start(f32[2,16,128]{2,1,0:T(8,128)} %constant.17.clone.twist) | copy-start | bytes 49156

commit v10 on v9

--- a/solution.py
+++ b/solution.py
@@ -199,12 +199,9 @@
         u, v = both[:LONG], both[LONG:]
         parts.append(joined([halves(u * c - v * s), halves(v * c + u * s)], 1))
     spectra = product(joined(parts, 0), right)
-    numerator = gain[0] * spectra[:LONG]
-    weight = gain[0] * gain[0]
+    quotient = gain[0] * spectra[:LONG]
     for d in range(1, NDIST):
-        numerator = numerator + gain[d] * spectra[LONG * d : LONG * (d + 1)]
-        weight = weight + gain[d] * gain[d]
-    quotient = numerator / (2.0 * (weight + REGULARIZER))
+        quotient = quotient + gain[d] * spectra[LONG * d : LONG * (d + 1)]
     both = product(halves(quotient), left)
     a, b = both[:, :LONG], both[:, LONG:]
     upright = joined([halves(a * c - b * s), halves(b * c + a * s)], 0)
@@ -233,17 +230,26 @@
         out[pl.ds(d, LONG, stride=NDIST), :] = band
 
 
-def middle_kernel(par, x, forward, right, left, back, twist, out):
+def gain_kernel(par, out):
     first_col = SHORT * lax.axis_index(PIX) + WIDE * lax.axis_index(DIST)
     defocus = [par[d : d + 1, :1] for d in range(NDIST)]
     blurring = [par[d : d + 1, 1:] for d in range(NDIST)]
     table = gains(defocus, blurring, first_col)
+    weight = table[0] * table[0]
+    for g in table[1:]:
+        weight = weight + g * g
+    share = 0.5 / (weight + REGULARIZER)
+    for d, g in enumerate(table):
+        out[d, :, :] = g * share
+
+
+def middle_kernel(gain, x, forward, right, left, back, twist, out):
     core = lax.axis_index("c")
     blocks = []
     for d in range(NDIST):
         start = NDIST * LONG * (d % 2) + 2 * (d // 2) + core
         blocks.append(x[pl.ds(start, LONG, stride=NDIST), :])
-    y = column_middle(blocks, table, forward[...], right[...], left[...], back[...], twist[...])
+    y = column_middle(blocks, gain[...], forward[...], right[...], left[...], back[...], twist[...])
     for low in range(2):
         out[pl.ds(low, LONG, stride=2), :] = y
 
@@ -280,8 +286,9 @@
     (sent,) = call(first_kernel, ((rows, LONG),), "rows_forward", None)(contrast[0], ROW_FORWARD, ROW_TW)
     par = lax.all_gather(jnp.stack([defocus, blurring], axis=1), DIST, axis=0, tiled=True)
     got = exchange(sent)
+    (gain,) = call(gain_kernel, ((NDIST, LONG, LONG),), "gains")(par)
     (middle,) = call(middle_kernel, ((2 * LONG, LONG),), "columns")(
-        par, got, COL_FORWARD, COL_RIGHT, COL_LEFT, COL_BACK, COL_TW
+        gain, got, COL_FORWARD, COL_RIGHT, COL_LEFT, COL_BACK, COL_TW
     )
     whole = exchange(middle)
     return call(last_kernel, ((2, SHORT, SIZE),), "rows_back")(whole, ROW_BACK, ROW_TW)[0]

time: 64.9 us -> 64.9 us (level)
    pallas_call x3 -> x4, Pallas kernels: 4.47 us -> 4.71 us  [run(): pl.pallas_call(kernel, out_shape=[jax.ShapeDtypeStruct(shape, jnp.float32...]
  transfers between devices with their start and end apart: 1 -> 1, of which waited for: 1 -> 0; matrix products, arithmetic and copies ran while one was open for 0% -> 0% of each run, Pallas kernels for 0% -> 0%
where the time goes in v10:
time: 64.9 us; the launch traced here: 64.6 us
  blocking collectives  33.6 us (52%)
  starting transfers between devices  24.8 us (38%)
  Pallas kernels  4.71 us (7%)
  between operations  1.38 us (2%)
    all_to_all x1, starting transfers between devices, exchange(): lax.all_to_all(sent, FLAT, 0, 0, axis_index_groups=chip_groups(), tiled=T...  24.8 us
    all_to_all x1, blocking collectives, exchange(): lax.all_to_all(sent, FLAT, 0, 0, axis_index_groups=chip_groups(), tiled=T...  21 us
    all_gather x2, blocking collectives, exchange(): return lax.all_gather(got.reshape(x.shape), 'c', axis=0, tiled=True)  6.73 us
    all_gather x1, blocking collectives, body(): lax.all_gather(jnp.stack([defocus, blurring], axis=1), DIST, axis=0, tile...  5.84 us
    pallas_call x4, Pallas kernels, run(): pl.pallas_call(kernel, out_shape=[jax.ShapeDtypeStruct(shape, jnp.float32...  4.71 us
  transfers between devices with their start and end apart: 1, of which 0 were waited for; matrix products, arithmetic and copies ran while one was open for 0% of the time, Pallas kernels for 0%

profile of v10, /device:TPU:1, one launch (start us, length us, event | category | flops | bytes accessed | tf_op | source)
XLA Modules:
  0.0 64.6 jit_solution(3938231520855590471)
XLA Ops:
  0.0 2.1 %rows_forward.1 = f32[512,128]{1,0:T(8,128)} custom-call(f32[2,16,2048]{2,1,0:T(8,128)} %bitcast.21, bf16[2,128,256]{2,1,0:T(8,128)(2,1)} %constant.16.clone.table, f32[2,16,128]{2,1,0:T(8,128)} %constant.17.clone.twist), custom_call_target="tpu_custom_call" | custom-call | tf_op jit(solution)/shard_map/rows_forward/pallas_call | solution.py:266
  2.1 24.8 %all-to-all-start = ((f32[256,2,128]{2,1,0:T(2,128)}), f32[256,2,128]{2,1,0:T(2,128)S(1)}, u32[]{:S(2)}, u32[]{:S(2)}) async-start(f32[256,2,128]{2,1,0:T(2,128)} %bitcast.19), calls=%async_computation | async-start | bytes 524288 | tf_op jit(solution)/shard_map/all_to_all | solution.py:280
  28.2 0.1 maximum_bitcast_fusion
  28.3 5.8 %all-gather.1 = f32[4,1,2]{2,1,0:T(1,128)S(1)} all-gather(f32[1,1,2]{2,1,0:T(1,128)S(1)} %maximum_bitcast_fusion), channel_id=1, replica_groups=mesh['l'=2,'c'=2,'z'=8,'x'=4,'h'=4] {'l','c'}, dimensions={0}, use_global_device_ids=true | all-gather | bytes 40 | tf_op jit(solution)/shard_map/all_gather | solution.py:287
  34.2 0.3 gains.1.gain
  34.4 0.0 all-to-all-done
  34.4 0.0 copy-start
  34.5 0.0 copy-start.1
  34.5 0.0 copy-start.2
  34.5 0.0 copy-start.3
  34.5 0.0 copy-start.4
  34.5 3.4 %all_gather.10.x = f32[1024,128]{1,0:T(8,128)S(1)} all-gather(f32[512,128]{1,0:T(8,128)S(1)} %bitcast.18), channel_id=1, replica_groups=mesh['l'=2,'c'=2,'z'=8,'x'=4,'h'=4] {'c'}, dimensions={0}, use_global_device_ids=true | all-gather | bytes 786432 | tf_op jit(solution)/shard_map/all_gather | solution.py:281
  37.9 0.0 copy-done
  37.9 0.0 copy-done.1
  37.9 0.0 copy-done.2
  37.9 0.0 copy-done.3
  37.9 0.0 copy-done.4
  38.0 1.1 %columns.1 = f32[256,128]{1,0:T(8,128)S(1)} custom-call(f32[4,128,128]{2,1,0:T(8,128)S(1)} %gains.1.gain, f32[1024,128]{1,0:T(8,128)S(1)} %all_gather.10.x, bf16[2,256,128]{2,1,0:T(8,128)(2,1)S(1)} %copy-done, bf16[2,256,128]{2,1,0:T(8,128)(2,1)S(1)} %copy-done.1, bf16[2,128,256]{2,1,0:T(8,128)(2,1)S(1)} %copy-done.2, bf16[2,128,256]{2,1,0:T(8,128)(2,1)S(1)} %copy-done.3, ...), custom_call_target="tpu_custom_call" | custom-call | tf_op jit(solution)/shard_map/columns/pallas_call | solution.py:266
  39.1 21.0 %all_to_all.10 = f32[256,1,128]{2,1,0:T(1,128)S(1)} all-to-all(f32[256,1,128]{2,1,0:T(1,128)S(1)} %bitcast.16), channel_id=1, replica_groups={{122,378,48,304,32,288,52,308,60,316,64,320,16,272,36,292,44,300,49,305..., dimensions={0} | all-to-all | bytes 262144 | tf_op jit(solution)/shard_map/all_to_all | solution.py:280
  60.1 0.0 copy-start.5
  60.1 0.0 copy-start.6
  60.1 3.3 %all-gather = f32[512,1,128]{2,0,1:T(8,128)S(1)} all-gather(f32[256,1,128]{2,0,1:T(8,128)S(1)} %bitcast.20), channel_id=2, replica_groups=mesh['l'=2,'c'=2,'z'=8,'x'=4,'h'=4] {'c'}, dimensions={0}, use_global_device_ids=true | all-gather | bytes 393216 | tf_op jit(solution)/shard_map/all_gather | solution.py:281
  63.4 0.0 copy-done.5
  63.4 0.0 copy-done.6
  63.4 1.2 %rows_back.1 = f32[2,16,2048]{2,1,0:T(8,128)} custom-call(f32[512,128]{1,0:T(8,128)S(1)} %bitcast.15, bf16[2,256,128]{2,1,0:T(8,128)(2,1)S(1)} %copy-done.5, f32[2,16,128]{2,1,0:T(8,128)S(1)} %copy-done.6), custom_call_target="tpu_custom_call" | custom-call | tf_op jit(solution)/shard_map/rows_back/pallas_call | solution.py:266
Async XLA Ops:
  2.1 32.3 %all-to-all-start = ((f32[256,2,128]{2,1,0:T(2,128)}), f32[256,2,128]{2,1,0:T(2,128)S(1)}, u32[]{:S(2)}, u32[]{:S(2)}) async-start(f32[256,2,128]{2,1,0:T(2,128)} %bitcast.19), calls=%async_computation | async-start | bytes 524288 | tf_op jit(solution)/shard_map/all_to_all | solution.py:280
  34.4 3.5 %copy-start = (bf16[2,256,128]{2,1,0:T(8,128)(2,1)S(1)}, bf16[2,256,128]{2,1,0:T(8,128)(2,1)}, u32[]{:S(2)}) copy-start(bf16[2,256,128]{2,1,0:T(8,128)(2,1)} %constant.18.clone.forward) | copy-start | bytes 393220
  34.5 3.5 %copy-start.1 = (bf16[2,256,128]{2,1,0:T(8,128)(2,1)S(1)}, bf16[2,256,128]{2,1,0:T(8,128)(2,1)}, u32[]{:S(2)}) copy-start(bf16[2,256,128]{2,1,0:T(8,128)(2,1)} %constant.19.clone.right) | copy-start | bytes 393220
  34.5 3.5 %copy-start.2 = (bf16[2,128,256]{2,1,0:T(8,128)(2,1)S(1)}, bf16[2,128,256]{2,1,0:T(8,128)(2,1)}, u32[]{:S(2)}) copy-start(bf16[2,128,256]{2,1,0:T(8,128)(2,1)} %constant.20.clone.left) | copy-start | bytes 393220
  34.5 3.5 %copy-start.3 = (bf16[2,128,256]{2,1,0:T(8,128)(2,1)S(1)}, bf16[2,128,256]{2,1,0:T(8,128)(2,1)}, u32[]{:S(2)}) copy-start(bf16[2,128,256]{2,1,0:T(8,128)(2,1)} %constant.21.clone.back) | copy-start | bytes 393220
  34.5 3.5 %copy-start.4 = (f32[2,128,128]{2,1,0:T(8,128)S(1)}, f32[2,128,128]{2,1,0:T(8,128)}, u32[]{:S(2)}) copy-start(f32[2,128,128]{2,1,0:T(8,128)} %constant.22.clone.twist) | copy-start | bytes 393220
  60.1 3.3 %copy-start.5 = (bf16[2,256,128]{2,1,0:T(8,128)(2,1)S(1)}, bf16[2,256,128]{2,1,0:T(8,128)(2,1)}, u32[]{:S(2)}) copy-start(bf16[2,256,128]{2,1,0:T(8,128)(2,1)} %constant.23.clone.table) | copy-start | bytes 393220
  60.1 3.3 %copy-start.6 = (f32[2,16,128]{2,1,0:T(8,128)S(1)}, f32[2,16,128]{2,1,0:T(8,128)}, u32[]{:S(2)}) copy-start(f32[2,16,128]{2,1,0:T(8,128)} %constant.17.clone.twist) | copy-start | bytes 49156

commit v11 on v10

--- a/solution.py
+++ b/solution.py
@@ -23,7 +23,7 @@
 FLAT = DIST + PIX
 
 
-FIRST = (7, 2, 2)
+FIRST = (5, 2, 2)
 
 
 def far_first():

time: 64.9 us -> 63.1 us (0.972)
  blocking collectives: 33.6 us -> 32 us
    all_gather x2, blocking collectives: 6.73 us -> 5.57 us  [exchange(): return lax.all_gather(got.reshape(x.shape), 'c', axis=0, tiled=True)]
where the time goes in v11:
time: 63.1 us; the launch traced here: 62.8 us
  blocking collectives  32 us (51%)
  starting transfers between devices  24.6 us (39%)
  Pallas kernels  4.71 us (7%)
  between operations  1.39 us (2%)
    all_to_all x1, starting transfers between devices, exchange(): lax.all_to_all(sent, FLAT, 0, 0, axis_index_groups=chip_groups(), tiled=T...  24.6 us
    all_to_all x1, blocking collectives, exchange(): lax.all_to_all(sent, FLAT, 0, 0, axis_index_groups=chip_groups(), tiled=T...  20.5 us
    all_gather x1, blocking collectives, body(): lax.all_gather(jnp.stack([defocus, blurring], axis=1), DIST, axis=0, tile...  6.01 us
    all_gather x2, blocking collectives, exchange(): return lax.all_gather(got.reshape(x.shape), 'c', axis=0, tiled=True)  5.57 us
    pallas_call x4, Pallas kernels, run(): pl.pallas_call(kernel, out_shape=[jax.ShapeDtypeStruct(shape, jnp.float32...  4.71 us
  transfers between devices with their start and end apart: 1, of which 0 were waited for; matrix products, arithmetic and copies ran while one was open for 0% of the time, Pallas kernels for 0%

profile of v11, /device:TPU:1, one launch (start us, length us, event | category | flops | bytes accessed | tf_op | source)
XLA Modules:
  0.0 62.8 jit_solution(5789001905405817779)
XLA Ops:
  0.0 2.1 %rows_forward.1 = f32[512,128]{1,0:T(8,128)} custom-call(f32[2,16,2048]{2,1,0:T(8,128)} %bitcast.21, bf16[2,128,256]{2,1,0:T(8,128)(2,1)} %constant.16.clone.table, f32[2,16,128]{2,1,0:T(8,128)} %constant.17.clone.twist), custom_call_target="tpu_custom_call" | custom-call | tf_op jit(solution)/shard_map/rows_forward/pallas_call | solution.py:266
  2.1 24.6 %all-to-all-start = ((f32[256,2,128]{2,1,0:T(2,128)}), f32[256,2,128]{2,1,0:T(2,128)S(1)}, u32[]{:S(2)}, u32[]{:S(2)}) async-start(f32[256,2,128]{2,1,0:T(2,128)} %bitcast.19), calls=%async_computation | async-start | bytes 524288 | tf_op jit(solution)/shard_map/all_to_all | solution.py:280
  28.0 0.1 maximum_bitcast_fusion
  28.1 6.0 %all-gather.1 = f32[4,1,2]{2,1,0:T(1,128)S(1)} all-gather(f32[1,1,2]{2,1,0:T(1,128)S(1)} %maximum_bitcast_fusion), channel_id=1, replica_groups=mesh['l'=2,'c'=2,'z'=8,'x'=4,'h'=4] {'l','c'}, dimensions={0}, use_global_device_ids=true | all-gather | bytes 40 | tf_op jit(solution)/shard_map/all_gather | solution.py:287
  34.1 0.3 gains.1.gain
  34.4 0.0 all-to-all-done
  34.4 0.0 copy-start
  34.4 0.0 copy-start.1
  34.4 0.0 copy-start.2
  34.4 0.0 copy-start.3
  34.5 0.0 copy-start.4
  34.5 2.3 %all_gather.10.x = f32[1024,128]{1,0:T(8,128)S(1)} all-gather(f32[512,128]{1,0:T(8,128)S(1)} %bitcast.18), channel_id=1, replica_groups=mesh['l'=2,'c'=2,'z'=8,'x'=4,'h'=4] {'c'}, dimensions={0}, use_global_device_ids=true | all-gather | bytes 786432 | tf_op jit(solution)/shard_map/all_gather | solution.py:281
  36.8 0.0 copy-done
  36.8 0.0 copy-done.1
  36.8 0.0 copy-done.2
  36.8 0.0 copy-done.3
  36.8 0.0 copy-done.4
  36.8 1.1 %columns.1 = f32[256,128]{1,0:T(8,128)S(1)} custom-call(f32[4,128,128]{2,1,0:T(8,128)S(1)} %gains.1.gain, f32[1024,128]{1,0:T(8,128)S(1)} %all_gather.10.x, bf16[2,256,128]{2,1,0:T(8,128)(2,1)S(1)} %copy-done, bf16[2,256,128]{2,1,0:T(8,128)(2,1)S(1)} %copy-done.1, bf16[2,128,256]{2,1,0:T(8,128)(2,1)S(1)} %copy-done.2, bf16[2,128,256]{2,1,0:T(8,128)(2,1)S(1)} %copy-done.3, ...), custom_call_target="tpu_custom_call" | custom-call | tf_op jit(solution)/shard_map/columns/pallas_call | solution.py:266
  37.9 20.5 %all_to_all.10 = f32[256,1,128]{2,1,0:T(1,128)S(1)} all-to-all(f32[256,1,128]{2,1,0:T(1,128)S(1)} %bitcast.16), channel_id=1, replica_groups={{90,346,16,272,0,256,20,276,28,284,32,288,4,260,12,268,17,273,19,275,24..., dimensions={0} | all-to-all | bytes 262144 | tf_op jit(solution)/shard_map/all_to_all | solution.py:280
  58.4 0.0 copy-start.5
  58.4 0.0 copy-start.6
  58.4 3.3 %all-gather = f32[512,1,128]{2,0,1:T(8,128)S(1)} all-gather(f32[256,1,128]{2,0,1:T(8,128)S(1)} %bitcast.20), channel_id=2, replica_groups=mesh['l'=2,'c'=2,'z'=8,'x'=4,'h'=4] {'c'}, dimensions={0}, use_global_device_ids=true | all-gather | bytes 393216 | tf_op jit(solution)/shard_map/all_gather | solution.py:281
  61.7 0.0 copy-done.5
  61.7 0.0 copy-done.6
  61.7 1.2 %rows_back.1 = f32[2,16,2048]{2,1,0:T(8,128)} custom-call(f32[512,128]{1,0:T(8,128)S(1)} %bitcast.15, bf16[2,256,128]{2,1,0:T(8,128)(2,1)S(1)} %copy-done.5, f32[2,16,128]{2,1,0:T(8,128)S(1)} %copy-done.6), custom_call_target="tpu_custom_call" | custom-call | tf_op jit(solution)/shard_map/rows_back/pallas_call | solution.py:266
Async XLA Ops:
  2.1 32.2 %all-to-all-start = ((f32[256,2,128]{2,1,0:T(2,128)}), f32[256,2,128]{2,1,0:T(2,128)S(1)}, u32[]{:S(2)}, u32[]{:S(2)}) async-start(f32[256,2,128]{2,1,0:T(2,128)} %bitcast.19), calls=%async_computation | async-start | bytes 524288 | tf_op jit(solution)/shard_map/all_to_all | solution.py:280
  34.4 2.4 %copy-start = (bf16[2,256,128]{2,1,0:T(8,128)(2,1)S(1)}, bf16[2,256,128]{2,1,0:T(8,128)(2,1)}, u32[]{:S(2)}) copy-start(bf16[2,256,128]{2,1,0:T(8,128)(2,1)} %constant.18.clone.forward) | copy-start | bytes 393220
  34.4 2.4 %copy-start.1 = (bf16[2,256,128]{2,1,0:T(8,128)(2,1)S(1)}, bf16[2,256,128]{2,1,0:T(8,128)(2,1)}, u32[]{:S(2)}) copy-start(bf16[2,256,128]{2,1,0:T(8,128)(2,1)} %constant.19.clone.right) | copy-start | bytes 393220
  34.4 2.4 %copy-start.2 = (bf16[2,128,256]{2,1,0:T(8,128)(2,1)S(1)}, bf16[2,128,256]{2,1,0:T(8,128)(2,1)}, u32[]{:S(2)}) copy-start(bf16[2,128,256]{2,1,0:T(8,128)(2,1)} %constant.20.clone.left) | copy-start | bytes 393220
  34.4 2.4 %copy-start.3 = (bf16[2,128,256]{2,1,0:T(8,128)(2,1)S(1)}, bf16[2,128,256]{2,1,0:T(8,128)(2,1)}, u32[]{:S(2)}) copy-start(bf16[2,128,256]{2,1,0:T(8,128)(2,1)} %constant.21.clone.back) | copy-start | bytes 393220
  34.5 2.3 %copy-start.4 = (f32[2,128,128]{2,1,0:T(8,128)S(1)}, f32[2,128,128]{2,1,0:T(8,128)}, u32[]{:S(2)}) copy-start(f32[2,128,128]{2,1,0:T(8,128)} %constant.22.clone.twist) | copy-start | bytes 393220
  58.4 3.3 %copy-start.5 = (bf16[2,256,128]{2,1,0:T(8,128)(2,1)S(1)}, bf16[2,256,128]{2,1,0:T(8,128)(2,1)}, u32[]{:S(2)}) copy-start(bf16[2,256,128]{2,1,0:T(8,128)(2,1)} %constant.23.clone.table) | copy-start | bytes 393220
  58.4 3.3 %copy-start.6 = (f32[2,16,128]{2,1,0:T(8,128)S(1)}, f32[2,16,128]{2,1,0:T(8,128)}, u32[]{:S(2)}) copy-start(f32[2,16,128]{2,1,0:T(8,128)} %constant.17.clone.twist) | copy-start | bytes 49156

commit v12 on v11

--- a/solution.py
+++ b/solution.py
@@ -23,7 +23,7 @@
 FLAT = DIST + PIX
 
 
-FIRST = (5, 2, 2)
+FIRST = (4, 2, 2)
 
 
 def far_first():

time: 63.1 us -> 63.5 us (level)
  starting transfers between devices: 24.6 us -> 25.4 us
    all_to_all x1, starting transfers between devices: 24.6 us -> 25.4 us  [exchange(): lax.all_to_all(sent, FLAT, 0, 0, axis_index_groups=chip_groups(), tiled=T...]
where the time goes in v12:
time: 63.5 us; the launch traced here: 63.2 us
  blocking collectives  31.6 us (50%)
  starting transfers between devices  25.4 us (40%)
  Pallas kernels  4.71 us (7%)
  between operations  1.39 us (2%)
    all_to_all x1, starting transfers between devices, exchange(): lax.all_to_all(sent, FLAT, 0, 0, axis_index_groups=chip_groups(), tiled=T...  25.4 us
    all_to_all x1, blocking collectives, exchange(): lax.all_to_all(sent, FLAT, 0, 0, axis_index_groups=chip_groups(), tiled=T...  20.2 us
    all_gather x1, blocking collectives, body(): lax.all_gather(jnp.stack([defocus, blurring], axis=1), DIST, axis=0, tile...  6.12 us
    all_gather x2, blocking collectives, exchange(): return lax.all_gather(got.reshape(x.shape), 'c', axis=0, tiled=True)  5.23 us
    pallas_call x4, Pallas kernels, run(): pl.pallas_call(kernel, out_shape=[jax.ShapeDtypeStruct(shape, jnp.float32...  4.71 us
  transfers between devices with their start and end apart: 1, of which 0 were waited for; matrix products, arithmetic and copies ran while one was open for 0% of the time, Pallas kernels for 0%

profile of v12, /device:TPU:1, one launch (start us, length us, event | category | flops | bytes accessed | tf_op | source)
XLA Modules:
  0.0 63.2 jit_solution(11308608743255971197)
XLA Ops:
  0.0 2.1 %rows_forward.1 = f32[512,128]{1,0:T(8,128)} custom-call(f32[2,16,2048]{2,1,0:T(8,128)} %bitcast.21, bf16[2,128,256]{2,1,0:T(8,128)(2,1)} %constant.16.clone.table, f32[2,16,128]{2,1,0:T(8,128)} %constant.17.clone.twist), custom_call_target="tpu_custom_call" | custom-call | tf_op jit(solution)/shard_map/rows_forward/pallas_call | solution.py:266
  2.1 25.4 %all-to-all-start = ((f32[256,2,128]{2,1,0:T(2,128)}), f32[256,2,128]{2,1,0:T(2,128)S(1)}, u32[]{:S(2)}, u32[]{:S(2)}) async-start(f32[256,2,128]{2,1,0:T(2,128)} %bitcast.19), calls=%async_computation | async-start | bytes 524288 | tf_op jit(solution)/shard_map/all_to_all | solution.py:280
  28.8 0.1 maximum_bitcast_fusion
  28.9 6.1 %all-gather.1 = f32[4,1,2]{2,1,0:T(1,128)S(1)} all-gather(f32[1,1,2]{2,1,0:T(1,128)S(1)} %maximum_bitcast_fusion), channel_id=1, replica_groups=mesh['l'=2,'c'=2,'z'=8,'x'=4,'h'=4] {'l','c'}, dimensions={0}, use_global_device_ids=true | all-gather | bytes 40 | tf_op jit(solution)/shard_map/all_gather | solution.py:287
  35.0 0.3 gains.1.gain
  35.3 0.0 all-to-all-done
  35.3 0.0 copy-start
  35.3 0.0 copy-start.1
  35.3 0.0 copy-start.2
  35.3 0.0 copy-start.3
  35.4 0.0 copy-start.4
  35.4 2.3 %all_gather.10.x = f32[1024,128]{1,0:T(8,128)S(1)} all-gather(f32[512,128]{1,0:T(8,128)S(1)} %bitcast.18), channel_id=1, replica_groups=mesh['l'=2,'c'=2,'z'=8,'x'=4,'h'=4] {'c'}, dimensions={0}, use_global_device_ids=true | all-gather | bytes 786432 | tf_op jit(solution)/shard_map/all_gather | solution.py:281
  37.7 0.0 copy-done
  37.7 0.0 copy-done.1
  37.7 0.0 copy-done.2
  37.7 0.0 copy-done.3
  37.7 0.0 copy-done.4
  37.7 1.1 %columns.1 = f32[256,128]{1,0:T(8,128)S(1)} custom-call(f32[4,128,128]{2,1,0:T(8,128)S(1)} %gains.1.gain, f32[1024,128]{1,0:T(8,128)S(1)} %all_gather.10.x, bf16[2,256,128]{2,1,0:T(8,128)(2,1)S(1)} %copy-done, bf16[2,256,128]{2,1,0:T(8,128)(2,1)S(1)} %copy-done.1, bf16[2,128,256]{2,1,0:T(8,128)(2,1)S(1)} %copy-done.2, bf16[2,128,256]{2,1,0:T(8,128)(2,1)S(1)} %copy-done.3, ...), custom_call_target="tpu_custom_call" | custom-call | tf_op jit(solution)/shard_map/columns/pallas_call | solution.py:266
  38.8 20.2 %all_to_all.10 = f32[256,1,128]{2,1,0:T(1,128)S(1)} all-to-all(f32[256,1,128]{2,1,0:T(1,128)S(1)} %bitcast.16), channel_id=1, replica_groups={{74,330,0,256,4,260,12,268,16,272,112,368,1,257,3,259,8,264,20,276,28,2..., dimensions={0} | all-to-all | bytes 262144 | tf_op jit(solution)/shard_map/all_to_all | solution.py:280
  59.1 0.0 copy-start.5
  59.1 0.0 copy-start.6
  59.1 2.9 %all-gather = f32[512,1,128]{2,0,1:T(8,128)S(1)} all-gather(f32[256,1,128]{2,0,1:T(8,128)S(1)} %bitcast.20), channel_id=2, replica_groups=mesh['l'=2,'c'=2,'z'=8,'x'=4,'h'=4] {'c'}, dimensions={0}, use_global_device_ids=true | all-gather | bytes 393216 | tf_op jit(solution)/shard_map/all_gather | solution.py:281
  62.0 0.0 copy-done.5
  62.0 0.0 copy-done.6
  62.0 1.2 %rows_back.1 = f32[2,16,2048]{2,1,0:T(8,128)} custom-call(f32[512,128]{1,0:T(8,128)S(1)} %bitcast.15, bf16[2,256,128]{2,1,0:T(8,128)(2,1)S(1)} %copy-done.5, f32[2,16,128]{2,1,0:T(8,128)S(1)} %copy-done.6), custom_call_target="tpu_custom_call" | custom-call | tf_op jit(solution)/shard_map/rows_back/pallas_call | solution.py:266
Async XLA Ops:
  2.1 33.1 %all-to-all-start = ((f32[256,2,128]{2,1,0:T(2,128)}), f32[256,2,128]{2,1,0:T(2,128)S(1)}, u32[]{:S(2)}, u32[]{:S(2)}) async-start(f32[256,2,128]{2,1,0:T(2,128)} %bitcast.19), calls=%async_computation | async-start | bytes 524288 | tf_op jit(solution)/shard_map/all_to_all | solution.py:280
  35.3 2.4 %copy-start = (bf16[2,256,128]{2,1,0:T(8,128)(2,1)S(1)}, bf16[2,256,128]{2,1,0:T(8,128)(2,1)}, u32[]{:S(2)}) copy-start(bf16[2,256,128]{2,1,0:T(8,128)(2,1)} %constant.18.clone.forward) | copy-start | bytes 393220
  35.3 2.4 %copy-start.1 = (bf16[2,256,128]{2,1,0:T(8,128)(2,1)S(1)}, bf16[2,256,128]{2,1,0:T(8,128)(2,1)}, u32[]{:S(2)}) copy-start(bf16[2,256,128]{2,1,0:T(8,128)(2,1)} %constant.19.clone.right) | copy-start | bytes 393220
  35.3 2.4 %copy-start.2 = (bf16[2,128,256]{2,1,0:T(8,128)(2,1)S(1)}, bf16[2,128,256]{2,1,0:T(8,128)(2,1)}, u32[]{:S(2)}) copy-start(bf16[2,128,256]{2,1,0:T(8,128)(2,1)} %constant.20.clone.left) | copy-start | bytes 393220
  35.3 2.4 %copy-start.3 = (bf16[2,128,256]{2,1,0:T(8,128)(2,1)S(1)}, bf16[2,128,256]{2,1,0:T(8,128)(2,1)}, u32[]{:S(2)}) copy-start(bf16[2,128,256]{2,1,0:T(8,128)(2,1)} %constant.21.clone.back) | copy-start | bytes 393220
  35.4 2.3 %copy-start.4 = (f32[2,128,128]{2,1,0:T(8,128)S(1)}, f32[2,128,128]{2,1,0:T(8,128)}, u32[]{:S(2)}) copy-start(f32[2,128,128]{2,1,0:T(8,128)} %constant.22.clone.twist) | copy-start | bytes 393220
  59.1 2.9 %copy-start.5 = (bf16[2,256,128]{2,1,0:T(8,128)(2,1)S(1)}, bf16[2,256,128]{2,1,0:T(8,128)(2,1)}, u32[]{:S(2)}) copy-start(bf16[2,256,128]{2,1,0:T(8,128)(2,1)} %constant.23.clone.table) | copy-start | bytes 393220
  59.1 2.9 %copy-start.6 = (f32[2,16,128]{2,1,0:T(8,128)S(1)}, f32[2,16,128]{2,1,0:T(8,128)}, u32[]{:S(2)}) copy-start(f32[2,16,128]{2,1,0:T(8,128)} %constant.17.clone.twist) | copy-start | bytes 49156

commit v13 on v12

--- a/solution.py
+++ b/solution.py
@@ -23,22 +23,24 @@
 FLAT = DIST + PIX
 
 
-FIRST = (4, 2, 2)
-
-
-def far_first():
+FIRST_OUT = (5, 2, 2)
+FIRST_BACK = (4, 2, 2)
+
+
+def far_first(first):
     place = np.unravel_index(np.arange(LONG), PIX_SIZES)
-    z, x, h = [np.abs(p - f) for p, f in zip(place, FIRST)]
+    z, x, h = [np.abs(p - f) for p, f in zip(place, first)]
     hops = np.minimum(z, 8 - z) + np.minimum(x, 4 - x) + 2 * np.minimum(h, 4 - h)
-    hops[np.ravel_multi_index(FIRST, PIX_SIZES)] = 99
+    hops[np.ravel_multi_index(first, PIX_SIZES)] = 99
     return np.argsort(-hops, kind="stable")
 
 
-ORDER = far_first()
-
-
-def chip_groups():
-    return [[(2 * low + core) * LONG + int(k) for k in ORDER for low in range(2)] for core in range(2)]
+OUT_ORDER = far_first(FIRST_OUT)
+BACK_ORDER = far_first(FIRST_BACK)
+
+
+def chip_groups(order):
+    return [[(2 * low + core) * LONG + int(k) for k in order for low in range(2)] for core in range(2)]
 
 
 def angle_tables(left, right, period):
@@ -80,12 +82,12 @@
     return np.stack([high, np.asarray(x - high.astype(np.float64), jnp.bfloat16)])
 
 
-ROW_FORWARD = split_table(np.concatenate([COS, SIN], axis=1)[ORDER])
-COL_FORWARD = split_table(np.concatenate([COS[:, ORDER], SIN[:, ORDER]], axis=0))
+ROW_FORWARD = split_table(np.concatenate([COS, SIN], axis=1)[OUT_ORDER])
+COL_FORWARD = split_table(np.concatenate([COS[:, OUT_ORDER], SIN[:, OUT_ORDER]], axis=0))
 COL_RIGHT = split_table(np.concatenate([RIGHT, turn_lanes(RIGHT)], axis=0))
 COL_LEFT = split_table(np.concatenate([BACK, turn_after(BACK)], axis=1))
-COL_BACK = split_table(np.concatenate([COS, -SIN], axis=1)[ORDER])
-ROW_BACK = split_table(np.concatenate([COS[ORDER], -SIN[ORDER]], axis=0))
+COL_BACK = split_table(np.concatenate([COS, -SIN], axis=1)[BACK_ORDER])
+ROW_BACK = split_table(np.concatenate([COS[BACK_ORDER], -SIN[BACK_ORDER]], axis=0))
 ROW_TW = f32(np.stack(ROW_TWIST))
 COL_TW = f32(np.stack(COL_TWIST))
 
@@ -230,7 +232,7 @@
         out[pl.ds(d, LONG, stride=NDIST), :] = band
 
 
-def gain_kernel(par, out):
+def shares(par):
     first_col = SHORT * lax.axis_index(PIX) + WIDE * lax.axis_index(DIST)
     defocus = [par[d : d + 1, :1] for d in range(NDIST)]
     blurring = [par[d : d + 1, 1:] for d in range(NDIST)]
@@ -239,17 +241,16 @@
     for g in table[1:]:
         weight = weight + g * g
     share = 0.5 / (weight + REGULARIZER)
-    for d, g in enumerate(table):
-        out[d, :, :] = g * share
-
-
-def middle_kernel(gain, x, forward, right, left, back, twist, out):
+    return [g * share for g in table]
+
+
+def middle_kernel(par, x, forward, right, left, back, twist, out):
     core = lax.axis_index("c")
     blocks = []
     for d in range(NDIST):
         start = NDIST * LONG * (d % 2) + 2 * (d // 2) + core
         blocks.append(x[pl.ds(start, LONG, stride=NDIST), :])
-    y = column_middle(blocks, gain[...], forward[...], right[...], left[...], back[...], twist[...])
+    y = column_middle(blocks, shares(par), forward[...], right[...], left[...], back[...], twist[...])
     for low in range(2):
         out[pl.ds(low, LONG, stride=2), :] = y
 
@@ -275,9 +276,9 @@
     return run
 
 
-def exchange(x):
+def exchange(x, order):
     sent = x.reshape(2 * LONG, -1, LONG)
-    got = lax.all_to_all(sent, FLAT, 0, 0, axis_index_groups=chip_groups(), tiled=True)
+    got = lax.all_to_all(sent, FLAT, 0, 0, axis_index_groups=chip_groups(order), tiled=True)
     return lax.all_gather(got.reshape(x.shape), "c", axis=0, tiled=True)
 
 
@@ -285,12 +286,11 @@
     rows = NDIST * LONG
     (sent,) = call(first_kernel, ((rows, LONG),), "rows_forward", None)(contrast[0], ROW_FORWARD, ROW_TW)
     par = lax.all_gather(jnp.stack([defocus, blurring], axis=1), DIST, axis=0, tiled=True)
-    got = exchange(sent)
-    (gain,) = call(gain_kernel, ((NDIST, LONG, LONG),), "gains")(par)
+    got = exchange(sent, OUT_ORDER)
     (middle,) = call(middle_kernel, ((2 * LONG, LONG),), "columns")(
-        gain, got, COL_FORWARD, COL_RIGHT, COL_LEFT, COL_BACK, COL_TW
+        par, got, COL_FORWARD, COL_RIGHT, COL_LEFT, COL_BACK, COL_TW
     )
-    whole = exchange(middle)
+    whole = exchange(middle, BACK_ORDER)
     return call(last_kernel, ((2, SHORT, SIZE),), "rows_back")(whole, ROW_BACK, ROW_TW)[0]
 
 

time: 63.5 us -> 62.5 us (0.984)
  starting transfers between devices: 25.4 us -> 24.6 us
    all_to_all x1, starting transfers between devices: 25.4 us -> 24.6 us  [exchange(): lax.all_to_all(sent, FLAT, 0, 0, axis_index_groups=chip_groups(order), ti...]
    pallas_call x4 -> x3, Pallas kernels: 4.71 us -> 4.47 us  [run(): pl.pallas_call(kernel, out_shape=[jax.ShapeDtypeStruct(shape, jnp.float32...]
where the time goes in v13:
time: 62.5 us; the launch traced here: 62.2 us
  blocking collectives  31.7 us (51%)
  starting transfers between devices  24.6 us (39%)
  Pallas kernels  4.47 us (7%)
  between operations  1.36 us (2%)
    all_to_all x1, starting transfers between devices, exchange(): lax.all_to_all(sent, FLAT, 0, 0, axis_index_groups=chip_groups(order), ti...  24.6 us
    all_to_all x1, blocking collectives, exchange(): lax.all_to_all(sent, FLAT, 0, 0, axis_index_groups=chip_groups(order), ti...  20.1 us
    all_gather x1, blocking collectives, body(): lax.all_gather(jnp.stack([defocus, blurring], axis=1), DIST, axis=0, tile...  6.01 us
    all_gather x2, blocking collectives, exchange(): return lax.all_gather(got.reshape(x.shape), 'c', axis=0, tiled=True)  5.57 us
    pallas_call x3, Pallas kernels, run(): pl.pallas_call(kernel, out_shape=[jax.ShapeDtypeStruct(shape, jnp.float32...  4.47 us
  transfers between devices with their start and end apart: 1, of which 0 were waited for; matrix products, arithmetic and copies ran while one was open for 0% of the time, Pallas kernels for 0%

profile of v13, /device:TPU:1, one launch (start us, length us, event | category | flops | bytes accessed | tf_op | source)
XLA Modules:
  0.0 62.2 jit_solution(3503647018448793793)
XLA Ops:
  0.0 2.1 %rows_forward.1 = f32[512,128]{1,0:T(8,128)} custom-call(f32[2,16,2048]{2,1,0:T(8,128)} %bitcast.21, bf16[2,128,256]{2,1,0:T(8,128)(2,1)} %constant.16.clone.table, f32[2,16,128]{2,1,0:T(8,128)} %constant.17.clone.twist), custom_call_target="tpu_custom_call" | custom-call | tf_op jit(solution)/shard_map/rows_forward/pallas_call | solution.py:267
  2.1 24.6 %all-to-all-start = ((f32[256,2,128]{2,1,0:T(2,128)}), f32[256,2,128]{2,1,0:T(2,128)S(1)}, u32[]{:S(2)}, u32[]{:S(2)}) async-start(f32[256,2,128]{2,1,0:T(2,128)} %bitcast.19), calls=%async_computation | async-start | bytes 524288 | tf_op jit(solution)/shard_map/all_to_all | solution.py:281
  28.0 0.1 maximum_bitcast_fusion
  28.1 6.0 %all-gather.1 = f32[4,1,2]{2,1,0:T(1,128)S(1)} all-gather(f32[1,1,2]{2,1,0:T(1,128)S(1)} %maximum_bitcast_fusion), channel_id=1, replica_groups=mesh['l'=2,'c'=2,'z'=8,'x'=4,'h'=4] {'l','c'}, dimensions={0}, use_global_device_ids=true | all-gather | bytes 40 | tf_op jit(solution)/shard_map/all_gather | solution.py:288
  34.1 0.0 all-to-all-done
  34.1 0.0 copy-start
  34.1 0.0 copy-start.1
  34.1 0.0 copy-start.2
  34.1 0.0 copy-start.3
  34.1 0.0 copy-start.4
  34.2 2.3 %all_gather.10.x = f32[1024,128]{1,0:T(8,128)S(1)} all-gather(f32[512,128]{1,0:T(8,128)S(1)} %bitcast.18), channel_id=1, replica_groups=mesh['l'=2,'c'=2,'z'=8,'x'=4,'h'=4] {'c'}, dimensions={0}, use_global_device_ids=true | all-gather | bytes 786432 | tf_op jit(solution)/shard_map/all_gather | solution.py:282
  36.5 0.0 copy-done
  36.5 0.0 copy-done.1
  36.5 0.0 copy-done.2
  36.5 0.0 copy-done.3
  36.5 0.0 copy-done.4
  36.5 1.1 %columns.1 = f32[256,128]{1,0:T(8,128)S(1)} custom-call(f32[4,2]{1,0:T(4,128)S(1)} %bitcast.17, f32[1024,128]{1,0:T(8,128)S(1)} %all_gather.10.x, bf16[2,256,128]{2,1,0:T(8,128)(2,1)S(1)} %copy-done, bf16[2,256,128]{2,1,0:T(8,128)(2,1)S(1)} %copy-done.1, bf16[2,128,256]{2,1,0:T(8,128)(2,1)S(1)} %copy-done.2, bf16[2,128,256]{2,1,0:T(8,128)(2,1)S(1)} %copy-done.3, ...), custom_call_target="tpu_custom_call" | custom-call | tf_op jit(solution)/shard_map/columns/pallas_call | solution.py:267
  37.7 20.1 %all_to_all.10 = f32[256,1,128]{2,1,0:T(1,128)S(1)} all-to-all(f32[256,1,128]{2,1,0:T(1,128)S(1)} %bitcast.16), channel_id=1, replica_groups={{74,330,0,256,4,260,12,268,16,272,112,368,1,257,3,259,8,264,20,276,28,2..., dimensions={0} | all-to-all | bytes 262144 | tf_op jit(solution)/shard_map/all_to_all | solution.py:281
  57.8 0.0 copy-start.5
  57.8 0.0 copy-start.6
  57.8 3.3 %all-gather = f32[512,1,128]{2,0,1:T(8,128)S(1)} all-gather(f32[256,1,128]{2,0,1:T(8,128)S(1)} %bitcast.20), channel_id=2, replica_groups=mesh['l'=2,'c'=2,'z'=8,'x'=4,'h'=4] {'c'}, dimensions={0}, use_global_device_ids=true | all-gather | bytes 393216 | tf_op jit(solution)/shard_map/all_gather | solution.py:282
  61.0 0.0 copy-done.5
  61.0 0.0 copy-done.6
  61.0 1.2 %rows_back.1 = f32[2,16,2048]{2,1,0:T(8,128)} custom-call(f32[512,128]{1,0:T(8,128)S(1)} %bitcast.15, bf16[2,256,128]{2,1,0:T(8,128)(2,1)S(1)} %copy-done.5, f32[2,16,128]{2,1,0:T(8,128)S(1)} %copy-done.6), custom_call_target="tpu_custom_call" | custom-call | tf_op jit(solution)/shard_map/rows_back/pallas_call | solution.py:267
Async XLA Ops:
  2.1 32.0 %all-to-all-start = ((f32[256,2,128]{2,1,0:T(2,128)}), f32[256,2,128]{2,1,0:T(2,128)S(1)}, u32[]{:S(2)}, u32[]{:S(2)}) async-start(f32[256,2,128]{2,1,0:T(2,128)} %bitcast.19), calls=%async_computation | async-start | bytes 524288 | tf_op jit(solution)/shard_map/all_to_all | solution.py:281
  34.1 2.4 %copy-start = (bf16[2,256,128]{2,1,0:T(8,128)(2,1)S(1)}, bf16[2,256,128]{2,1,0:T(8,128)(2,1)}, u32[]{:S(2)}) copy-start(bf16[2,256,128]{2,1,0:T(8,128)(2,1)} %constant.18.clone.forward) | copy-start | bytes 393220
  34.1 2.4 %copy-start.1 = (bf16[2,256,128]{2,1,0:T(8,128)(2,1)S(1)}, bf16[2,256,128]{2,1,0:T(8,128)(2,1)}, u32[]{:S(2)}) copy-start(bf16[2,256,128]{2,1,0:T(8,128)(2,1)} %constant.19.clone.right) | copy-start | bytes 393220
  34.1 2.4 %copy-start.2 = (bf16[2,128,256]{2,1,0:T(8,128)(2,1)S(1)}, bf16[2,128,256]{2,1,0:T(8,128)(2,1)}, u32[]{:S(2)}) copy-start(bf16[2,128,256]{2,1,0:T(8,128)(2,1)} %constant.20.clone.left) | copy-start | bytes 393220
  34.1 2.4 %copy-start.3 = (bf16[2,128,256]{2,1,0:T(8,128)(2,1)S(1)}, bf16[2,128,256]{2,1,0:T(8,128)(2,1)}, u32[]{:S(2)}) copy-start(bf16[2,128,256]{2,1,0:T(8,128)(2,1)} %constant.21.clone.back) | copy-start | bytes 393220
  34.1 2.3 %copy-start.4 = (f32[2,128,128]{2,1,0:T(8,128)S(1)}, f32[2,128,128]{2,1,0:T(8,128)}, u32[]{:S(2)}) copy-start(f32[2,128,128]{2,1,0:T(8,128)} %constant.22.clone.twist) | copy-start | bytes 393220
  57.8 3.3 %copy-start.5 = (bf16[2,256,128]{2,1,0:T(8,128)(2,1)S(1)}, bf16[2,256,128]{2,1,0:T(8,128)(2,1)}, u32[]{:S(2)}) copy-start(bf16[2,256,128]{2,1,0:T(8,128)(2,1)} %constant.23.clone.table) | copy-start | bytes 393220
  57.8 3.3 %copy-start.6 = (f32[2,16,128]{2,1,0:T(8,128)S(1)}, f32[2,16,128]{2,1,0:T(8,128)}, u32[]{:S(2)}) copy-start(f32[2,16,128]{2,1,0:T(8,128)} %constant.17.clone.twist) | copy-start | bytes 49156

commit v14 on v13

--- a/solution.py
+++ b/solution.py
@@ -27,16 +27,16 @@
 FIRST_BACK = (4, 2, 2)
 
 
-def far_first(first):
+def by_hops(first, sign):
     place = np.unravel_index(np.arange(LONG), PIX_SIZES)
     z, x, h = [np.abs(p - f) for p, f in zip(place, first)]
     hops = np.minimum(z, 8 - z) + np.minimum(x, 4 - x) + 2 * np.minimum(h, 4 - h)
-    hops[np.ravel_multi_index(first, PIX_SIZES)] = 99
-    return np.argsort(-hops, kind="stable")
-
-
-OUT_ORDER = far_first(FIRST_OUT)
-BACK_ORDER = far_first(FIRST_BACK)
+    hops[np.ravel_multi_index(first, PIX_SIZES)] = -99 * sign
+    return np.argsort(sign * hops, kind="stable")
+
+
+OUT_ORDER = by_hops(FIRST_OUT, 1)
+BACK_ORDER = by_hops(FIRST_BACK, -1)
 
 
 def chip_groups(order):

time: 62.5 us -> 63.7 us (1.019)
  starting transfers between devices: 24.6 us -> 26.2 us
    all_to_all x1, starting transfers between devices: 24.6 us -> 26.2 us  [exchange(): lax.all_to_all(sent, FLAT, 0, 0, axis_index_groups=chip_groups(order), ti...]
where the time goes in v14:
time: 63.7 us; the launch traced here: 63.4 us
  blocking collectives  31.3 us (49%)
  starting transfers between devices  26.2 us (41%)
  Pallas kernels  4.47 us (7%)
  between operations  1.36 us (2%)
    all_to_all x1, starting transfers between devices, exchange(): lax.all_to_all(sent, FLAT, 0, 0, axis_index_groups=chip_groups(order), ti...  26.2 us
    all_to_all x1, blocking collectives, exchange(): lax.all_to_all(sent, FLAT, 0, 0, axis_index_groups=chip_groups(order), ti...  20 us
    all_gather x1, blocking collectives, body(): lax.all_gather(jnp.stack([defocus, blurring], axis=1), DIST, axis=0, tile...  5.92 us
    all_gather x2, blocking collectives, exchange(): return lax.all_gather(got.reshape(x.shape), 'c', axis=0, tiled=True)  5.3 us
    pallas_call x3, Pallas kernels, run(): pl.pallas_call(kernel, out_shape=[jax.ShapeDtypeStruct(shape, jnp.float32...  4.47 us
  transfers between devices with their start and end apart: 1, of which 0 were waited for; matrix products, arithmetic and copies ran while one was open for 0% of the time, Pallas kernels for 0%

profile of v14, /device:TPU:1, one launch (start us, length us, event | category | flops | bytes accessed | tf_op | source)
XLA Modules:
  0.0 63.4 jit_solution(10856462179855353109)
XLA Ops:
  0.0 2.1 %rows_forward.1 = f32[512,128]{1,0:T(8,128)} custom-call(f32[2,16,2048]{2,1,0:T(8,128)} %bitcast.21, bf16[2,128,256]{2,1,0:T(8,128)(2,1)} %constant.16.clone.table, f32[2,16,128]{2,1,0:T(8,128)} %constant.17.clone.twist), custom_call_target="tpu_custom_call" | custom-call | tf_op jit(solution)/shard_map/rows_forward/pallas_call | solution.py:267
  2.1 26.2 %all-to-all-start = ((f32[256,2,128]{2,1,0:T(2,128)}), f32[256,2,128]{2,1,0:T(2,128)S(1)}, u32[]{:S(2)}, u32[]{:S(2)}) async-start(f32[256,2,128]{2,1,0:T(2,128)} %bitcast.19), calls=%async_computation | async-start | bytes 524288 | tf_op jit(solution)/shard_map/all_to_all | solution.py:281
  29.7 0.1 maximum_bitcast_fusion
  29.8 5.9 %all-gather.1 = f32[4,1,2]{2,1,0:T(1,128)S(1)} all-gather(f32[1,1,2]{2,1,0:T(1,128)S(1)} %maximum_bitcast_fusion), channel_id=1, replica_groups=mesh['l'=2,'c'=2,'z'=8,'x'=4,'h'=4] {'l','c'}, dimensions={0}, use_global_device_ids=true | all-gather | bytes 40 | tf_op jit(solution)/shard_map/all_gather | solution.py:288
  35.7 0.0 all-to-all-done
  35.7 0.0 copy-start
  35.7 0.0 copy-start.1
  35.7 0.0 copy-start.2
  35.7 0.0 copy-start.3
  35.7 0.0 copy-start.4
  35.7 2.3 %all_gather.10.x = f32[1024,128]{1,0:T(8,128)S(1)} all-gather(f32[512,128]{1,0:T(8,128)S(1)} %bitcast.18), channel_id=1, replica_groups=mesh['l'=2,'c'=2,'z'=8,'x'=4,'h'=4] {'c'}, dimensions={0}, use_global_device_ids=true | all-gather | bytes 786432 | tf_op jit(solution)/shard_map/all_gather | solution.py:282
  38.0 0.0 copy-done
  38.0 0.0 copy-done.1
  38.0 0.0 copy-done.2
  38.0 0.0 copy-done.3
  38.1 0.0 copy-done.4
  38.1 1.1 %columns.1 = f32[256,128]{1,0:T(8,128)S(1)} custom-call(f32[4,2]{1,0:T(4,128)S(1)} %bitcast.17, f32[1024,128]{1,0:T(8,128)S(1)} %all_gather.10.x, bf16[2,256,128]{2,1,0:T(8,128)(2,1)S(1)} %copy-done, bf16[2,256,128]{2,1,0:T(8,128)(2,1)S(1)} %copy-done.1, bf16[2,128,256]{2,1,0:T(8,128)(2,1)S(1)} %copy-done.2, bf16[2,128,256]{2,1,0:T(8,128)(2,1)S(1)} %copy-done.3, ...), custom_call_target="tpu_custom_call" | custom-call | tf_op jit(solution)/shard_map/columns/pallas_call | solution.py:267
  39.2 20.0 %all_to_all.10 = f32[256,1,128]{2,1,0:T(1,128)S(1)} all-to-all(f32[256,1,128]{2,1,0:T(1,128)S(1)} %bitcast.16), channel_id=1, replica_groups={{74,330,0,256,4,260,12,268,16,272,112,368,1,257,3,259,8,264,20,276,28,2..., dimensions={0} | all-to-all | bytes 262144 | tf_op jit(solution)/shard_map/all_to_all | solution.py:281
  59.3 0.0 copy-start.5
  59.3 0.0 copy-start.6
  59.3 3.0 %all-gather = f32[512,1,128]{2,0,1:T(8,128)S(1)} all-gather(f32[256,1,128]{2,0,1:T(8,128)S(1)} %bitcast.20), channel_id=2, replica_groups=mesh['l'=2,'c'=2,'z'=8,'x'=4,'h'=4] {'c'}, dimensions={0}, use_global_device_ids=true | all-gather | bytes 393216 | tf_op jit(solution)/shard_map/all_gather | solution.py:282
  62.2 0.0 copy-done.5
  62.3 0.0 copy-done.6
  62.3 1.2 %rows_back.1 = f32[2,16,2048]{2,1,0:T(8,128)} custom-call(f32[512,128]{1,0:T(8,128)S(1)} %bitcast.15, bf16[2,256,128]{2,1,0:T(8,128)(2,1)S(1)} %copy-done.5, f32[2,16,128]{2,1,0:T(8,128)S(1)} %copy-done.6), custom_call_target="tpu_custom_call" | custom-call | tf_op jit(solution)/shard_map/rows_back/pallas_call | solution.py:267
Async XLA Ops:
  2.1 33.5 %all-to-all-start = ((f32[256,2,128]{2,1,0:T(2,128)}), f32[256,2,128]{2,1,0:T(2,128)S(1)}, u32[]{:S(2)}, u32[]{:S(2)}) async-start(f32[256,2,128]{2,1,0:T(2,128)} %bitcast.19), calls=%async_computation | async-start | bytes 524288 | tf_op jit(solution)/shard_map/all_to_all | solution.py:281
  35.7 2.4 %copy-start = (bf16[2,256,128]{2,1,0:T(8,128)(2,1)S(1)}, bf16[2,256,128]{2,1,0:T(8,128)(2,1)}, u32[]{:S(2)}) copy-start(bf16[2,256,128]{2,1,0:T(8,128)(2,1)} %constant.18.clone.forward) | copy-start | bytes 393220
  35.7 2.4 %copy-start.1 = (bf16[2,256,128]{2,1,0:T(8,128)(2,1)S(1)}, bf16[2,256,128]{2,1,0:T(8,128)(2,1)}, u32[]{:S(2)}) copy-start(bf16[2,256,128]{2,1,0:T(8,128)(2,1)} %constant.19.clone.right) | copy-start | bytes 393220
  35.7 2.4 %copy-start.2 = (bf16[2,128,256]{2,1,0:T(8,128)(2,1)S(1)}, bf16[2,128,256]{2,1,0:T(8,128)(2,1)}, u32[]{:S(2)}) copy-start(bf16[2,128,256]{2,1,0:T(8,128)(2,1)} %constant.20.clone.left) | copy-start | bytes 393220
  35.7 2.4 %copy-start.3 = (bf16[2,128,256]{2,1,0:T(8,128)(2,1)S(1)}, bf16[2,128,256]{2,1,0:T(8,128)(2,1)}, u32[]{:S(2)}) copy-start(bf16[2,128,256]{2,1,0:T(8,128)(2,1)} %constant.21.clone.back) | copy-start | bytes 393220
  35.7 2.3 %copy-start.4 = (f32[2,128,128]{2,1,0:T(8,128)S(1)}, f32[2,128,128]{2,1,0:T(8,128)}, u32[]{:S(2)}) copy-start(f32[2,128,128]{2,1,0:T(8,128)} %constant.22.clone.twist) | copy-start | bytes 393220
  59.3 3.0 %copy-start.5 = (bf16[2,256,128]{2,1,0:T(8,128)(2,1)S(1)}, bf16[2,256,128]{2,1,0:T(8,128)(2,1)}, u32[]{:S(2)}) copy-start(bf16[2,256,128]{2,1,0:T(8,128)(2,1)} %constant.23.clone.table) | copy-start | bytes 393220
  59.3 3.0 %copy-start.6 = (f32[2,16,128]{2,1,0:T(8,128)S(1)}, f32[2,16,128]{2,1,0:T(8,128)}, u32[]{:S(2)}) copy-start(f32[2,16,128]{2,1,0:T(8,128)} %constant.17.clone.twist) | copy-start | bytes 49156

commit v15 on v13

--- a/solution.py
+++ b/solution.py
@@ -102,12 +102,11 @@
 
 
 def product(a, b, a_dim=1, b_dim=0):
-    def one(x, y):
-        return lax.dot_general(
-            x, y, (((a_dim,), (b_dim,)), ((), ())), preferred_element_type=jnp.float32
-        )
-
-    return one(a[0], b[0]) + (one(a[0], b[1]) + one(a[1], b[0]))
+    left = jnp.concatenate([a[0], a[0], a[1]], axis=a_dim)
+    right = jnp.concatenate([b[0], b[1], b[0]], axis=b_dim)
+    return lax.dot_general(
+        left, right, (((a_dim,), (b_dim,)), ((), ())), preferred_element_type=jnp.float32
+    )
 
 
 def four_point(z, sign):

time: 62.5 us -> 62.4 us (level)
  no operation moved by 1% of the time
where the time goes in v15:
time: 62.4 us; the launch traced here: 62.2 us
  blocking collectives  31.7 us (51%)
  starting transfers between devices  24.6 us (39%)
  Pallas kernels  4.41 us (7%)
  between operations  1.36 us (2%)
    all_to_all x1, starting transfers between devices, exchange(): lax.all_to_all(sent, FLAT, 0, 0, axis_index_groups=chip_groups(order), ti...  24.6 us
    all_to_all x1, blocking collectives, exchange(): lax.all_to_all(sent, FLAT, 0, 0, axis_index_groups=chip_groups(order), ti...  20.1 us
    all_gather x1, blocking collectives, body(): lax.all_gather(jnp.stack([defocus, blurring], axis=1), DIST, axis=0, tile...  6.01 us
    all_gather x2, blocking collectives, exchange(): return lax.all_gather(got.reshape(x.shape), 'c', axis=0, tiled=True)  5.57 us
    pallas_call x3, Pallas kernels, run(): pl.pallas_call(kernel, out_shape=[jax.ShapeDtypeStruct(shape, jnp.float32...  4.41 us
  transfers between devices with their start and end apart: 1, of which 0 were waited for; matrix products, arithmetic and copies ran while one was open for 0% of the time, Pallas kernels for 0%

profile of v15, /device:TPU:1, one launch (start us, length us, event | category | flops | bytes accessed | tf_op | source)
XLA Modules:
  0.0 62.2 jit_solution(8302729446859325890)
XLA Ops:
  0.0 2.1 %rows_forward.1 = f32[512,128]{1,0:T(8,128)} custom-call(f32[2,16,2048]{2,1,0:T(8,128)} %bitcast.21, bf16[2,128,256]{2,1,0:T(8,128)(2,1)} %constant.16.clone.table, f32[2,16,128]{2,1,0:T(8,128)} %constant.17.clone.twist), custom_call_target="tpu_custom_call" | custom-call | tf_op jit(solution)/shard_map/rows_forward/pallas_call | solution.py:266
  2.1 24.6 %all-to-all-start = ((f32[256,2,128]{2,1,0:T(2,128)}), f32[256,2,128]{2,1,0:T(2,128)S(1)}, u32[]{:S(2)}, u32[]{:S(2)}) async-start(f32[256,2,128]{2,1,0:T(2,128)} %bitcast.19), calls=%async_computation | async-start | bytes 524288 | tf_op jit(solution)/shard_map/all_to_all | solution.py:280
  28.0 0.1 maximum_bitcast_fusion
  28.1 6.0 %all-gather.1 = f32[4,1,2]{2,1,0:T(1,128)S(1)} all-gather(f32[1,1,2]{2,1,0:T(1,128)S(1)} %maximum_bitcast_fusion), channel_id=1, replica_groups=mesh['l'=2,'c'=2,'z'=8,'x'=4,'h'=4] {'l','c'}, dimensions={0}, use_global_device_ids=true | all-gather | bytes 40 | tf_op jit(solution)/shard_map/all_gather | solution.py:287
  34.1 0.0 all-to-all-done
  34.1 0.0 copy-start
  34.1 0.0 copy-start.1
  34.1 0.0 copy-start.2
  34.1 0.0 copy-start.3
  34.1 0.0 copy-start.4
  34.2 2.3 %all_gather.10.x = f32[1024,128]{1,0:T(8,128)S(1)} all-gather(f32[512,128]{1,0:T(8,128)S(1)} %bitcast.18), channel_id=1, replica_groups=mesh['l'=2,'c'=2,'z'=8,'x'=4,'h'=4] {'c'}, dimensions={0}, use_global_device_ids=true | all-gather | bytes 786432 | tf_op jit(solution)/shard_map/all_gather | solution.py:281
  36.5 0.0 copy-done
  36.5 0.0 copy-done.1
  36.5 0.0 copy-done.2
  36.5 0.0 copy-done.3
  36.5 0.0 copy-done.4
  36.5 1.1 %columns.1 = f32[256,128]{1,0:T(8,128)S(1)} custom-call(f32[4,2]{1,0:T(4,128)S(1)} %bitcast.17, f32[1024,128]{1,0:T(8,128)S(1)} %all_gather.10.x, bf16[2,256,128]{2,1,0:T(8,128)(2,1)S(1)} %copy-done, bf16[2,256,128]{2,1,0:T(8,128)(2,1)S(1)} %copy-done.1, bf16[2,128,256]{2,1,0:T(8,128)(2,1)S(1)} %copy-done.2, bf16[2,128,256]{2,1,0:T(8,128)(2,1)S(1)} %copy-done.3, ...), custom_call_target="tpu_custom_call" | custom-call | tf_op jit(solution)/shard_map/columns/pallas_call | solution.py:266
  37.6 20.1 %all_to_all.10 = f32[256,1,128]{2,1,0:T(1,128)S(1)} all-to-all(f32[256,1,128]{2,1,0:T(1,128)S(1)} %bitcast.16), channel_id=1, replica_groups={{74,330,0,256,4,260,12,268,16,272,112,368,1,257,3,259,8,264,20,276,28,2..., dimensions={0} | all-to-all | bytes 262144 | tf_op jit(solution)/shard_map/all_to_all | solution.py:280
  57.7 0.0 copy-start.5
  57.7 0.0 copy-start.6
  57.7 3.3 %all-gather = f32[512,1,128]{2,0,1:T(8,128)S(1)} all-gather(f32[256,1,128]{2,0,1:T(8,128)S(1)} %bitcast.20), channel_id=2, replica_groups=mesh['l'=2,'c'=2,'z'=8,'x'=4,'h'=4] {'c'}, dimensions={0}, use_global_device_ids=true | all-gather | bytes 393216 | tf_op jit(solution)/shard_map/all_gather | solution.py:281
  61.0 0.0 copy-done.5
  61.0 0.0 copy-done.6
  61.0 1.2 %rows_back.1 = f32[2,16,2048]{2,1,0:T(8,128)} custom-call(f32[512,128]{1,0:T(8,128)S(1)} %bitcast.15, bf16[2,256,128]{2,1,0:T(8,128)(2,1)S(1)} %copy-done.5, f32[2,16,128]{2,1,0:T(8,128)S(1)} %copy-done.6), custom_call_target="tpu_custom_call" | custom-call | tf_op jit(solution)/shard_map/rows_back/pallas_call | solution.py:266
Async XLA Ops:
  2.1 32.0 %all-to-all-start = ((f32[256,2,128]{2,1,0:T(2,128)}), f32[256,2,128]{2,1,0:T(2,128)S(1)}, u32[]{:S(2)}, u32[]{:S(2)}) async-start(f32[256,2,128]{2,1,0:T(2,128)} %bitcast.19), calls=%async_computation | async-start | bytes 524288 | tf_op jit(solution)/shard_map/all_to_all | solution.py:280
  34.1 2.4 %copy-start = (bf16[2,256,128]{2,1,0:T(8,128)(2,1)S(1)}, bf16[2,256,128]{2,1,0:T(8,128)(2,1)}, u32[]{:S(2)}) copy-start(bf16[2,256,128]{2,1,0:T(8,128)(2,1)} %constant.18.clone.forward) | copy-start | bytes 393220
  34.1 2.4 %copy-start.1 = (bf16[2,256,128]{2,1,0:T(8,128)(2,1)S(1)}, bf16[2,256,128]{2,1,0:T(8,128)(2,1)}, u32[]{:S(2)}) copy-start(bf16[2,256,128]{2,1,0:T(8,128)(2,1)} %constant.19.clone.right) | copy-start | bytes 393220
  34.1 2.4 %copy-start.2 = (bf16[2,128,256]{2,1,0:T(8,128)(2,1)S(1)}, bf16[2,128,256]{2,1,0:T(8,128)(2,1)}, u32[]{:S(2)}) copy-start(bf16[2,128,256]{2,1,0:T(8,128)(2,1)} %constant.20.clone.left) | copy-start | bytes 393220
  34.1 2.4 %copy-start.3 = (bf16[2,128,256]{2,1,0:T(8,128)(2,1)S(1)}, bf16[2,128,256]{2,1,0:T(8,128)(2,1)}, u32[]{:S(2)}) copy-start(bf16[2,128,256]{2,1,0:T(8,128)(2,1)} %constant.21.clone.back) | copy-start | bytes 393220
  34.1 2.3 %copy-start.4 = (f32[2,128,128]{2,1,0:T(8,128)S(1)}, f32[2,128,128]{2,1,0:T(8,128)}, u32[]{:S(2)}) copy-start(f32[2,128,128]{2,1,0:T(8,128)} %constant.22.clone.twist) | copy-start | bytes 393220
  57.7 3.3 %copy-start.5 = (bf16[2,256,128]{2,1,0:T(8,128)(2,1)S(1)}, bf16[2,256,128]{2,1,0:T(8,128)(2,1)}, u32[]{:S(2)}) copy-start(bf16[2,256,128]{2,1,0:T(8,128)(2,1)} %constant.23.clone.table) | copy-start | bytes 393220
  57.7 3.3 %copy-start.6 = (f32[2,16,128]{2,1,0:T(8,128)S(1)}, f32[2,16,128]{2,1,0:T(8,128)}, u32[]{:S(2)}) copy-start(f32[2,16,128]{2,1,0:T(8,128)} %constant.17.clone.twist) | copy-start | bytes 49156

commit v16 on v15

--- a/solution.py
+++ b/solution.py
@@ -23,7 +23,7 @@
 FLAT = DIST + PIX
 
 
-FIRST_OUT = (5, 2, 2)
+FIRST_OUT = (6, 2, 2)
 FIRST_BACK = (4, 2, 2)
 
 

time: 62.4 us -> 63.3 us (1.014)
  blocking collectives: 31.7 us -> 32.5 us
    all_gather x2, blocking collectives: 5.57 us -> 6.58 us  [exchange(): return lax.all_gather(got.reshape(x.shape), 'c', axis=0, tiled=True)]
where the time goes in v16:
time: 63.3 us; the launch traced here: 63 us
  blocking collectives  32.5 us (51%)
  starting transfers between devices  24.7 us (39%)
  Pallas kernels  4.41 us (7%)
  between operations  1.35 us (2%)
    all_to_all x1, starting transfers between devices, exchange(): lax.all_to_all(sent, FLAT, 0, 0, axis_index_groups=chip_groups(order), ti...  24.7 us
    all_to_all x1, blocking collectives, exchange(): lax.all_to_all(sent, FLAT, 0, 0, axis_index_groups=chip_groups(order), ti...  20 us
    all_gather x2, blocking collectives, exchange(): return lax.all_gather(got.reshape(x.shape), 'c', axis=0, tiled=True)  6.58 us
    all_gather x1, blocking collectives, body(): lax.all_gather(jnp.stack([defocus, blurring], axis=1), DIST, axis=0, tile...  5.84 us
    pallas_call x3, Pallas kernels, run(): pl.pallas_call(kernel, out_shape=[jax.ShapeDtypeStruct(shape, jnp.float32...  4.41 us
  transfers between devices with their start and end apart: 1, of which 0 were waited for; matrix products, arithmetic and copies ran while one was open for 0% of the time, Pallas kernels for 0%

profile of v16, /device:TPU:1, one launch (start us, length us, event | category | flops | bytes accessed | tf_op | source)
XLA Modules:
  0.0 63.0 jit_solution(10989184711548378317)
XLA Ops:
  0.0 2.1 %rows_forward.1 = f32[512,128]{1,0:T(8,128)} custom-call(f32[2,16,2048]{2,1,0:T(8,128)} %bitcast.21, bf16[2,128,256]{2,1,0:T(8,128)(2,1)} %constant.16.clone.table, f32[2,16,128]{2,1,0:T(8,128)} %constant.17.clone.twist), custom_call_target="tpu_custom_call" | custom-call | tf_op jit(solution)/shard_map/rows_forward/pallas_call | solution.py:266
  2.1 24.7 %all-to-all-start = ((f32[256,2,128]{2,1,0:T(2,128)}), f32[256,2,128]{2,1,0:T(2,128)S(1)}, u32[]{:S(2)}, u32[]{:S(2)}) async-start(f32[256,2,128]{2,1,0:T(2,128)} %bitcast.19), calls=%async_computation | async-start | bytes 524288 | tf_op jit(solution)/shard_map/all_to_all | solution.py:280
  28.1 0.1 maximum_bitcast_fusion
  28.2 5.8 %all-gather.1 = f32[4,1,2]{2,1,0:T(1,128)S(1)} all-gather(f32[1,1,2]{2,1,0:T(1,128)S(1)} %maximum_bitcast_fusion), channel_id=1, replica_groups=mesh['l'=2,'c'=2,'z'=8,'x'=4,'h'=4] {'l','c'}, dimensions={0}, use_global_device_ids=true | all-gather | bytes 40 | tf_op jit(solution)/shard_map/all_gather | solution.py:287
  34.0 0.0 all-to-all-done
  34.0 0.0 copy-start
  34.0 0.0 copy-start.1
  34.0 0.0 copy-start.2
  34.0 0.0 copy-start.3
  34.0 0.0 copy-start.4
  34.1 3.3 %all_gather.10.x = f32[1024,128]{1,0:T(8,128)S(1)} all-gather(f32[512,128]{1,0:T(8,128)S(1)} %bitcast.18), channel_id=1, replica_groups=mesh['l'=2,'c'=2,'z'=8,'x'=4,'h'=4] {'c'}, dimensions={0}, use_global_device_ids=true | all-gather | bytes 786432 | tf_op jit(solution)/shard_map/all_gather | solution.py:281
  37.4 0.0 copy-done
  37.4 0.0 copy-done.1
  37.4 0.0 copy-done.2
  37.4 0.0 copy-done.3
  37.4 0.0 copy-done.4
  37.4 1.1 %columns.1 = f32[256,128]{1,0:T(8,128)S(1)} custom-call(f32[4,2]{1,0:T(4,128)S(1)} %bitcast.17, f32[1024,128]{1,0:T(8,128)S(1)} %all_gather.10.x, bf16[2,256,128]{2,1,0:T(8,128)(2,1)S(1)} %copy-done, bf16[2,256,128]{2,1,0:T(8,128)(2,1)S(1)} %copy-done.1, bf16[2,128,256]{2,1,0:T(8,128)(2,1)S(1)} %copy-done.2, bf16[2,128,256]{2,1,0:T(8,128)(2,1)S(1)} %copy-done.3, ...), custom_call_target="tpu_custom_call" | custom-call | tf_op jit(solution)/shard_map/columns/pallas_call | solution.py:266
  38.5 20.0 %all_to_all.10 = f32[256,1,128]{2,1,0:T(1,128)S(1)} all-to-all(f32[256,1,128]{2,1,0:T(1,128)S(1)} %bitcast.16), channel_id=1, replica_groups={{74,330,0,256,4,260,12,268,16,272,112,368,1,257,3,259,8,264,20,276,28,2..., dimensions={0} | all-to-all | bytes 262144 | tf_op jit(solution)/shard_map/all_to_all | solution.py:280
  58.5 0.0 copy-start.5
  58.5 0.0 copy-start.6
  58.5 3.2 %all-gather = f32[512,1,128]{2,0,1:T(8,128)S(1)} all-gather(f32[256,1,128]{2,0,1:T(8,128)S(1)} %bitcast.20), channel_id=2, replica_groups=mesh['l'=2,'c'=2,'z'=8,'x'=4,'h'=4] {'c'}, dimensions={0}, use_global_device_ids=true | all-gather | bytes 393216 | tf_op jit(solution)/shard_map/all_gather | solution.py:281
  61.8 0.0 copy-done.5
  61.8 0.0 copy-done.6
  61.8 1.2 %rows_back.1 = f32[2,16,2048]{2,1,0:T(8,128)} custom-call(f32[512,128]{1,0:T(8,128)S(1)} %bitcast.15, bf16[2,256,128]{2,1,0:T(8,128)(2,1)S(1)} %copy-done.5, f32[2,16,128]{2,1,0:T(8,128)S(1)} %copy-done.6), custom_call_target="tpu_custom_call" | custom-call | tf_op jit(solution)/shard_map/rows_back/pallas_call | solution.py:266
Async XLA Ops:
  2.1 31.9 %all-to-all-start = ((f32[256,2,128]{2,1,0:T(2,128)}), f32[256,2,128]{2,1,0:T(2,128)S(1)}, u32[]{:S(2)}, u32[]{:S(2)}) async-start(f32[256,2,128]{2,1,0:T(2,128)} %bitcast.19), calls=%async_computation | async-start | bytes 524288 | tf_op jit(solution)/shard_map/all_to_all | solution.py:280
  34.0 3.4 %copy-start = (bf16[2,256,128]{2,1,0:T(8,128)(2,1)S(1)}, bf16[2,256,128]{2,1,0:T(8,128)(2,1)}, u32[]{:S(2)}) copy-start(bf16[2,256,128]{2,1,0:T(8,128)(2,1)} %constant.18.clone.forward) | copy-start | bytes 393220
  34.0 3.4 %copy-start.1 = (bf16[2,256,128]{2,1,0:T(8,128)(2,1)S(1)}, bf16[2,256,128]{2,1,0:T(8,128)(2,1)}, u32[]{:S(2)}) copy-start(bf16[2,256,128]{2,1,0:T(8,128)(2,1)} %constant.19.clone.right) | copy-start | bytes 393220
  34.0 3.4 %copy-start.2 = (bf16[2,128,256]{2,1,0:T(8,128)(2,1)S(1)}, bf16[2,128,256]{2,1,0:T(8,128)(2,1)}, u32[]{:S(2)}) copy-start(bf16[2,128,256]{2,1,0:T(8,128)(2,1)} %constant.20.clone.left) | copy-start | bytes 393220
  34.0 3.4 %copy-start.3 = (bf16[2,128,256]{2,1,0:T(8,128)(2,1)S(1)}, bf16[2,128,256]{2,1,0:T(8,128)(2,1)}, u32[]{:S(2)}) copy-start(bf16[2,128,256]{2,1,0:T(8,128)(2,1)} %constant.21.clone.back) | copy-start | bytes 393220
  34.0 3.4 %copy-start.4 = (f32[2,128,128]{2,1,0:T(8,128)S(1)}, f32[2,128,128]{2,1,0:T(8,128)}, u32[]{:S(2)}) copy-start(f32[2,128,128]{2,1,0:T(8,128)} %constant.22.clone.twist) | copy-start | bytes 393220
  58.5 3.3 %copy-start.5 = (bf16[2,256,128]{2,1,0:T(8,128)(2,1)S(1)}, bf16[2,256,128]{2,1,0:T(8,128)(2,1)}, u32[]{:S(2)}) copy-start(bf16[2,256,128]{2,1,0:T(8,128)(2,1)} %constant.23.clone.table) | copy-start | bytes 393220
  58.5 3.3 %copy-start.6 = (f32[2,16,128]{2,1,0:T(8,128)S(1)}, f32[2,16,128]{2,1,0:T(8,128)}, u32[]{:S(2)}) copy-start(f32[2,16,128]{2,1,0:T(8,128)} %constant.17.clone.twist) | copy-start | bytes 49156

commit v17 on v15

--- a/solution.py
+++ b/solution.py
@@ -39,8 +39,12 @@
 BACK_ORDER = far_first(FIRST_BACK)
 
 
-def chip_groups(order):
-    return [[(2 * low + core) * LONG + int(k) for k in order for low in range(2)] for core in range(2)]
+def out_groups():
+    return [[(2 * low + core) * LONG + int(k) for k in OUT_ORDER for low in range(2)] for core in range(2)]
+
+
+def back_groups():
+    return [[(2 * low + core) * LONG + int(k) for low in range(2) for k in BACK_ORDER] for core in range(2)]
 
 
 def angle_tables(left, right, period):
@@ -251,11 +255,12 @@
         blocks.append(x[pl.ds(start, LONG, stride=NDIST), :])
     y = column_middle(blocks, shares(par), forward[...], right[...], left[...], back[...], twist[...])
     for low in range(2):
-        out[pl.ds(low, LONG, stride=2), :] = y
+        out[LONG * low : LONG * (low + 1), :] = y
 
 
 def last_kernel(x, table, twist, out):
-    blocks = [x[pl.ds(2 * LONG * (d % 2) + d // 2, LONG, stride=2), :] for d in range(NDIST)]
+    starts = [LONG * (2 * (d % 2) + d // 2) for d in range(NDIST)]
+    blocks = [x[start : start + LONG, :] for start in starts]
     for j, (r, i) in enumerate(row_back(blocks, table[...], twist[...])):
         out[0, :, LONG * j : LONG * (j + 1)] = r
         out[1, :, LONG * j : LONG * (j + 1)] = i
@@ -275,9 +280,9 @@
     return run
 
 
-def exchange(x, order):
+def exchange(x, groups):
     sent = x.reshape(2 * LONG, -1, LONG)
-    got = lax.all_to_all(sent, FLAT, 0, 0, axis_index_groups=chip_groups(order), tiled=True)
+    got = lax.all_to_all(sent, FLAT, 0, 0, axis_index_groups=groups, tiled=True)
     return lax.all_gather(got.reshape(x.shape), "c", axis=0, tiled=True)
 
 
@@ -285,11 +290,11 @@
     rows = NDIST * LONG
     (sent,) = call(first_kernel, ((rows, LONG),), "rows_forward", None)(contrast[0], ROW_FORWARD, ROW_TW)
     par = lax.all_gather(jnp.stack([defocus, blurring], axis=1), DIST, axis=0, tiled=True)
-    got = exchange(sent, OUT_ORDER)
+    got = exchange(sent, out_groups())
     (middle,) = call(middle_kernel, ((2 * LONG, LONG),), "columns")(
         par, got, COL_FORWARD, COL_RIGHT, COL_LEFT, COL_BACK, COL_TW
     )
-    whole = exchange(middle, BACK_ORDER)
+    whole = exchange(middle, back_groups())
     return call(last_kernel, ((2, SHORT, SIZE),), "rows_back")(whole, ROW_BACK, ROW_TW)[0]
 
 

time: 62.4 us -> 62.4 us (level)
  no operation moved by 1% of the time
where the time goes in v17:
time: 62.4 us; the launch traced here: 62.1 us
  blocking collectives  31.6 us (51%)
  starting transfers between devices  24.6 us (39%)
  Pallas kernels  4.41 us (7%)
  between operations  1.36 us (2%)
    all_to_all x1, starting transfers between devices, exchange(): got = lax.all_to_all(sent, FLAT, 0, 0, axis_index_groups=groups, tiled=True)  24.6 us
    all_to_all x1, blocking collectives, exchange(): got = lax.all_to_all(sent, FLAT, 0, 0, axis_index_groups=groups, tiled=True)  20 us
    all_gather x1, blocking collectives, body(): lax.all_gather(jnp.stack([defocus, blurring], axis=1), DIST, axis=0, tile...  6.01 us
    all_gather x2, blocking collectives, exchange(): return lax.all_gather(got.reshape(x.shape), 'c', axis=0, tiled=True)  5.61 us
    pallas_call x3, Pallas kernels, run(): pl.pallas_call(kernel, out_shape=[jax.ShapeDtypeStruct(shape, jnp.float32...  4.41 us
  transfers between devices with their start and end apart: 1, of which 0 were waited for; matrix products, arithmetic and copies ran while one was open for 0% of the time, Pallas kernels for 0%

profile of v17, /device:TPU:1, one launch (start us, length us, event | category | flops | bytes accessed | tf_op | source)
XLA Modules:
  0.0 62.1 jit_solution(13515109708593560239)
XLA Ops:
  0.0 2.1 %rows_forward.1 = f32[512,128]{1,0:T(8,128)} custom-call(f32[2,16,2048]{2,1,0:T(8,128)} %bitcast.21, bf16[2,128,256]{2,1,0:T(8,128)(2,1)} %constant.16.clone.table, f32[2,16,128]{2,1,0:T(8,128)} %constant.17.clone.twist), custom_call_target="tpu_custom_call" | custom-call | tf_op jit(solution)/shard_map/rows_forward/pallas_call | solution.py:271
  2.1 24.6 %all-to-all-start = ((f32[256,2,128]{2,1,0:T(2,128)}), f32[256,2,128]{2,1,0:T(2,128)S(1)}, u32[]{:S(2)}, u32[]{:S(2)}) async-start(f32[256,2,128]{2,1,0:T(2,128)} %bitcast.19), calls=%async_computation | async-start | bytes 524288 | tf_op jit(solution)/shard_map/all_to_all | solution.py:285
  28.0 0.1 maximum_bitcast_fusion
  28.1 6.0 %all-gather.1 = f32[4,1,2]{2,1,0:T(1,128)S(1)} all-gather(f32[1,1,2]{2,1,0:T(1,128)S(1)} %maximum_bitcast_fusion), channel_id=1, replica_groups=mesh['l'=2,'c'=2,'z'=8,'x'=4,'h'=4] {'l','c'}, dimensions={0}, use_global_device_ids=true | all-gather | bytes 40 | tf_op jit(solution)/shard_map/all_gather | solution.py:292
  34.1 0.0 all-to-all-done
  34.1 0.0 copy-start
  34.1 0.0 copy-start.1
  34.1 0.0 copy-start.2
  34.1 0.0 copy-start.3
  34.1 0.0 copy-start.4
  34.2 2.3 %all_gather.10.x = f32[1024,128]{1,0:T(8,128)S(1)} all-gather(f32[512,128]{1,0:T(8,128)S(1)} %bitcast.18), channel_id=1, replica_groups=mesh['l'=2,'c'=2,'z'=8,'x'=4,'h'=4] {'c'}, dimensions={0}, use_global_device_ids=true | all-gather | bytes 786432 | tf_op jit(solution)/shard_map/all_gather | solution.py:286
  36.5 0.0 copy-done
  36.5 0.0 copy-done.1
  36.5 0.0 copy-done.2
  36.5 0.0 copy-done.3
  36.5 0.0 copy-done.4
  36.5 1.1 %columns.1 = f32[256,128]{1,0:T(8,128)S(1)} custom-call(f32[4,2]{1,0:T(4,128)S(1)} %bitcast.17, f32[1024,128]{1,0:T(8,128)S(1)} %all_gather.10.x, bf16[2,256,128]{2,1,0:T(8,128)(2,1)S(1)} %copy-done, bf16[2,256,128]{2,1,0:T(8,128)(2,1)S(1)} %copy-done.1, bf16[2,128,256]{2,1,0:T(8,128)(2,1)S(1)} %copy-done.2, bf16[2,128,256]{2,1,0:T(8,128)(2,1)S(1)} %copy-done.3, ...), custom_call_target="tpu_custom_call" | custom-call | tf_op jit(solution)/shard_map/columns/pallas_call | solution.py:271
  37.6 20.0 %all_to_all.10 = f32[256,1,128]{2,1,0:T(1,128)S(1)} all-to-all(f32[256,1,128]{2,1,0:T(1,128)S(1)} %bitcast.16), channel_id=1, replica_groups={{74,0,4,12,16,112,1,3,8,20,28,32,96,116,124,5,7,13,15,17,19,24,36,44,48..., dimensions={0} | all-to-all | bytes 262144 | tf_op jit(solution)/shard_map/all_to_all | solution.py:285
  57.6 0.0 copy-start.5
  57.6 0.0 copy-start.6
  57.6 3.3 %all-gather = f32[512,1,128]{2,0,1:T(8,128)S(1)} all-gather(f32[256,1,128]{2,0,1:T(8,128)S(1)} %bitcast.20), channel_id=2, replica_groups=mesh['l'=2,'c'=2,'z'=8,'x'=4,'h'=4] {'c'}, dimensions={0}, use_global_device_ids=true | all-gather | bytes 393216 | tf_op jit(solution)/shard_map/all_gather | solution.py:286
  60.9 0.0 copy-done.5
  60.9 0.0 copy-done.6
  60.9 1.2 %rows_back.1 = f32[2,16,2048]{2,1,0:T(8,128)} custom-call(f32[512,128]{1,0:T(8,128)S(1)} %bitcast.15, bf16[2,256,128]{2,1,0:T(8,128)(2,1)S(1)} %copy-done.5, f32[2,16,128]{2,1,0:T(8,128)S(1)} %copy-done.6), custom_call_target="tpu_custom_call" | custom-call | tf_op jit(solution)/shard_map/rows_back/pallas_call | solution.py:271
Async XLA Ops:
  2.1 32.0 %all-to-all-start = ((f32[256,2,128]{2,1,0:T(2,128)}), f32[256,2,128]{2,1,0:T(2,128)S(1)}, u32[]{:S(2)}, u32[]{:S(2)}) async-start(f32[256,2,128]{2,1,0:T(2,128)} %bitcast.19), calls=%async_computation | async-start | bytes 524288 | tf_op jit(solution)/shard_map/all_to_all | solution.py:285
  34.1 2.4 %copy-start = (bf16[2,256,128]{2,1,0:T(8,128)(2,1)S(1)}, bf16[2,256,128]{2,1,0:T(8,128)(2,1)}, u32[]{:S(2)}) copy-start(bf16[2,256,128]{2,1,0:T(8,128)(2,1)} %constant.18.clone.forward) | copy-start | bytes 393220
  34.1 2.4 %copy-start.1 = (bf16[2,256,128]{2,1,0:T(8,128)(2,1)S(1)}, bf16[2,256,128]{2,1,0:T(8,128)(2,1)}, u32[]{:S(2)}) copy-start(bf16[2,256,128]{2,1,0:T(8,128)(2,1)} %constant.19.clone.right) | copy-start | bytes 393220
  34.1 2.4 %copy-start.2 = (bf16[2,128,256]{2,1,0:T(8,128)(2,1)S(1)}, bf16[2,128,256]{2,1,0:T(8,128)(2,1)}, u32[]{:S(2)}) copy-start(bf16[2,128,256]{2,1,0:T(8,128)(2,1)} %constant.20.clone.left) | copy-start | bytes 393220
  34.1 2.4 %copy-start.3 = (bf16[2,128,256]{2,1,0:T(8,128)(2,1)S(1)}, bf16[2,128,256]{2,1,0:T(8,128)(2,1)}, u32[]{:S(2)}) copy-start(bf16[2,128,256]{2,1,0:T(8,128)(2,1)} %constant.21.clone.back) | copy-start | bytes 393220
  34.1 2.3 %copy-start.4 = (f32[2,128,128]{2,1,0:T(8,128)S(1)}, f32[2,128,128]{2,1,0:T(8,128)}, u32[]{:S(2)}) copy-start(f32[2,128,128]{2,1,0:T(8,128)} %constant.22.clone.twist) | copy-start | bytes 393220
  57.6 3.3 %copy-start.5 = (bf16[2,256,128]{2,1,0:T(8,128)(2,1)S(1)}, bf16[2,256,128]{2,1,0:T(8,128)(2,1)}, u32[]{:S(2)}) copy-start(bf16[2,256,128]{2,1,0:T(8,128)(2,1)} %constant.23.clone.table) | copy-start | bytes 393220
  57.6 3.3 %copy-start.6 = (f32[2,16,128]{2,1,0:T(8,128)S(1)}, f32[2,16,128]{2,1,0:T(8,128)}, u32[]{:S(2)}) copy-start(f32[2,16,128]{2,1,0:T(8,128)} %constant.17.clone.twist) | copy-start | bytes 49156

commit v18 on v17

--- a/solution.py
+++ b/solution.py
@@ -39,12 +39,8 @@
 BACK_ORDER = far_first(FIRST_BACK)
 
 
-def out_groups():
-    return [[(2 * low + core) * LONG + int(k) for k in OUT_ORDER for low in range(2)] for core in range(2)]
-
-
-def back_groups():
-    return [[(2 * low + core) * LONG + int(k) for low in range(2) for k in BACK_ORDER] for core in range(2)]
+def chip_groups(order):
+    return [[(2 * low + core) * LONG + int(k) for low in range(2) for k in order] for core in range(2)]
 
 
 def angle_tables(left, right, period):
@@ -232,7 +228,7 @@
 
 def first_kernel(images, table, twist, out):
     for d, band in enumerate(row_forward(images[...], table[...], twist[...])):
-        out[pl.ds(d, LONG, stride=NDIST), :] = band
+        out[pl.ds(2 * LONG * (d // 2) + d % 2, LONG, stride=2), :] = band
 
 
 def shares(par):
@@ -251,8 +247,8 @@
     core = lax.axis_index("c")
     blocks = []
     for d in range(NDIST):
-        start = NDIST * LONG * (d % 2) + 2 * (d // 2) + core
-        blocks.append(x[pl.ds(start, LONG, stride=NDIST), :])
+        start = NDIST * LONG * (d % 2) + 2 * LONG * (d // 2) + core
+        blocks.append(x[pl.ds(start, LONG, stride=2), :])
     y = column_middle(blocks, shares(par), forward[...], right[...], left[...], back[...], twist[...])
     for low in range(2):
         out[LONG * low : LONG * (low + 1), :] = y
@@ -290,11 +286,11 @@
     rows = NDIST * LONG
     (sent,) = call(first_kernel, ((rows, LONG),), "rows_forward", None)(contrast[0], ROW_FORWARD, ROW_TW)
     par = lax.all_gather(jnp.stack([defocus, blurring], axis=1), DIST, axis=0, tiled=True)
-    got = exchange(sent, out_groups())
+    got = exchange(sent, chip_groups(OUT_ORDER))
     (middle,) = call(middle_kernel, ((2 * LONG, LONG),), "columns")(
         par, got, COL_FORWARD, COL_RIGHT, COL_LEFT, COL_BACK, COL_TW
     )
-    whole = exchange(middle, back_groups())
+    whole = exchange(middle, chip_groups(BACK_ORDER))
     return call(last_kernel, ((2, SHORT, SIZE),), "rows_back")(whole, ROW_BACK, ROW_TW)[0]
 
 

time: 62.4 us -> 62.3 us (level)
  no operation moved by 1% of the time
where the time goes in v18:
time: 62.3 us; the launch traced here: 62 us
  blocking collectives  31.6 us (51%)
  starting transfers between devices  24.6 us (39%)
  Pallas kernels  4.41 us (7%)
  between operations  1.36 us (2%)
    all_to_all x1, starting transfers between devices, exchange(): got = lax.all_to_all(sent, FLAT, 0, 0, axis_index_groups=groups, tiled=True)  24.6 us
    all_to_all x1, blocking collectives, exchange(): got = lax.all_to_all(sent, FLAT, 0, 0, axis_index_groups=groups, tiled=True)  20.3 us
    all_gather x1, blocking collectives, body(): lax.all_gather(jnp.stack([defocus, blurring], axis=1), DIST, axis=0, tile...  6.02 us
    all_gather x2, blocking collectives, exchange(): return lax.all_gather(got.reshape(x.shape), 'c', axis=0, tiled=True)  5.25 us
    pallas_call x3, Pallas kernels, run(): pl.pallas_call(kernel, out_shape=[jax.ShapeDtypeStruct(shape, jnp.float32...  4.41 us
  transfers between devices with their start and end apart: 1, of which 0 were waited for; matrix products, arithmetic and copies ran while one was open for 0% of the time, Pallas kernels for 0%

profile of v18, /device:TPU:1, one launch (start us, length us, event | category | flops | bytes accessed | tf_op | source)
XLA Modules:
  0.0 62.0 jit_solution(2810185971520543989)
XLA Ops:
  0.0 2.1 %rows_forward.1 = f32[512,128]{1,0:T(8,128)} custom-call(f32[2,16,2048]{2,1,0:T(8,128)} %bitcast.21, bf16[2,128,256]{2,1,0:T(8,128)(2,1)} %constant.16.clone.table, f32[2,16,128]{2,1,0:T(8,128)} %constant.17.clone.twist), custom_call_target="tpu_custom_call" | custom-call | tf_op jit(solution)/shard_map/rows_forward/pallas_call | solution.py:267
  2.1 24.6 %all-to-all-start = ((f32[256,2,128]{2,1,0:T(2,128)}), f32[256,2,128]{2,1,0:T(2,128)S(1)}, u32[]{:S(2)}, u32[]{:S(2)}) async-start(f32[256,2,128]{2,1,0:T(2,128)} %bitcast.19), calls=%async_computation | async-start | bytes 524288 | tf_op jit(solution)/shard_map/all_to_all | solution.py:281
  28.0 0.1 maximum_bitcast_fusion
  28.1 6.0 %all-gather.1 = f32[4,1,2]{2,1,0:T(1,128)S(1)} all-gather(f32[1,1,2]{2,1,0:T(1,128)S(1)} %maximum_bitcast_fusion), channel_id=1, replica_groups=mesh['l'=2,'c'=2,'z'=8,'x'=4,'h'=4] {'l','c'}, dimensions={0}, use_global_device_ids=true | all-gather | bytes 40 | tf_op jit(solution)/shard_map/all_gather | solution.py:288
  34.1 0.0 all-to-all-done
  34.1 0.0 copy-start
  34.1 0.0 copy-start.1
  34.1 0.0 copy-start.2
  34.1 0.0 copy-start.3
  34.1 0.0 copy-start.4
  34.2 2.3 %all_gather.10.x = f32[1024,128]{1,0:T(8,128)S(1)} all-gather(f32[512,128]{1,0:T(8,128)S(1)} %bitcast.18), channel_id=1, replica_groups=mesh['l'=2,'c'=2,'z'=8,'x'=4,'h'=4] {'c'}, dimensions={0}, use_global_device_ids=true | all-gather | bytes 786432 | tf_op jit(solution)/shard_map/all_gather | solution.py:282
  36.5 0.0 copy-done
  36.5 0.0 copy-done.1
  36.5 0.0 copy-done.2
  36.5 0.0 copy-done.3
  36.5 0.0 copy-done.4
  36.5 1.1 %columns.1 = f32[256,128]{1,0:T(8,128)S(1)} custom-call(f32[4,2]{1,0:T(4,128)S(1)} %bitcast.17, f32[1024,128]{1,0:T(8,128)S(1)} %all_gather.10.x, bf16[2,256,128]{2,1,0:T(8,128)(2,1)S(1)} %copy-done, bf16[2,256,128]{2,1,0:T(8,128)(2,1)S(1)} %copy-done.1, bf16[2,128,256]{2,1,0:T(8,128)(2,1)S(1)} %copy-done.2, bf16[2,128,256]{2,1,0:T(8,128)(2,1)S(1)} %copy-done.3, ...), custom_call_target="tpu_custom_call" | custom-call | tf_op jit(solution)/shard_map/columns/pallas_call | solution.py:267
  37.6 20.3 %all_to_all.10 = f32[256,1,128]{2,1,0:T(1,128)S(1)} all-to-all(f32[256,1,128]{2,1,0:T(1,128)S(1)} %bitcast.16), channel_id=1, replica_groups={{74,0,4,12,16,112,1,3,8,20,28,32,96,116,124,5,7,13,15,17,19,24,36,44,48..., dimensions={0} | all-to-all | bytes 262144 | tf_op jit(solution)/shard_map/all_to_all | solution.py:281
  57.9 0.0 copy-start.5
  57.9 0.0 copy-start.6
  57.9 2.9 %all-gather = f32[512,1,128]{2,0,1:T(8,128)S(1)} all-gather(f32[256,1,128]{2,0,1:T(8,128)S(1)} %bitcast.20), channel_id=2, replica_groups=mesh['l'=2,'c'=2,'z'=8,'x'=4,'h'=4] {'c'}, dimensions={0}, use_global_device_ids=true | all-gather | bytes 393216 | tf_op jit(solution)/shard_map/all_gather | solution.py:282
  60.8 0.0 copy-done.5
  60.8 0.0 copy-done.6
  60.8 1.2 %rows_back.1 = f32[2,16,2048]{2,1,0:T(8,128)} custom-call(f32[512,128]{1,0:T(8,128)S(1)} %bitcast.15, bf16[2,256,128]{2,1,0:T(8,128)(2,1)S(1)} %copy-done.5, f32[2,16,128]{2,1,0:T(8,128)S(1)} %copy-done.6), custom_call_target="tpu_custom_call" | custom-call | tf_op jit(solution)/shard_map/rows_back/pallas_call | solution.py:267
Async XLA Ops:
  2.1 32.0 %all-to-all-start = ((f32[256,2,128]{2,1,0:T(2,128)}), f32[256,2,128]{2,1,0:T(2,128)S(1)}, u32[]{:S(2)}, u32[]{:S(2)}) async-start(f32[256,2,128]{2,1,0:T(2,128)} %bitcast.19), calls=%async_computation | async-start | bytes 524288 | tf_op jit(solution)/shard_map/all_to_all | solution.py:281
  34.1 2.4 %copy-start = (bf16[2,256,128]{2,1,0:T(8,128)(2,1)S(1)}, bf16[2,256,128]{2,1,0:T(8,128)(2,1)}, u32[]{:S(2)}) copy-start(bf16[2,256,128]{2,1,0:T(8,128)(2,1)} %constant.18.clone.forward) | copy-start | bytes 393220
  34.1 2.4 %copy-start.1 = (bf16[2,256,128]{2,1,0:T(8,128)(2,1)S(1)}, bf16[2,256,128]{2,1,0:T(8,128)(2,1)}, u32[]{:S(2)}) copy-start(bf16[2,256,128]{2,1,0:T(8,128)(2,1)} %constant.19.clone.right) | copy-start | bytes 393220
  34.1 2.4 %copy-start.2 = (bf16[2,128,256]{2,1,0:T(8,128)(2,1)S(1)}, bf16[2,128,256]{2,1,0:T(8,128)(2,1)}, u32[]{:S(2)}) copy-start(bf16[2,128,256]{2,1,0:T(8,128)(2,1)} %constant.20.clone.left) | copy-start | bytes 393220
  34.1 2.4 %copy-start.3 = (bf16[2,128,256]{2,1,0:T(8,128)(2,1)S(1)}, bf16[2,128,256]{2,1,0:T(8,128)(2,1)}, u32[]{:S(2)}) copy-start(bf16[2,128,256]{2,1,0:T(8,128)(2,1)} %constant.21.clone.back) | copy-start | bytes 393220
  34.1 2.3 %copy-start.4 = (f32[2,128,128]{2,1,0:T(8,128)S(1)}, f32[2,128,128]{2,1,0:T(8,128)}, u32[]{:S(2)}) copy-start(f32[2,128,128]{2,1,0:T(8,128)} %constant.22.clone.twist) | copy-start | bytes 393220
  57.9 2.9 %copy-start.5 = (bf16[2,256,128]{2,1,0:T(8,128)(2,1)S(1)}, bf16[2,256,128]{2,1,0:T(8,128)(2,1)}, u32[]{:S(2)}) copy-start(bf16[2,256,128]{2,1,0:T(8,128)(2,1)} %constant.23.clone.table) | copy-start | bytes 393220
  57.9 2.9 %copy-start.6 = (f32[2,16,128]{2,1,0:T(8,128)S(1)}, f32[2,16,128]{2,1,0:T(8,128)}, u32[]{:S(2)}) copy-start(f32[2,16,128]{2,1,0:T(8,128)} %constant.17.clone.twist) | copy-start | bytes 49156

commit v19 on v17

--- a/solution.py
+++ b/solution.py
@@ -23,7 +23,7 @@
 FLAT = DIST + PIX
 
 
-FIRST_OUT = (5, 2, 2)
+FIRST_OUT = (5, 1, 2)
 FIRST_BACK = (4, 2, 2)
 
 

time: 62.4 us -> 63.1 us (1.011)
  blocking collectives: 31.6 us -> 32.9 us
  starting transfers between devices: 24.6 us -> 23.9 us
    all_gather x2, blocking collectives: 5.61 us -> 7.18 us  [exchange(): return lax.all_gather(got.reshape(x.shape), 'c', axis=0, tiled=True)]
    all_to_all x1, starting transfers between devices: 24.6 us -> 23.9 us  [exchange(): got = lax.all_to_all(sent, FLAT, 0, 0, axis_index_groups=groups, tiled=True)]
  transfers between devices with their start and end apart: 1 -> 1, of which waited for: 0 -> 1; matrix products, arithmetic and copies ran while one was open for 0% -> 0% of each run, Pallas kernels for 0% -> 0%
where the time goes in v19:
time: 63.1 us; the launch traced here: 62.8 us
  blocking collectives  32.9 us (52%)
  starting transfers between devices  23.9 us (38%)
  Pallas kernels  4.41 us (7%)
  between operations  1.34 us (2%)
    all_to_all x1, starting transfers between devices, exchange(): got = lax.all_to_all(sent, FLAT, 0, 0, axis_index_groups=groups, tiled=True)  23.9 us
    all_to_all x1, blocking collectives, exchange(): got = lax.all_to_all(sent, FLAT, 0, 0, axis_index_groups=groups, tiled=True)  19.6 us
    all_gather x2, blocking collectives, exchange(): return lax.all_gather(got.reshape(x.shape), 'c', axis=0, tiled=True)  7.18 us
    all_gather x1, blocking collectives, body(): lax.all_gather(jnp.stack([defocus, blurring], axis=1), DIST, axis=0, tile...  6.12 us
    pallas_call x3, Pallas kernels, run(): pl.pallas_call(kernel, out_shape=[jax.ShapeDtypeStruct(shape, jnp.float32...  4.41 us
  transfers between devices with their start and end apart: 1, of which 1 were waited for; matrix products, arithmetic and copies ran while one was open for 0% of the time, Pallas kernels for 0%

profile of v19, /device:TPU:1, one launch (start us, length us, event | category | flops | bytes accessed | tf_op | source)
XLA Modules:
  0.0 62.8 jit_solution(3461342411746470426)
XLA Ops:
  0.0 2.1 %rows_forward.1 = f32[512,128]{1,0:T(8,128)} custom-call(f32[2,16,2048]{2,1,0:T(8,128)} %bitcast.21, bf16[2,128,256]{2,1,0:T(8,128)(2,1)} %constant.16.clone.table, f32[2,16,128]{2,1,0:T(8,128)} %constant.17.clone.twist), custom_call_target="tpu_custom_call" | custom-call | tf_op jit(solution)/shard_map/rows_forward/pallas_call | solution.py:271
  2.1 23.9 %all-to-all-start = ((f32[256,2,128]{2,1,0:T(2,128)}), f32[256,2,128]{2,1,0:T(2,128)S(1)}, u32[]{:S(2)}, u32[]{:S(2)}) async-start(f32[256,2,128]{2,1,0:T(2,128)} %bitcast.19), calls=%async_computation | async-start | bytes 524288 | tf_op jit(solution)/shard_map/all_to_all | solution.py:285
  27.3 0.1 maximum_bitcast_fusion
  27.4 6.1 %all-gather.1 = f32[4,1,2]{2,1,0:T(1,128)S(1)} all-gather(f32[1,1,2]{2,1,0:T(1,128)S(1)} %maximum_bitcast_fusion), channel_id=1, replica_groups=mesh['l'=2,'c'=2,'z'=8,'x'=4,'h'=4] {'l','c'}, dimensions={0}, use_global_device_ids=true | all-gather | bytes 40 | tf_op jit(solution)/shard_map/all_gather | solution.py:292
  33.5 0.1 all-to-all-done
  33.6 0.0 copy-start
  33.6 0.0 copy-start.1
  33.6 0.0 copy-start.2
  33.6 0.0 copy-start.3
  33.7 0.0 copy-start.4
  33.7 3.9 %all_gather.10.x = f32[1024,128]{1,0:T(8,128)S(1)} all-gather(f32[512,128]{1,0:T(8,128)S(1)} %bitcast.18), channel_id=1, replica_groups=mesh['l'=2,'c'=2,'z'=8,'x'=4,'h'=4] {'c'}, dimensions={0}, use_global_device_ids=true | all-gather | bytes 786432 | tf_op jit(solution)/shard_map/all_gather | solution.py:286
  37.5 0.0 copy-done
  37.5 0.0 copy-done.1
  37.6 0.0 copy-done.2
  37.6 0.0 copy-done.3
  37.6 0.0 copy-done.4
  37.6 1.1 %columns.1 = f32[256,128]{1,0:T(8,128)S(1)} custom-call(f32[4,2]{1,0:T(4,128)S(1)} %bitcast.17, f32[1024,128]{1,0:T(8,128)S(1)} %all_gather.10.x, bf16[2,256,128]{2,1,0:T(8,128)(2,1)S(1)} %copy-done, bf16[2,256,128]{2,1,0:T(8,128)(2,1)S(1)} %copy-done.1, bf16[2,128,256]{2,1,0:T(8,128)(2,1)S(1)} %copy-done.2, bf16[2,128,256]{2,1,0:T(8,128)(2,1)S(1)} %copy-done.3, ...), custom_call_target="tpu_custom_call" | custom-call | tf_op jit(solution)/shard_map/columns/pallas_call | solution.py:271
  38.7 19.6 %all_to_all.10 = f32[256,1,128]{2,1,0:T(1,128)S(1)} all-to-all(f32[256,1,128]{2,1,0:T(1,128)S(1)} %bitcast.16), channel_id=1, replica_groups={{74,0,4,12,16,112,1,3,8,20,28,32,96,116,124,5,7,13,15,17,19,24,36,44,48..., dimensions={0} | all-to-all | bytes 262144 | tf_op jit(solution)/shard_map/all_to_all | solution.py:285
  58.3 0.0 copy-start.5
  58.3 0.0 copy-start.6
  58.3 3.3 %all-gather = f32[512,1,128]{2,0,1:T(8,128)S(1)} all-gather(f32[256,1,128]{2,0,1:T(8,128)S(1)} %bitcast.20), channel_id=2, replica_groups=mesh['l'=2,'c'=2,'z'=8,'x'=4,'h'=4] {'c'}, dimensions={0}, use_global_device_ids=true | all-gather | bytes 393216 | tf_op jit(solution)/shard_map/all_gather | solution.py:286
  61.6 0.0 copy-done.5
  61.6 0.0 copy-done.6
  61.6 1.2 %rows_back.1 = f32[2,16,2048]{2,1,0:T(8,128)} custom-call(f32[512,128]{1,0:T(8,128)S(1)} %bitcast.15, bf16[2,256,128]{2,1,0:T(8,128)(2,1)S(1)} %copy-done.5, f32[2,16,128]{2,1,0:T(8,128)S(1)} %copy-done.6), custom_call_target="tpu_custom_call" | custom-call | tf_op jit(solution)/shard_map/rows_back/pallas_call | solution.py:271
Async XLA Ops:
  2.1 31.5 %all-to-all-start = ((f32[256,2,128]{2,1,0:T(2,128)}), f32[256,2,128]{2,1,0:T(2,128)S(1)}, u32[]{:S(2)}, u32[]{:S(2)}) async-start(f32[256,2,128]{2,1,0:T(2,128)} %bitcast.19), calls=%async_computation | async-start | bytes 524288 | tf_op jit(solution)/shard_map/all_to_all | solution.py:285
  33.6 3.9 %copy-start = (bf16[2,256,128]{2,1,0:T(8,128)(2,1)S(1)}, bf16[2,256,128]{2,1,0:T(8,128)(2,1)}, u32[]{:S(2)}) copy-start(bf16[2,256,128]{2,1,0:T(8,128)(2,1)} %constant.18.clone.forward) | copy-start | bytes 393220
  33.6 3.9 %copy-start.1 = (bf16[2,256,128]{2,1,0:T(8,128)(2,1)S(1)}, bf16[2,256,128]{2,1,0:T(8,128)(2,1)}, u32[]{:S(2)}) copy-start(bf16[2,256,128]{2,1,0:T(8,128)(2,1)} %constant.19.clone.right) | copy-start | bytes 393220
  33.6 3.9 %copy-start.2 = (bf16[2,128,256]{2,1,0:T(8,128)(2,1)S(1)}, bf16[2,128,256]{2,1,0:T(8,128)(2,1)}, u32[]{:S(2)}) copy-start(bf16[2,128,256]{2,1,0:T(8,128)(2,1)} %constant.20.clone.left) | copy-start | bytes 393220
  33.6 3.9 %copy-start.3 = (bf16[2,128,256]{2,1,0:T(8,128)(2,1)S(1)}, bf16[2,128,256]{2,1,0:T(8,128)(2,1)}, u32[]{:S(2)}) copy-start(bf16[2,128,256]{2,1,0:T(8,128)(2,1)} %constant.21.clone.back) | copy-start | bytes 393220
  33.7 3.9 %copy-start.4 = (f32[2,128,128]{2,1,0:T(8,128)S(1)}, f32[2,128,128]{2,1,0:T(8,128)}, u32[]{:S(2)}) copy-start(f32[2,128,128]{2,1,0:T(8,128)} %constant.22.clone.twist) | copy-start | bytes 393220
  58.3 3.3 %copy-start.5 = (bf16[2,256,128]{2,1,0:T(8,128)(2,1)S(1)}, bf16[2,256,128]{2,1,0:T(8,128)(2,1)}, u32[]{:S(2)}) copy-start(bf16[2,256,128]{2,1,0:T(8,128)(2,1)} %constant.23.clone.table) | copy-start | bytes 393220
  58.3 3.3 %copy-start.6 = (f32[2,16,128]{2,1,0:T(8,128)S(1)}, f32[2,16,128]{2,1,0:T(8,128)}, u32[]{:S(2)}) copy-start(f32[2,16,128]{2,1,0:T(8,128)} %constant.17.clone.twist) | copy-start | bytes 49156

commit v20 on v17

--- a/solution.py
+++ b/solution.py
@@ -24,7 +24,7 @@
 
 
 FIRST_OUT = (5, 2, 2)
-FIRST_BACK = (4, 2, 2)
+FIRST_BACK = (5, 2, 2)
 
 
 def far_first(first):

time: 62.4 us -> 63.1 us (1.011)
  blocking collectives: 31.6 us -> 32.3 us
    all_to_all x1, blocking collectives: 20 us -> 20.8 us  [exchange(): got = lax.all_to_all(sent, FLAT, 0, 0, axis_index_groups=groups, tiled=True)]
where the time goes in v20:
time: 63.1 us; the launch traced here: 62.8 us
  blocking collectives  32.3 us (51%)
  starting transfers between devices  24.6 us (39%)
  Pallas kernels  4.41 us (7%)
  between operations  1.36 us (2%)
    all_to_all x1, starting transfers between devices, exchange(): got = lax.all_to_all(sent, FLAT, 0, 0, axis_index_groups=groups, tiled=True)  24.6 us
    all_to_all x1, blocking collectives, exchange(): got = lax.all_to_all(sent, FLAT, 0, 0, axis_index_groups=groups, tiled=True)  20.8 us
    all_gather x1, blocking collectives, body(): lax.all_gather(jnp.stack([defocus, blurring], axis=1), DIST, axis=0, tile...  6.01 us
    all_gather x2, blocking collectives, exchange(): return lax.all_gather(got.reshape(x.shape), 'c', axis=0, tiled=True)  5.51 us
    pallas_call x3, Pallas kernels, run(): pl.pallas_call(kernel, out_shape=[jax.ShapeDtypeStruct(shape, jnp.float32...  4.41 us
  transfers between devices with their start and end apart: 1, of which 0 were waited for; matrix products, arithmetic and copies ran while one was open for 0% of the time, Pallas kernels for 0%

profile of v20, /device:TPU:1, one launch (start us, length us, event | category | flops | bytes accessed | tf_op | source)
XLA Modules:
  0.0 62.8 jit_solution(5895548547644301714)
XLA Ops:
  0.0 2.1 %rows_forward.1 = f32[512,128]{1,0:T(8,128)} custom-call(f32[2,16,2048]{2,1,0:T(8,128)} %bitcast.21, bf16[2,128,256]{2,1,0:T(8,128)(2,1)} %constant.16.clone.table, f32[2,16,128]{2,1,0:T(8,128)} %constant.17.clone.twist), custom_call_target="tpu_custom_call" | custom-call | tf_op jit(solution)/shard_map/rows_forward/pallas_call | solution.py:271
  2.1 24.6 %all-to-all-start = ((f32[256,2,128]{2,1,0:T(2,128)}), f32[256,2,128]{2,1,0:T(2,128)S(1)}, u32[]{:S(2)}, u32[]{:S(2)}) async-start(f32[256,2,128]{2,1,0:T(2,128)} %bitcast.19), calls=%async_computation | async-start | bytes 524288 | tf_op jit(solution)/shard_map/all_to_all | solution.py:285
  28.0 0.1 maximum_bitcast_fusion
  28.1 6.0 %all-gather.1 = f32[4,1,2]{2,1,0:T(1,128)S(1)} all-gather(f32[1,1,2]{2,1,0:T(1,128)S(1)} %maximum_bitcast_fusion), channel_id=1, replica_groups=mesh['l'=2,'c'=2,'z'=8,'x'=4,'h'=4] {'l','c'}, dimensions={0}, use_global_device_ids=true | all-gather | bytes 40 | tf_op jit(solution)/shard_map/all_gather | solution.py:292
  34.1 0.0 all-to-all-done
  34.1 0.0 copy-start
  34.1 0.0 copy-start.1
  34.1 0.0 copy-start.2
  34.1 0.0 copy-start.3
  34.1 0.0 copy-start.4
  34.2 2.3 %all_gather.10.x = f32[1024,128]{1,0:T(8,128)S(1)} all-gather(f32[512,128]{1,0:T(8,128)S(1)} %bitcast.18), channel_id=1, replica_groups=mesh['l'=2,'c'=2,'z'=8,'x'=4,'h'=4] {'c'}, dimensions={0}, use_global_device_ids=true | all-gather | bytes 786432 | tf_op jit(solution)/shard_map/all_gather | solution.py:286
  36.5 0.0 copy-done
  36.5 0.0 copy-done.1
  36.5 0.0 copy-done.2
  36.5 0.0 copy-done.3
  36.5 0.0 copy-done.4
  36.5 1.1 %columns.1 = f32[256,128]{1,0:T(8,128)S(1)} custom-call(f32[4,2]{1,0:T(4,128)S(1)} %bitcast.17, f32[1024,128]{1,0:T(8,128)S(1)} %all_gather.10.x, bf16[2,256,128]{2,1,0:T(8,128)(2,1)S(1)} %copy-done, bf16[2,256,128]{2,1,0:T(8,128)(2,1)S(1)} %copy-done.1, bf16[2,128,256]{2,1,0:T(8,128)(2,1)S(1)} %copy-done.2, bf16[2,128,256]{2,1,0:T(8,128)(2,1)S(1)} %copy-done.3, ...), custom_call_target="tpu_custom_call" | custom-call | tf_op jit(solution)/shard_map/columns/pallas_call | solution.py:271
  37.6 20.8 %all_to_all.10 = f32[256,1,128]{2,1,0:T(1,128)S(1)} all-to-all(f32[256,1,128]{2,1,0:T(1,128)S(1)} %bitcast.16), channel_id=1, replica_groups={{90,16,0,20,28,32,4,12,17,19,24,36,44,48,112,1,3,8,21,23,29,31,33,35,40..., dimensions={0} | all-to-all | bytes 262144 | tf_op jit(solution)/shard_map/all_to_all | solution.py:285
  58.4 0.0 copy-start.5
  58.4 0.0 copy-start.6
  58.4 3.2 %all-gather = f32[512,1,128]{2,0,1:T(8,128)S(1)} all-gather(f32[256,1,128]{2,0,1:T(8,128)S(1)} %bitcast.20), channel_id=2, replica_groups=mesh['l'=2,'c'=2,'z'=8,'x'=4,'h'=4] {'c'}, dimensions={0}, use_global_device_ids=true | all-gather | bytes 393216 | tf_op jit(solution)/shard_map/all_gather | solution.py:286
  61.6 0.0 copy-done.5
  61.6 0.0 copy-done.6
  61.6 1.2 %rows_back.1 = f32[2,16,2048]{2,1,0:T(8,128)} custom-call(f32[512,128]{1,0:T(8,128)S(1)} %bitcast.15, bf16[2,256,128]{2,1,0:T(8,128)(2,1)S(1)} %copy-done.5, f32[2,16,128]{2,1,0:T(8,128)S(1)} %copy-done.6), custom_call_target="tpu_custom_call" | custom-call | tf_op jit(solution)/shard_map/rows_back/pallas_call | solution.py:271
Async XLA Ops:
  2.1 32.0 %all-to-all-start = ((f32[256,2,128]{2,1,0:T(2,128)}), f32[256,2,128]{2,1,0:T(2,128)S(1)}, u32[]{:S(2)}, u32[]{:S(2)}) async-start(f32[256,2,128]{2,1,0:T(2,128)} %bitcast.19), calls=%async_computation | async-start | bytes 524288 | tf_op jit(solution)/shard_map/all_to_all | solution.py:285
  34.1 2.4 %copy-start = (bf16[2,256,128]{2,1,0:T(8,128)(2,1)S(1)}, bf16[2,256,128]{2,1,0:T(8,128)(2,1)}, u32[]{:S(2)}) copy-start(bf16[2,256,128]{2,1,0:T(8,128)(2,1)} %constant.18.clone.forward) | copy-start | bytes 393220
  34.1 2.4 %copy-start.1 = (bf16[2,256,128]{2,1,0:T(8,128)(2,1)S(1)}, bf16[2,256,128]{2,1,0:T(8,128)(2,1)}, u32[]{:S(2)}) copy-start(bf16[2,256,128]{2,1,0:T(8,128)(2,1)} %constant.19.clone.right) | copy-start | bytes 393220
  34.1 2.4 %copy-start.2 = (bf16[2,128,256]{2,1,0:T(8,128)(2,1)S(1)}, bf16[2,128,256]{2,1,0:T(8,128)(2,1)}, u32[]{:S(2)}) copy-start(bf16[2,128,256]{2,1,0:T(8,128)(2,1)} %constant.20.clone.left) | copy-start | bytes 393220
  34.1 2.4 %copy-start.3 = (bf16[2,128,256]{2,1,0:T(8,128)(2,1)S(1)}, bf16[2,128,256]{2,1,0:T(8,128)(2,1)}, u32[]{:S(2)}) copy-start(bf16[2,128,256]{2,1,0:T(8,128)(2,1)} %constant.21.clone.back) | copy-start | bytes 393220
  34.1 2.3 %copy-start.4 = (f32[2,128,128]{2,1,0:T(8,128)S(1)}, f32[2,128,128]{2,1,0:T(8,128)}, u32[]{:S(2)}) copy-start(f32[2,128,128]{2,1,0:T(8,128)} %constant.22.clone.twist) | copy-start | bytes 393220
  58.4 3.2 %copy-start.5 = (bf16[2,256,128]{2,1,0:T(8,128)(2,1)S(1)}, bf16[2,256,128]{2,1,0:T(8,128)(2,1)}, u32[]{:S(2)}) copy-start(bf16[2,256,128]{2,1,0:T(8,128)(2,1)} %constant.23.clone.table) | copy-start | bytes 393220
  58.4 3.2 %copy-start.6 = (f32[2,16,128]{2,1,0:T(8,128)S(1)}, f32[2,16,128]{2,1,0:T(8,128)}, u32[]{:S(2)}) copy-start(f32[2,16,128]{2,1,0:T(8,128)} %constant.17.clone.twist) | copy-start | bytes 49156
